TPU v7x, 256 devices: a whole 4x4x8 slice. The times are simulated.
256 devices in a mesh: rows: 64 (over x, z_hi, y), grp: 4 (over z_lo, core).
Axes of the slice: x: 4, y: 4, z: 8 (z_hi: 4, z_lo: 2; z = z_hi * 2 + z_lo), core: 2. Of those that a mesh axis runs over, the one named last changes fastest.
Arguments:
- vector: float32 [1024, 16, 384], P(('rows', 'grp')), may hold values from -20 to 20
- near_cols: int32 [1024, 3], P(('rows', 'grp')), may hold values from 0 to 1023, as said below
- near_blocks: bfloat16 [1024, 3, 384, 384], P(('rows', 'grp')), may hold values from -2 to 2
- col_basis: bfloat16 [1024, 32, 384], P(('rows', 'grp')), may hold values from -0.3125 to 0.3125
- row_basis: bfloat16 [1024, 32, 384], P(('rows', 'grp')), may hold values from -1 to 1
- leaf_far: int32 [1024, 8], P(('rows', 'grp')), may hold values from 0 to 1023, as said below
- leaf_coupling: bfloat16 [1024, 32, 256], P(('rows', 'grp')), may hold values from -0.375 to 0.375
- leaf_transfer: float32 [1024, 32, 32], P(('rows', 'grp')), may hold values from -0.5 to 0.5
- box_far: int32 [256, 4], P(('rows', 'grp')), may hold values from 0 to 255, as said below
- box_coupling: bfloat16 [256, 32, 128], P(('rows', 'grp')), may hold values from -0.5 to 0.5
- box_transfer: float32 [256, 32, 32], P(('rows', 'grp')), may hold values from -1 to 1
- coarse_far: int32 [64, 4], P('rows'), may hold values from 0 to 63, as said below
- coarse_coupling: bfloat16 [64, 32, 128], P('rows'), may hold values from -0.5 to 0.5
Outputs:
- basis: float32 [1024, 16, 384], P(('rows', 'grp'))
- remainder: float32 [1024, 16, 384], P(('rows', 'grp'))
- hessenberg: float32 [16, 5], replicated
Inputs may be any that keep to these rules, and one draw needn't show every extreme that they name: `near_cols`: entry 0 of leaf l is l itself; the other entries are distinct leaves l + o with 0 < |o| <= 4. `leaf_far`: the entries of leaf l are distinct leaves g with |g - l| > 4 and |g // 16 - l // 16| <= 1. `box_far`: the entries of box x are distinct boxes y with |y - x| > 1 and |y // 4 - x // 4| <= 1. `coarse_far`: the entries of group g are distinct groups h with |h - g| > 1.
All inputs are finite; a program needn't handle non-finite values.
Results may differ from a plain program's by a relative error of at most 0.015.
Values may be sent and summed in bfloat16 or wider, within the bound.
No kernel may reach another device: no remote copies, remote signals or barrier semaphores. Data moves between devices by JAX's collectives and lax.ppermute only.
A program may use at most 64 MiB of HBM per device.

v0:
```python
import functools

import jax
import jax.numpy as jnp
from jax import lax
from jax.sharding import Mesh
from jax.sharding import PartitionSpec as P

R = 32
GRP = ("grp_0", "grp_1")
ROWS = ("rows_0", "rows_1", "rows_2")
ROWS_GRP = ("rows_0", "rows_1", "rows_2", "grp_0", "grp_1")


epsilon = 1e-06


def extended(array, sides, width):
    edges = {}
    for axis, dim in sides:
        count, length = (lax.axis_size(axis), array.shape[dim])
        up = [(i, (i + 1) % count) for i in range(count - 1)]
        last = lax.slice_in_dim(array, length - width, length, axis=dim)
        initial = lax.slice_in_dim(array, 0, width, axis=dim)
        edges[dim] = (
            lax.ppermute(last, axis, up),
            lax.ppermute(initial, axis, [(b, a) for a, b in up]),
        )
    done = []
    for _, dim in sides:
        low, high = edges[dim]
        around = [(width, width) if d in done else (0, 0) for d in range(array.ndim)]
        array = jnp.concatenate([jnp.pad(low, around), array, jnp.pad(high, around)], axis=dim)
        done.append(dim)
    return array


def from_everyone(array, axis):
    copies = jnp.broadcast_to(array, (lax.axis_size(axis), *array.shape))
    return lax.all_to_all(copies, axis, split_axis=0, concat_axis=0, tiled=True)


def joined_along(pieces, dim):
    pieces = jnp.moveaxis(pieces, 0, dim)
    dims = pieces.shape
    return pieces.reshape(*dims[:dim], dims[dim] * dims[dim + 1], *dims[dim + 2 :])


def collect(array, axis, dim):
    pieces = from_everyone(array, axis)
    return joined_along(pieces, dim)


def of_everyone(array, axis):
    return from_everyone(array, axis).sum(axis=0)


def padded(block, sides, width):
    for axis, dim in sides:
        count = lax.axis_size(axis)
        forward = [(i, i + 1) for i in range(count - 1)]
        backward = [(target, source) for source, target in forward]
        low = lax.ppermute(
            lax.slice_in_dim(block, block.shape[dim] - width, None, axis=dim), axis, forward
        )
        high = lax.ppermute(lax.slice_in_dim(block, 0, width, axis=dim), axis, backward)
        block = jnp.concatenate([low, block, high], axis=dim)
    return block


def by_axis(array, axes):
    return functools.reduce(lax.psum, axes, array)


def pick_flat(source, indices):
    chosen = jnp.take(source, indices, axis=0)
    target_count, slot_count = indices.shape
    chosen = chosen.reshape(target_count, slot_count, -1, R)
    chosen = jnp.transpose(chosen, (0, 2, 1, 3))
    return chosen.reshape(target_count, -1, slot_count * R)


def shards(
    vector,
    near_cols,
    near_blocks,
    col_basis,
    row_basis,
    leaf_far,
    leaf_coupling,
    leaf_transfer,
    box_far,
    box_coupling,
    box_transfer,
    coarse_far,
    coarse_coupling,
):
    leaf_count, rhs_count, cell_count = vector.shape
    group_size = lax.axis_size(GRP)
    row_count = lax.axis_size(ROWS)
    row_index = lax.axis_index(ROWS)
    device = row_index * group_size + lax.axis_index(GRP)
    first_leaf = device * leaf_count
    total_count = leaf_count * row_count * group_size * cell_count
    coef_width = rhs_count * R

    def apply_operator(field):
        field_bf = field.astype(jnp.bfloat16)
        widened = extended(field_bf, ((ROWS_GRP, 0),), leaf_count)
        picked = jnp.take(widened, near_cols - (first_leaf - leaf_count), axis=0)
        near_sum = jnp.einsum(
            "lkbj,lkij->lbi", picked, near_blocks, preferred_element_type=jnp.float32
        )
        leaf_coef = jnp.einsum(
            "lbj,lrj->lbr", field_bf, col_basis, preferred_element_type=jnp.float32
        ).astype(jnp.bfloat16)
        box_coef = jnp.einsum("lbr,lrs->bs", leaf_coef.astype(jnp.float32), leaf_transfer).astype(
            jnp.bfloat16
        )
        parent_part = jnp.dot(box_coef.astype(jnp.float32), box_transfer[0]).astype(jnp.bfloat16)
        leaf_rows = leaf_coef.reshape(leaf_count, coef_width)
        box_row = box_coef.reshape(1, coef_width)
        parent_row = parent_part.reshape(1, coef_width)
        packed = jnp.concatenate([leaf_rows, box_row], axis=0)
        group_block = collect(packed, GRP, 0).reshape(group_size, -1, coef_width)
        group_own = of_everyone(parent_row.astype(jnp.float32), GRP)
        group_all = collect(group_own.astype(jnp.bfloat16), ROWS, 0)
        inner_block = group_block.reshape(-1, coef_width)
        window = padded(inner_block, ((ROWS, 0),), group_size * (leaf_count + 1))
        window = window.reshape(3 * group_size, leaf_count + 1, coef_width)
        leaf_source = window[:, :leaf_count].reshape(-1, coef_width)
        box_source = window[:, leaf_count]
        leaf_base = (row_index - 1) * group_size * leaf_count
        box_base = (row_index - 1) * group_size
        leaf_field = jnp.einsum(
            "lbm,lrm->lbr",
            pick_flat(leaf_source, leaf_far - leaf_base),
            leaf_coupling,
            preferred_element_type=jnp.float32,
        )
        box_field = jnp.einsum(
            "xbm,xrm->xbr",
            pick_flat(box_source, box_far - box_base),
            box_coupling,
            preferred_element_type=jnp.float32,
        )[0]
        group_field = jnp.einsum(
            "gbm,grm->gbr",
            pick_flat(group_all, coarse_far),
            coarse_coupling,
            preferred_element_type=jnp.float32,
        )[0]
        box_local = box_field + jnp.einsum("bs,rs->br", group_field, box_transfer[0])
        leaf_local = leaf_field + jnp.einsum("bs,lrs->lbr", box_local, leaf_transfer)
        leaf_local = leaf_local.astype(jnp.bfloat16)
        far_sum = jnp.einsum(
            "lbr,lrj->lbj", leaf_local, row_basis, preferred_element_type=jnp.float32
        )
        return 0.5 * field + near_sum + far_sum

    def stacked_means(pairs):
        partial_sums = jnp.stack(
            [jnp.sum(left * right, axis=(0, 2)) for left, right in pairs], axis=0
        )
        return by_axis(partial_sums, ROWS_GRP) / total_count

    def spread_rhs(values):
        return values[None, :, None]

    norm_first = jnp.sqrt(stacked_means([(vector, vector)])[0] + epsilon)
    first_basis = vector / spread_rhs(norm_first)
    image_one = apply_operator(first_basis)
    first_gram = stacked_means(
        [(first_basis, image_one), (image_one, image_one), (first_basis, first_basis)]
    )
    proj_first = first_gram[0]
    first_square = first_gram[2]
    image_one = image_one - spread_rhs(proj_first) * first_basis
    image_square = first_gram[1] - proj_first * proj_first * (2.0 - first_square)
    norm_image = jnp.sqrt(image_square + epsilon)
    basis = image_one / spread_rhs(norm_image)
    remainder = apply_operator(basis)
    second_gram = stacked_means(
        [
            (first_basis, remainder),
            (basis, remainder),
            (remainder, remainder),
            (basis, first_basis),
            (basis, basis),
        ]
    )
    first_with = second_gram[0]
    basis_with = second_gram[1]
    image_square_two = second_gram[2]
    cross_term = second_gram[3]
    basis_square = second_gram[4]
    proj_basis = basis_with - first_with * cross_term
    remainder = remainder - spread_rhs(first_with) * first_basis
    remainder = remainder - spread_rhs(proj_basis) * basis
    last_square = (
        image_square_two
        + first_with * first_with * first_square
        + proj_basis * proj_basis * basis_square
        - 2.0 * first_with * first_with
        - 2.0 * proj_basis * basis_with
        + 2.0 * first_with * proj_basis * cross_term
    )
    norm_last = jnp.sqrt(last_square + epsilon)
    hessenberg = jnp.stack([proj_first, norm_image, first_with, proj_basis, norm_last], axis=1)
    return (basis, remainder, hessenberg)


def solution(mesh):
    finer = Mesh(
        mesh.devices.reshape(4, 4, 4, 2, 2), ("rows_0", "rows_1", "rows_2", "grp_0", "grp_1")
    )
    placed = (
        P(ROWS_GRP, None, None),
        P(ROWS_GRP, None),
        P(ROWS_GRP, None, None, None),
        P(ROWS_GRP, None, None),
        P(ROWS_GRP, None, None),
        P(ROWS_GRP, None),
        P(ROWS_GRP, None, None),
        P(ROWS_GRP, None, None),
        P(ROWS_GRP, None),
        P(ROWS_GRP, None, None),
        P(ROWS_GRP, None, None),
        P(ROWS, None),
        P(ROWS, None, None),
    )
    return jax.shard_map(
        shards,
        mesh=finer,
        in_specs=placed,
        out_specs=(P(ROWS_GRP, None, None), P(ROWS_GRP, None, None), P()),
        check_vma=False,
    )
```

profile of v0, /device:TPU:1, one launch (start us, length us, event | category | flops | bytes accessed | tf_op | source)
XLA Modules:
  0.0 347.3 jit_solution(838673261103749024)
XLA Ops:
  1.8 9.3 %psum.105 = f32[1,16]{1,0:T(1,128)S(1)} all-reduce(f32[1,16]{1,0:T(1,128)S(1)} %bitcast.290), channel_id=1, replica_groups=mesh['rows_0'=4,'rows_1'=4,'rows_2'=4,'grp_0'=2,'grp_1'=2] {'rows_0'}, use_global_device_ids=true, to_apply=%region_1.0 | all-reduce | flops 16 | bytes 128 | tf_op jit(solution)/shard_map/psum | solution.py:72
  11.1 12.9 %psum.106 = f32[1,16]{1,0:T(1,128)S(1)} all-reduce(f32[1,16]{1,0:T(1,128)S(1)} %psum.105), channel_id=1, replica_groups=mesh['rows_0'=4,'rows_1'=4,'rows_2'=4,'grp_0'=2,'grp_1'=2] {'rows_1'}, use_global_device_ids=true, to_apply=%region_2.0 | all-reduce | flops 16 | bytes 128 | tf_op jit(solution)/shard_map/psum | solution.py:72
  24.0 8.7 %psum.107 = f32[1,16]{1,0:T(1,128)S(1)} all-reduce(f32[1,16]{1,0:T(1,128)S(1)} %psum.106), channel_id=1, replica_groups=mesh['rows_0'=4,'rows_1'=4,'rows_2'=4,'grp_0'=2,'grp_1'=2] {'rows_2'}, use_global_device_ids=true, to_apply=%region_3.0 | all-reduce | flops 16 | bytes 128 | tf_op jit(solution)/shard_map/psum | solution.py:72
  32.8 3.8 %psum.108 = f32[1,16]{1,0:T(1,128)S(1)} all-reduce(f32[1,16]{1,0:T(1,128)S(1)} %psum.107), channel_id=1, replica_groups=mesh['rows_0'=4,'rows_1'=4,'rows_2'=4,'grp_0'=2,'grp_1'=2] {'grp_0'}, use_global_device_ids=true, to_apply=%region_4.0 | all-reduce | flops 16 | bytes 128 | tf_op jit(solution)/shard_map/psum | solution.py:72
  36.5 9.9 %psum.109 = f32[1,16]{1,0:T(1,128)S(1)} all-reduce(f32[1,16]{1,0:T(1,128)S(1)} %psum.108), channel_id=1, replica_groups=mesh['rows_0'=4,'rows_1'=4,'rows_2'=4,'grp_0'=2,'grp_1'=2] {'grp_1'}, use_global_device_ids=true, to_apply=%region_5.0 | all-reduce | flops 16 | bytes 128 | tf_op jit(solution)/shard_map/psum | solution.py:72
  46.5 1.6 fusion.49
  48.1 2.9 collective-permute-start
  50.9 2.0 collective-permute-start.1
  59.8 3.8 %all-to-all-start.1 = ((f32[4,1,512]{2,1,0:T(1,128)}), f32[4,1,512]{2,1,0:T(1,128)}, u32[]{:S(2)}, u32[]{:S(2)}) async-start(f32[4,1,512]{2,1,0:T(1,128)} %broadcast_in_dim.58), calls=%async_computation.1 | async-start | bytes 16384 | tf_op jit(solution)/shard_map/all_to_all | solution.py:40
  74.5 3.9 %all-to-all-start = ((bf16[4,5,512]{2,1,0:T(8,128)(2,1)}), bf16[4,5,512]{2,1,0:T(8,128)(2,1)}, u32[]{:S(2)}, u32[]{:S(2)}) async-start(bf16[4,5,512]{2,1,0:T(8,128)(2,1)} %broadcast_in_dim.57), calls=%async_computation | async-start | bytes 65536 | tf_op jit(solution)/shard_map/all_to_all | solution.py:40
  80.9 2.5 reduce.2
  84.9 9.2 %all-to-all-start.2 = ((bf16[64,2,256]{2,1,0:T(2,128)(2,1)}), bf16[64,2,256]{2,1,0:T(2,128)(2,1)}, u32[]{:S(2)}, u32[]{:S(2)}) async-start(bf16[64,2,256]{2,1,0:T(2,128)(2,1)} %reshape.581), calls=%async_computation.2 | async-start | bytes 131072 | tf_op jit(solution)/shard_map/all_to_all | solution.py:40
  95.5 3.4 collective-permute-start.2
  100.2 1.5 pad_maximum_fusion
  101.8 2.3 gather_fusion
  104.0 2.7 fusion.1
  110.6 1.5 slice.64
  112.7 2.0 gather_fusion.2
  121.6 2.2 gather_fusion.1
  125.2 1.5 reshape.445
  126.8 1.6 copy.56
  128.4 1.7 reshape.446
  130.0 1.6 fusion.64
  133.0 1.5 reshape.582
  134.6 1.5 copy.83
  136.1 2.1 gather_fusion.3
  143.7 1.6 fusion.7
  145.2 2.7 multiply_reduce_fusion.7
  149.2 14.7 %psum.110 = f32[3,16]{1,0:T(4,128)} all-reduce(f32[3,16]{1,0:T(4,128)} %pad_maximum_fusion.6), channel_id=1, replica_groups=mesh['rows_0'=4,'rows_1'=4,'rows_2'=4,'grp_0'=2,'grp_1'=2] {'rows_0'}, use_global_device_ids=true, to_apply=%region_10.15 | all-reduce | flops 48 | bytes 384 | tf_op jit(solution)/shard_map/psum | solution.py:72
  163.9 8.8 %psum.111 = f32[3,16]{1,0:T(4,128)} all-reduce(f32[3,16]{1,0:T(4,128)} %psum.110), channel_id=1, replica_groups=mesh['rows_0'=4,'rows_1'=4,'rows_2'=4,'grp_0'=2,'grp_1'=2] {'rows_1'}, use_global_device_ids=true, to_apply=%region_11.16 | all-reduce | flops 48 | bytes 384 | tf_op jit(solution)/shard_map/psum | solution.py:72
  172.7 7.5 %psum.112 = f32[3,16]{1,0:T(4,128)} all-reduce(f32[3,16]{1,0:T(4,128)} %psum.111), channel_id=1, replica_groups=mesh['rows_0'=4,'rows_1'=4,'rows_2'=4,'grp_0'=2,'grp_1'=2] {'rows_2'}, use_global_device_ids=true, to_apply=%region_12.17 | all-reduce | flops 48 | bytes 384 | tf_op jit(solution)/shard_map/psum | solution.py:72
  180.2 4.5 %psum.113 = f32[3,16]{1,0:T(4,128)} all-reduce(f32[3,16]{1,0:T(4,128)} %psum.112), channel_id=1, replica_groups=mesh['rows_0'=4,'rows_1'=4,'rows_2'=4,'grp_0'=2,'grp_1'=2] {'grp_0'}, use_global_device_ids=true, to_apply=%region_13.18 | all-reduce | flops 48 | bytes 384 | tf_op jit(solution)/shard_map/psum | solution.py:72
  184.7 11.8 %psum.114 = f32[3,16]{1,0:T(4,128)} all-reduce(f32[3,16]{1,0:T(4,128)} %psum.113), channel_id=1, replica_groups=mesh['rows_0'=4,'rows_1'=4,'rows_2'=4,'grp_0'=2,'grp_1'=2] {'grp_1'}, use_global_device_ids=true, to_apply=%region_14.19 | all-reduce | flops 48 | bytes 384 | tf_op jit(solution)/shard_map/psum | solution.py:72
  197.8 1.7 fusion.55
  201.7 1.6 fusion.13
  207.5 3.8 %collective-permute-start.4 = (bf16[4,16,384]{2,1,0:T(8,128)(2,1)}, bf16[4,16,384]{2,1,0:T(8,128)(2,1)}, u32[]{:S(2)}, u32[]{:S(2)}) collective-permute-start(bf16[4,16,384]{2,1,0:T(8,128)(2,1)} %copy-done.1), channel_id=1, source_target_pairs={{0,1},{1,2},{2,3},{3,4},{4,5},{5,6},{6,7},{7,8},{8,9},{9,10},{10,1... | collective-permute-start | bytes 147464 | tf_op jit(solution)/shard_map/ppermute | solution.py:26
  211.3 1.9 collective-permute-start.5
  215.9 3.8 %all-to-all-start.4 = ((f32[4,1,512]{2,1,0:T(1,128)}), f32[4,1,512]{2,1,0:T(1,128)}, u32[]{:S(2)}, u32[]{:S(2)}) async-start(f32[4,1,512]{2,1,0:T(1,128)} %broadcast_in_dim.61), calls=%async_computation.4 | async-start | bytes 16384 | tf_op jit(solution)/shard_map/all_to_all | solution.py:40
  221.0 2.0 all-to-all-done.4
  224.3 4.5 %all-to-all-start.3 = ((bf16[4,5,512]{2,1,0:T(8,128)(2,1)}), bf16[4,5,512]{2,1,0:T(8,128)(2,1)}, u32[]{:S(2)}, u32[]{:S(2)}) async-start(bf16[4,5,512]{2,1,0:T(8,128)(2,1)} %broadcast_in_dim.60), calls=%async_computation.3 | async-start | bytes 65536 | tf_op jit(solution)/shard_map/all_to_all | solution.py:40
  231.5 2.5 reduce.3
  235.5 9.5 %all-to-all-start.5 = ((bf16[64,2,256]{2,1,0:T(2,128)(2,1)}), bf16[64,2,256]{2,1,0:T(2,128)(2,1)}, u32[]{:S(2)}, u32[]{:S(2)}) async-start(bf16[64,2,256]{2,1,0:T(2,128)(2,1)} %reshape.583), calls=%async_computation.5 | async-start | bytes 131072 | tf_op jit(solution)/shard_map/all_to_all | solution.py:40
  246.4 3.4 collective-permute-start.6
  251.1 1.5 pad_maximum_fusion.1
  252.7 2.3 gather_fusion.4
  254.9 2.7 fusion
  261.5 1.5 slice.66
  263.6 2.0 gather_fusion.6
  272.5 2.2 gather_fusion.5
  276.1 1.5 reshape.458
  277.6 1.6 copy.61
  279.2 1.7 reshape.459
  280.8 1.6 fusion.65
  283.9 1.5 reshape.584
  285.4 1.5 copy.82
  286.9 2.1 gather_fusion.7
  294.5 1.6 fusion.6
  296.1 2.8 multiply_reduce_fusion.1
  299.5 14.0 %psum.115 = f32[5,16]{1,0:T(8,128)S(1)} all-reduce(f32[5,16]{1,0:T(8,128)S(1)} %stack.49), channel_id=1, replica_groups=mesh['rows_0'=4,'rows_1'=4,'rows_2'=4,'grp_0'=2,'grp_1'=2] {'rows_0'}, use_global_device_ids=true, to_apply=%region_21.26 | all-reduce | flops 80 | bytes 640 | tf_op jit(solution)/shard_map/psum | solution.py:72
  313.6 8.1 %psum.116 = f32[5,16]{1,0:T(8,128)S(1)} all-reduce(f32[5,16]{1,0:T(8,128)S(1)} %psum.115), channel_id=1, replica_groups=mesh['rows_0'=4,'rows_1'=4,'rows_2'=4,'grp_0'=2,'grp_1'=2] {'rows_1'}, use_global_device_ids=true, to_apply=%region_22.27 | all-reduce | flops 80 | bytes 640 | tf_op jit(solution)/shard_map/psum | solution.py:72
  321.7 7.1 %psum.117 = f32[5,16]{1,0:T(8,128)S(1)} all-reduce(f32[5,16]{1,0:T(8,128)S(1)} %psum.116), channel_id=1, replica_groups=mesh['rows_0'=4,'rows_1'=4,'rows_2'=4,'grp_0'=2,'grp_1'=2] {'rows_2'}, use_global_device_ids=true, to_apply=%region_23.28 | all-reduce | flops 80 | bytes 640 | tf_op jit(solution)/shard_map/psum | solution.py:72
  328.8 3.8 %psum.118 = f32[5,16]{1,0:T(8,128)S(1)} all-reduce(f32[5,16]{1,0:T(8,128)S(1)} %psum.117), channel_id=1, replica_groups=mesh['rows_0'=4,'rows_1'=4,'rows_2'=4,'grp_0'=2,'grp_1'=2] {'grp_0'}, use_global_device_ids=true, to_apply=%region_24.29 | all-reduce | flops 80 | bytes 640 | tf_op jit(solution)/shard_map/psum | solution.py:72
  332.7 10.8 %psum.119 = f32[5,16]{1,0:T(8,128)S(1)} all-reduce(f32[5,16]{1,0:T(8,128)S(1)} %psum.118), channel_id=1, replica_groups=mesh['rows_0'=4,'rows_1'=4,'rows_2'=4,'grp_0'=2,'grp_1'=2] {'grp_1'}, use_global_device_ids=true, to_apply=%region_25.30 | all-reduce | flops 80 | bytes 640 | tf_op jit(solution)/shard_map/psum | solution.py:72
  344.3 1.7 multiply_subtract_fusion
  (112 shorter events, 88.5 us)
Async XLA Ops:
  0.6 103.4 %copy-start = (bf16[4,3,384,384]{3,2,1,0:T(8,128)(2,1)S(1)}, bf16[4,3,384,384]{3,2,1,0:T(8,128)(2,1)}, u32[]{:S(2)}) copy-start(bf16[4,3,384,384]{3,2,1,0:T(8,128)(2,1)} %param.23) | copy-start | bytes 10616836
  46.5 6.5 %copy-start.8 = (f32[16]{0:T(128)}, f32[16]{0:T(128)S(1)}, u32[]{:S(2)}) copy-start(f32[16]{0:T(128)S(1)} %sqrt_bitcast_fusion) | copy-start | bytes 196
  48.1 52.2 %collective-permute-start = (bf16[4,16,384]{2,1,0:T(8,128)(2,1)}, bf16[4,16,384]{2,1,0:T(8,128)(2,1)}, u32[]{:S(2)}, u32[]{:S(2)}) collective-permute-start(bf16[4,16,384]{2,1,0:T(8,128)(2,1)} %fusion.49), channel_id=1, source_target_pairs={{0,1},{1,2},{2,3},{3,4},{4,5},{5,6},{6,7},{7,8},{8,9},{9,10},{10,1... | collective-permute-start | bytes 147464 | tf_op jit(solution)/shard_map/ppermute | solution.py:26
  50.9 49.3 %collective-permute-start.1 = (bf16[4,16,384]{2,1,0:T(8,128)(2,1)}, bf16[4,16,384]{2,1,0:T(8,128)(2,1)}, u32[]{:S(2)}, u32[]{:S(2)}) collective-permute-start(bf16[4,16,384]{2,1,0:T(8,128)(2,1)} %fusion.49), channel_id=1, source_target_pairs={{1,0},{2,1},{3,2},{4,3},{5,4},{6,5},{7,6},{8,7},{9,8},{10,9},{11,1... | collective-permute-start | bytes 147464 | tf_op jit(solution)/shard_map/ppermute | solution.py:27
  55.1 0.6 copy-start.6
  59.8 14.1 %all-to-all-start.1 = ((f32[4,1,512]{2,1,0:T(1,128)}), f32[4,1,512]{2,1,0:T(1,128)}, u32[]{:S(2)}, u32[]{:S(2)}) async-start(f32[4,1,512]{2,1,0:T(1,128)} %broadcast_in_dim.58), calls=%async_computation.1 | async-start | bytes 16384 | tf_op jit(solution)/shard_map/all_to_all | solution.py:40
  74.5 10.5 %all-to-all-start = ((bf16[4,5,512]{2,1,0:T(8,128)(2,1)}), bf16[4,5,512]{2,1,0:T(8,128)(2,1)}, u32[]{:S(2)}, u32[]{:S(2)}) async-start(bf16[4,5,512]{2,1,0:T(8,128)(2,1)} %broadcast_in_dim.57), calls=%async_computation | async-start | bytes 65536 | tf_op jit(solution)/shard_map/all_to_all | solution.py:40
  83.4 60.3 %copy-start.2 = (f32[1,32,32]{2,1,0:T(8,128)S(1)}, f32[1,32,32]{2,1,0:T(8,128)}, u32[]{:S(2)}) copy-start(f32[1,32,32]{2,1,0:T(8,128)} %param.31) | copy-start | bytes 12292
  84.9 48.1 %all-to-all-start.2 = ((bf16[64,2,256]{2,1,0:T(2,128)(2,1)}), bf16[64,2,256]{2,1,0:T(2,128)(2,1)}, u32[]{:S(2)}, u32[]{:S(2)}) async-start(bf16[64,2,256]{2,1,0:T(2,128)(2,1)} %reshape.581), calls=%async_computation.2 | async-start | bytes 131072 | tf_op jit(solution)/shard_map/all_to_all | solution.py:40
  95.5 11.2 %collective-permute-start.2 = (bf16[20,512]{1,0:T(8,128)(2,1)}, bf16[20,512]{1,0:T(8,128)(2,1)}, u32[]{:S(2)}, u32[]{:S(2)}) collective-permute-start(bf16[20,512]{1,0:T(8,128)(2,1)} %reshape_reshape_reshape.6), channel_id=1, source_target_pairs={{0,4},{4,8},{8,12},{12,16},{16,20},{20,24},{24,28},{28,32},{32,36}... | collective-permute-start | bytes 61448 | tf_op jit(solution)/shard_map/ppermute | solution.py:63
  98.9 7.8 %collective-permute-start.3 = (bf16[20,512]{1,0:T(8,128)(2,1)}, bf16[20,512]{1,0:T(8,128)(2,1)}, u32[]{:S(2)}, u32[]{:S(2)}) collective-permute-start(bf16[20,512]{1,0:T(8,128)(2,1)} %reshape_reshape_reshape.6), channel_id=1, source_target_pairs={{4,0},{8,4},{12,8},{16,12},{20,16},{24,20},{28,24},{32,28},{36,32}... | collective-permute-start | bytes 61448 | tf_op jit(solution)/shard_map/ppermute | solution.py:66
  104.0 2.7 copy-start.5
  197.2 0.6 copy-start.7
  199.5 0.6 copy-start.1
  201.1 0.6 copy-start.3
  207.5 43.6 %collective-permute-start.4 = (bf16[4,16,384]{2,1,0:T(8,128)(2,1)}, bf16[4,16,384]{2,1,0:T(8,128)(2,1)}, u32[]{:S(2)}, u32[]{:S(2)}) collective-permute-start(bf16[4,16,384]{2,1,0:T(8,128)(2,1)} %copy-done.1), channel_id=1, source_target_pairs={{0,1},{1,2},{2,3},{3,4},{4,5},{5,6},{6,7},{7,8},{8,9},{9,10},{10,1... | collective-permute-start | bytes 147464 | tf_op jit(solution)/shard_map/ppermute | solution.py:26
  211.3 39.8 %collective-permute-start.5 = (bf16[4,16,384]{2,1,0:T(8,128)(2,1)}, bf16[4,16,384]{2,1,0:T(8,128)(2,1)}, u32[]{:S(2)}, u32[]{:S(2)}) collective-permute-start(bf16[4,16,384]{2,1,0:T(8,128)(2,1)} %copy-done.1), channel_id=1, source_target_pairs={{1,0},{2,1},{3,2},{4,3},{5,4},{6,5},{7,6},{8,7},{9,8},{10,9},{11,1... | collective-permute-start | bytes 147464 | tf_op jit(solution)/shard_map/ppermute | solution.py:27
  215.9 7.1 %all-to-all-start.4 = ((f32[4,1,512]{2,1,0:T(1,128)}), f32[4,1,512]{2,1,0:T(1,128)}, u32[]{:S(2)}, u32[]{:S(2)}) async-start(f32[4,1,512]{2,1,0:T(1,128)} %broadcast_in_dim.61), calls=%async_computation.4 | async-start | bytes 16384 | tf_op jit(solution)/shard_map/all_to_all | solution.py:40
  224.3 11.2 %all-to-all-start.3 = ((bf16[4,5,512]{2,1,0:T(8,128)(2,1)}), bf16[4,5,512]{2,1,0:T(8,128)(2,1)}, u32[]{:S(2)}, u32[]{:S(2)}) async-start(bf16[4,5,512]{2,1,0:T(8,128)(2,1)} %broadcast_in_dim.60), calls=%async_computation.3 | async-start | bytes 65536 | tf_op jit(solution)/shard_map/all_to_all | solution.py:40
  235.5 48.3 %all-to-all-start.5 = ((bf16[64,2,256]{2,1,0:T(2,128)(2,1)}), bf16[64,2,256]{2,1,0:T(2,128)(2,1)}, u32[]{:S(2)}, u32[]{:S(2)}) async-start(bf16[64,2,256]{2,1,0:T(2,128)(2,1)} %reshape.583), calls=%async_computation.5 | async-start | bytes 131072 | tf_op jit(solution)/shard_map/all_to_all | solution.py:40
  246.4 11.2 %collective-permute-start.6 = (bf16[20,512]{1,0:T(8,128)(2,1)}, bf16[20,512]{1,0:T(8,128)(2,1)}, u32[]{:S(2)}, u32[]{:S(2)}) collective-permute-start(bf16[20,512]{1,0:T(8,128)(2,1)} %reshape_reshape_reshape.7), channel_id=1, source_target_pairs={{0,4},{4,8},{8,12},{12,16},{16,20},{20,24},{24,28},{28,32},{32,36}... | collective-permute-start | bytes 61448 | tf_op jit(solution)/shard_map/ppermute | solution.py:63
  249.8 7.8 %collective-permute-start.7 = (bf16[20,512]{1,0:T(8,128)(2,1)}, bf16[20,512]{1,0:T(8,128)(2,1)}, u32[]{:S(2)}, u32[]{:S(2)}) collective-permute-start(bf16[20,512]{1,0:T(8,128)(2,1)} %reshape_reshape_reshape.7), channel_id=1, source_target_pairs={{4,0},{8,4},{12,8},{16,12},{20,16},{24,20},{28,24},{32,28},{36,32}... | collective-permute-start | bytes 61448 | tf_op jit(solution)/shard_map/ppermute | solution.py:66
  254.9 2.7 copy-start.4
where the time goes:
time: 352 us; the launch traced here: 347 us
  blocking collectives  136 us (39%)
  local copies, waits for them, and re-layouts  86 us (24%)
  starting transfers between devices  54.8 us (16%)
  other arithmetic  40 us (11%)
  matrix products  27.6 us (8%)
    psum x15, blocking collectives, by_axis(): return functools.reduce(lax.psum, axes, array)  136 us
    all_to_all x6, starting transfers between devices, from_everyone(): return lax.all_to_all(copies, axis, split_axis=0, concat_axis=0, tiled=True)  34.7 us
    reshape x10, local copies, waits for them, and re-layouts, pick_flat(): chosen = chosen.reshape(target_count, slot_count, -1, R)  13.9 us
    gather x6, local copies, waits for them, and re-layouts, pick_flat(): chosen = jnp.take(source, indices, axis=0)  12.6 us
    unnamed x26, local copies, waits for them, and re-layouts  12.2 us
    select_n x6, other arithmetic, pick_flat(): chosen = jnp.take(source, indices, axis=0)  8.31 us
    broadcast_in_dim x7, local copies, waits for them, and re-layouts, from_everyone(): copies = jnp.broadcast_to(array, (lax.axis_size(axis), *array.shape))  7.1 us
  transfers between devices with their start and end apart: 14, of which 1 were waited for; matrix products, arithmetic and copies ran while one was open for 30% of the time, Pallas kernels for 0%

commit v1 on v0

v1 whole, which is shorter than its diff:
```python
import jax
import jax.numpy as jnp
from jax import lax
from jax.experimental import pallas as pl
from jax.experimental.pallas import tpu as pltpu
from jax.sharding import Mesh
from jax.sharding import PartitionSpec as P

R = 32
GRP = ("grp_0", "grp_1")
ROWS = ("rows_0", "rows_1", "rows_2")
ROWS_GRP = ("rows_0", "rows_1", "rows_2", "grp_0", "grp_1")
BF = jnp.bfloat16
F32 = jnp.float32

epsilon = 1e-06
SMALL = 2.0**-40
SWITCH = 2.0**-20

NT = (((1,), (1,)), ((), ()))
NN = (((1,), (0,)), ((), ()))

VMEM = pl.BlockSpec(memory_space=pltpu.VMEM)
SMEM = pl.BlockSpec(memory_space=pltpu.SMEM)


def dot(left, right, dims=NN):
    return lax.dot_general(left, right, dims, preferred_element_type=F32)


def row_col(shape):
    return (
        lax.broadcasted_iota(jnp.int32, shape, 0),
        lax.broadcasted_iota(jnp.int32, shape, 1),
    )


def diagonal(leaves, nrhs):
    row, col = row_col((leaves * nrhs, leaves * R))
    return row // nrhs == col // R


def over_leaves(array, leaves):
    step = array.shape[0] // leaves
    total = array[:step]
    for l in range(1, leaves):
        total = total + array[l * step : (l + 1) * step]
    return total


def coefficients(field_bf, col_basis, leaf_transfer, box_transfer, packet_ref, parent_ref):
    leaves = col_basis.shape[0]
    nrhs = field_bf.shape[0] // leaves
    full = dot(field_bf, col_basis.reshape(leaves * R, -1), NT)
    leaf = over_leaves(jnp.where(diagonal(leaves, nrhs), full, 0.0), leaves).astype(BF)
    transfer = leaf_transfer.reshape(leaves * R, R).astype(BF)
    box = dot(leaf, transfer).astype(BF)
    parent = dot(box, box_transfer.astype(BF)).astype(BF)
    row, col = row_col((R, leaves * R))
    spread = dot(box, (row == col).astype(BF)).astype(BF)
    packet = jnp.concatenate([leaf, spread], axis=0)
    packet_ref[...] = jnp.broadcast_to(packet[None], packet_ref.shape)
    tiled = dot(parent, (row == col % R).astype(BF))
    per_row = nrhs * R // (leaves * R)
    row, col = row_col((nrhs, leaves * R))
    tiled = jnp.where(row // per_row == col // R, tiled, 0.0).astype(BF)
    row, col = row_col((8, nrhs))
    dense = dot((row == col % per_row).astype(BF), tiled).astype(BF)[:per_row]
    parent_ref[...] = jnp.broadcast_to(dense[None], parent_ref.shape)


def start_kernel(vector, col_basis, leaf_transfer, box_transfer, field_ref, packet_ref, parent_ref):
    leaves, nrhs, width = vector.shape
    field = vector[...].reshape(leaves * nrhs, width).astype(BF)
    field_ref[...] = field
    coefficients(
        field, col_basis[...], leaf_transfer[...], box_transfer[0], packet_ref, parent_ref
    )


def near_kernel(near_cols, low, field, high, blocks, out, window):
    nrhs = out.shape[0]
    leaves = field.shape[0] // nrhs
    leaf = pl.program_id(0)

    @pl.when(leaf == 0)
    def _():
        for i, part in enumerate((low, field, high)):
            window[i * leaves : (i + 1) * leaves] = part[...].reshape(leaves, nrhs, -1)

    base = device_index() * leaves - leaves
    total = None
    for k in range(blocks.shape[1]):
        picked = window[near_cols[leaf, k] - base]
        term = dot(picked, blocks[0, k], NT)
        total = term if total is None else total + term
    out[...] = total


def device_index():
    index = lax.axis_index(ROWS_GRP[0])
    for axis in ROWS_GRP[1:]:
        index = index * lax.axis_size(axis) + lax.axis_index(axis)
    return index


def row_index():
    index = lax.axis_index(ROWS[0])
    for axis in ROWS[1:]:
        index = index * lax.axis_size(axis) + lax.axis_index(axis)
    return index


def fine_kernel(
    leaf_far, box_far, low, own, high, leaf_coupling, box_coupling, leaf_out, box_out, window
):
    group = own.shape[0]
    nrhs = box_out.shape[0]
    lanes = own.shape[2]
    leaves, kf = leaf_far.shape
    for i, part in enumerate((low, own, high)):
        window[i * group : (i + 1) * group] = part[...]
    first_box = (row_index() - 1) * group
    first_leaf = first_box * leaves
    _, col = row_col((nrhs, lanes))
    block = col // R
    per_tile = lanes // R
    rows = []
    for l in range(leaves):
        tiles = []
        for t in range(kf // per_tile):
            tile = jnp.zeros((nrhs, lanes), F32)
            for i in range(per_tile):
                index = leaf_far[l, t * per_tile + i] - first_leaf
                box = index // leaves
                item = index - box * leaves
                values = window[box, :nrhs].astype(F32)
                shift = lax.rem(i - item + per_tile, per_tile) * R
                values = pltpu.roll(values, shift, 1)
                tile = jnp.where(block == i, values, tile)
            tiles.append(tile.astype(BF))
        rows.append(jnp.concatenate(tiles, axis=1))
    gathered = jnp.concatenate(rows, axis=0)
    leaf_out[...] = dot(gathered, leaf_coupling[...].reshape(leaves * R, -1), NT)
    tile = jnp.zeros((nrhs, lanes), F32)
    for k in range(box_far.shape[1]):
        values = window[box_far[0, k] - first_box, nrhs:].astype(F32)
        if k:
            values = pltpu.roll(values, k * R, 1)
        tile = tile + values
    box_out[...] = dot(tile.astype(BF), box_coupling[0], NT)


def downward(
    coarse_far, parents, near, leaf_field, box_field, coarse_coupling, box_transfer,
    leaf_transfer, row_basis, stack,
):
    leaves = row_basis.shape[0]
    nrhs = near.shape[0] // leaves
    group = 4
    kc = coarse_far.shape[1]
    per_row, lanes = parents.shape[1:]
    for k in range(kc):
        first = coarse_far[0, k] * group
        total = parents[first].astype(F32)
        for j in range(1, group):
            total = total + parents[first + j].astype(F32)
        stack[k * per_row : (k + 1) * per_row] = total
    dense = stack[...].astype(BF)
    row, col = row_col((kc * nrhs, kc * per_row))
    pick = (row // nrhs == col // per_row) & (row % per_row == col % per_row)
    wide = dot(pick.astype(BF), dense)
    row, col = row_col((kc * nrhs, lanes))
    wide = jnp.where(row % nrhs // per_row == col // R, wide, 0.0)
    half = wide + pltpu.roll(wide, 2 * R, 1)
    wide = half + pltpu.roll(half, R, 1)
    wide = jnp.where(row // nrhs == col // R, wide, 0.0)
    gathered = over_leaves(wide, kc).astype(BF)
    group_field = dot(gathered, coarse_coupling[0], NT)
    box_local = box_field[...] + dot(group_field.astype(BF), box_transfer[0].astype(BF), NT)
    transfer = leaf_transfer[...].reshape(leaves * R, R).astype(BF)
    shared = dot(box_local.astype(BF), transfer, NT)
    local = leaf_field[...] + jnp.concatenate([shared] * leaves, axis=0)
    local = jnp.where(diagonal(leaves, nrhs), local, 0.0).astype(BF)
    return near[...] + dot(local, row_basis[...].reshape(leaves * R, -1))


def middle_kernel(
    coarse_far, parents, near, leaf_field, box_field, coarse_coupling, box_transfer,
    leaf_transfer, row_basis, col_basis, image_ref, field_ref, packet_ref, parent_ref, stack,
):
    image = downward(
        coarse_far, parents, near, leaf_field, box_field, coarse_coupling, box_transfer,
        leaf_transfer, row_basis, stack,
    )
    image_ref[...] = image
    field = image.astype(BF)
    field_ref[...] = field
    coefficients(
        field, col_basis[...], leaf_transfer[...], box_transfer[0], packet_ref, parent_ref
    )


def products_kernel(
    coarse_far, parents, near, leaf_field, box_field, coarse_coupling, box_transfer,
    leaf_transfer, row_basis, vector, image, second_ref, sums_ref, stack,
):
    leaves, nrhs, width = vector.shape
    second = downward(
        coarse_far, parents, near, leaf_field, box_field, coarse_coupling, box_transfer,
        leaf_transfer, row_basis, stack,
    )
    second_ref[...] = second
    first = vector[...].reshape(leaves * nrhs, width)
    middle = image[...]
    small = second * SMALL
    pairs = (
        (first, first), (first, middle), (middle, middle), (first, second),
        (middle, second), (second, second), (middle, small), (small, small),
    )
    parts = []
    for left, right in pairs:
        product = over_leaves(left * right, leaves)
        part = product[:, :128]
        for i in range(1, width // 128):
            part = part + product[:, i * 128 : (i + 1) * 128]
        parts.append(part)
    table = jnp.concatenate(parts, axis=0)
    sums = jnp.sum(table.T, axis=0, keepdims=True)
    sums_ref[...] = jnp.broadcast_to(sums[None], sums_ref.shape)


def finish_kernel(sums, vector, image, second, basis_ref, remainder_ref, hessenberg_ref):
    leaves, nrhs, width = vector.shape
    count = sums.shape[0] * leaves * width
    total = jnp.sum(sums[...], axis=0)
    row, col = row_col((nrhs, total.shape[1]))
    total = jnp.broadcast_to(total, (nrhs, total.shape[1]))

    def mean(i):
        own = jnp.where(col == i * nrhs + row, total, 0.0)
        return jnp.sum(own, axis=1, keepdims=True) / count

    vv, vu, uu, vz = mean(0), mean(1), mean(2), mean(3)
    large = mean(7) > SWITCH
    uz = jnp.where(large, mean(6), mean(4))
    zz = jnp.where(large, mean(7), mean(5))
    unit = jnp.where(large, 1.0 / SMALL, 1.0)
    square_first = vv + epsilon
    norm_first = jnp.sqrt(square_first)
    ratio = vu / square_first
    proj_first = 0.5 * vv / square_first + ratio
    shift = proj_first - 0.5
    square_image = (uu - 2.0 * shift * vu + shift * shift * vv) / square_first
    norm_image = jnp.sqrt(square_image + epsilon)
    scale = 1.0 / (norm_first * norm_image)
    on_z = scale * unit
    on_u = scale * (0.5 - shift)
    on_v = -0.5 * shift * scale
    v_with = scale * vz + on_u * vu + on_v * vv
    u_with = on_z * uz + on_u * uu + on_v * vu
    proj_second = v_with / norm_first
    cross = scale * (vu - shift * vv) / norm_first
    proj_basis = scale * u_with - scale * shift * v_with - proj_second * cross
    on_u = on_u - proj_basis * scale
    on_v = on_v - proj_second / norm_first + proj_basis * scale * shift
    square_last = (
        on_z * (on_z * zz)
        + 2.0 * on_u * (on_z * uz)
        + 2.0 * on_v * (scale * vz)
        + on_u * (on_u * uu)
        + 2.0 * on_v * (on_u * vu)
        + on_v * (on_v * vv)
    )
    norm_last = jnp.sqrt(square_last + epsilon)
    for l in range(leaves):
        rows = pl.ds(l * nrhs, nrhs)
        v = vector[l]
        u = image[rows, :]
        basis_ref[l] = scale * u - (scale * shift) * v
        remainder_ref[l] = scale * second[rows, :] + on_u * u + on_v * v
    row, col = row_col((nrhs, 128))
    table = jnp.zeros((nrhs, 128), F32)
    for i, entry in enumerate((proj_first, norm_image, proj_second, proj_basis, norm_last)):
        table = jnp.where(col == i, entry, table)
    hessenberg_ref[...] = table[:, :5]


def shards(
    vector,
    near_cols,
    near_blocks,
    col_basis,
    row_basis,
    leaf_far,
    leaf_coupling,
    leaf_transfer,
    box_far,
    box_coupling,
    box_transfer,
    coarse_far,
    coarse_coupling,
):
    leaves, nrhs, width = vector.shape
    group = lax.axis_size(GRP)
    rows = lax.axis_size(ROWS)
    devices = rows * group
    kn = near_cols.shape[1]
    lanes = leaves * R
    flat = leaves * nrhs
    dense = nrhs * R // lanes
    shape = jax.ShapeDtypeStruct

    upward_out = (
        shape((flat, width), BF),
        shape((group, 2 * nrhs, lanes), BF),
        shape((devices, dense, lanes), BF),
    )

    def exchange(field, packet, parent):
        parents = lax.all_to_all(parent, ROWS_GRP, 0, 0, tiled=True)
        up = [(i, i + 1) for i in range(devices - 1)]
        down = [(b, a) for a, b in up]
        low_field = lax.ppermute(field, ROWS_GRP, up)
        high_field = lax.ppermute(field, ROWS_GRP, down)
        own = lax.all_to_all(packet, GRP, 0, 0, tiled=True)
        up = [(i, i + 1) for i in range(rows - 1)]
        down = [(b, a) for a, b in up]
        low = lax.ppermute(own, ROWS, up)
        high = lax.ppermute(own, ROWS, down)
        whole = pl.BlockSpec((flat, width), lambda l: (0, 0))
        near = pl.pallas_call(
            near_kernel,
            grid=(leaves,),
            in_specs=[
                SMEM, whole, whole, whole,
                pl.BlockSpec((1, kn, width, width), lambda l: (l, 0, 0, 0)),
            ],
            out_specs=pl.BlockSpec((nrhs, width), lambda l: (l, 0)),
            out_shape=shape((flat, width), F32),
            scratch_shapes=[pltpu.VMEM((3 * leaves, nrhs, width), BF)],
            name="near",
        )(near_cols, low_field, field, high_field, near_blocks)
        leaf_field, box_field = pl.pallas_call(
            fine_kernel,
            in_specs=[SMEM, SMEM] + [VMEM] * 5,
            out_specs=(VMEM, VMEM),
            out_shape=(shape((flat, lanes), F32), shape((nrhs, R), F32)),
            scratch_shapes=[pltpu.VMEM((3 * group, 2 * nrhs, lanes), BF)],
            name="fine",
        )(leaf_far, box_far, low, own, high, leaf_coupling, box_coupling)
        return (
            coarse_far, parents, near, leaf_field, box_field, coarse_coupling, box_transfer,
            leaf_transfer, row_basis,
        )

    stack = pltpu.VMEM((coarse_far.shape[1] * dense, lanes), F32)
    upward = pl.pallas_call(
        start_kernel,
        in_specs=[VMEM] * 4,
        out_specs=(VMEM,) * 3,
        out_shape=upward_out,
        name="start",
    )(vector, col_basis, leaf_transfer, box_transfer)
    image, *upward = pl.pallas_call(
        middle_kernel,
        in_specs=[SMEM] + [VMEM] * 9,
        out_specs=(VMEM,) * 4,
        out_shape=(shape((flat, width), F32), *upward_out),
        scratch_shapes=[stack],
        name="middle",
    )(*exchange(*upward), col_basis)
    second, sums = pl.pallas_call(
        products_kernel,
        in_specs=[SMEM] + [VMEM] * 10,
        out_specs=(VMEM,) * 2,
        out_shape=(shape((flat, width), F32), shape((devices, 1, 8 * nrhs), F32)),
        scratch_shapes=[stack],
        name="products",
    )(*exchange(*upward), vector, image)
    sums = lax.all_to_all(sums, ROWS_GRP, 0, 0, tiled=True)
    return pl.pallas_call(
        finish_kernel,
        in_specs=[VMEM] * 4,
        out_specs=(VMEM,) * 3,
        out_shape=(
            shape(vector.shape, F32),
            shape(vector.shape, F32),
            shape((nrhs, 5), F32),
        ),
        name="finish",
    )(sums, vector, image, second)


def solution(mesh):
    finer = Mesh(
        mesh.devices.reshape(4, 4, 4, 2, 2), ("rows_0", "rows_1", "rows_2", "grp_0", "grp_1")
    )
    placed = (
        P(ROWS_GRP, None, None),
        P(ROWS_GRP, None),
        P(ROWS_GRP, None, None, None),
        P(ROWS_GRP, None, None),
        P(ROWS_GRP, None, None),
        P(ROWS_GRP, None),
        P(ROWS_GRP, None, None),
        P(ROWS_GRP, None, None),
        P(ROWS_GRP, None),
        P(ROWS_GRP, None, None),
        P(ROWS_GRP, None, None),
        P(ROWS, None),
        P(ROWS, None, None),
    )
    return jax.shard_map(
        shards,
        mesh=finer,
        in_specs=placed,
        out_specs=(P(ROWS_GRP, None, None), P(ROWS_GRP, None, None), P()),
        check_vma=False,
    )
```

time: 352 us -> 138 us (0.39); the launches traced: 347 us -> 138 us
  blocking collectives: 136 us -> 50.6 us
  local copies, waits for them, and re-layouts: 86 us -> 7.55 us
  other arithmetic: 40 us -> 0 us
  matrix products: 27.6 us -> 0 us
  Pallas kernels: 0 us -> 23.3 us
    psum x15 -> x0, blocking collectives: 136 us -> none  [by_axis(): return functools.reduce(lax.psum, axes, array)]
    all_to_all x0 -> x3, blocking collectives: none -> 50.6 us  [the longest x1 33.6 us: shards(): sums = lax.all_to_all(sums, ROWS_GRP, 0, 0, tiled=True)]
    reshape x20 -> x0, local copies, waits for them, and re-layouts: 27.8 us -> none  [the longest x10 13.9 us: pick_flat(): chosen = chosen.reshape(target_count, slot_count, -1, R)]
    dot_general x16 -> x0, matrix products: 27.6 us -> none  [the longest x2 5.46 us: apply_operator(): jnp.einsum('lkbj,lkij->lbi', picked, near_blocks, preferred_element_type=...]
    pallas_call x0 -> x8, Pallas kernels: none -> 23.3 us  [the longest x2 8.84 us: exchange(): pl.pallas_call(near_kernel, grid=(leaves,), in_specs=[SMEM, whole, whole,...]
    gather x8 -> x0, local copies, waits for them, and re-layouts: 17.1 us -> none  [the longest x6 12.6 us: pick_flat(): chosen = jnp.take(source, indices, axis=0)]
    another operation x10 -> x0, local copies, waits for them, and re-layouts: 10.8 us -> none
    select_n x6 -> x0, other arithmetic: 8.31 us -> none  [pick_flat(): chosen = jnp.take(source, indices, axis=0)]
  transfers between devices with their start and end apart: 14 -> 10, of which waited for: 1 -> 0; matrix products, arithmetic and copies ran while one was open for 30% -> 0% of each run, Pallas kernels for 0% -> 9%
where the time goes in v1:
time: 138 us
  starting transfers between devices  55.2 us (40%)
  blocking collectives  50.6 us (37%)
  Pallas kernels  23.3 us (17%)
  local copies, waits for them, and re-layouts  7.55 us (5%)
    all_to_all x1, blocking collectives, shards(): sums = lax.all_to_all(sums, ROWS_GRP, 0, 0, tiled=True)  33.6 us
    all_to_all x2, starting transfers between devices, exchange(): parents = lax.all_to_all(parent, ROWS_GRP, 0, 0, tiled=True)  32.7 us
    all_to_all x2, blocking collectives, exchange(): own = lax.all_to_all(packet, GRP, 0, 0, tiled=True)  17.1 us
    pallas_call x2, Pallas kernels, exchange(): pl.pallas_call(near_kernel, grid=(leaves,), in_specs=[SMEM, whole, whole,...  8.84 us
    ppermute x2, starting transfers between devices, exchange(): high_field = lax.ppermute(field, ROWS_GRP, down)  8.11 us
    ppermute x2, starting transfers between devices, exchange(): low = lax.ppermute(own, ROWS, up)  7.98 us
    unnamed x24, local copies, waits for them, and re-layouts  6.19 us
    pallas_call x2, Pallas kernels, exchange(): pl.pallas_call(fine_kernel, in_specs=[SMEM, SMEM] + [VMEM] * 5, out_specs...  3.91 us
  transfers between devices with their start and end apart: 10, of which 0 were waited for; matrix products, arithmetic and copies ran while one was open for 0% of the time, Pallas kernels for 9%

profile of v1, /device:TPU:1, one launch (start us, length us, event | category | flops | bytes accessed | tf_op | source)
XLA Modules:
  0.0 137.5 jit_solution(180297653512736567)
XLA Ops:
  0.6 2.4 %start.1 = (bf16[64,384]{1,0:T(8,128)(2,1)}, bf16[4,32,128]{2,1,0:T(8,128)(2,1)}, bf16[256,4,128]{2,1,0:T(4,128)(2,1)}) custom-call(f32[4,16,384]{2,1,0:T(8,128)} %vector.5, bf16[4,32,384]{2,1,0:T(8,128)(2,1)} %col_basis.3, f32[4,32,32]{2,1,0:T(8,128)} %leaf_transfer.5, f32[1,32,32]{2,1,0:T(8,128)} %box_transfer.5), custom_call_target="tpu_custom_call" | custom-call | tf_op jit(solution)/shard_map/start/pallas_call | solution.py:358
  3.0 9.6 %all_to_all.25.own = bf16[4,32,128]{2,1,0:T(8,128)(2,1)S(1)} all-to-all(bf16[4,32,128]{2,1,0:T(8,128)(2,1)} %get-tuple-element.18), channel_id=1, replica_groups=mesh['rows_0'=4,'rows_1'=4,'rows_2'=4,'grp_0'=2,'grp_1'=2] {'grp_0','grp..., dimensions={0} | all-to-all | bytes 65536 | tf_op jit(solution)/shard_map/all_to_all | solution.py:326
  12.6 0.0 copy-start.2
  12.6 13.2 %all-to-all-start = ((bf16[256,4,128]{2,1,0:T(4,128)(2,1)}), bf16[256,4,128]{2,1,0:T(4,128)(2,1)S(1)}, u32[]{:S(2)}, u32[]{:S(2)}) async-start(bf16[256,4,128]{2,1,0:T(4,128)(2,1)} %get-tuple-element.16), calls=%async_computation | async-start | bytes 524288 | tf_op jit(solution)/shard_map/all_to_all | solution.py:321
  25.8 4.1 %collective-permute-start.1 = (bf16[64,384]{1,0:T(8,128)(2,1)}, bf16[64,384]{1,0:T(8,128)(2,1)S(1)}, u32[]{:S(2)}, u32[]{:S(2)}) collective-permute-start(bf16[64,384]{1,0:T(8,128)(2,1)} %get-tuple-element.17.field), channel_id=1, source_target_pairs={{1,0},{2,1},{3,2},{4,3},{5,4},{6,5},{7,6},{8,7},{9,8},{10,9},{11,1... | collective-permute-start | bytes 147464 | tf_op jit(solution)/shard_map/ppermute | solution.py:325
  29.9 1.9 %collective-permute-start = (bf16[64,384]{1,0:T(8,128)(2,1)}, bf16[64,384]{1,0:T(8,128)(2,1)S(1)}, u32[]{:S(2)}, u32[]{:S(2)}) collective-permute-start(bf16[64,384]{1,0:T(8,128)(2,1)} %get-tuple-element.17.field), channel_id=1, source_target_pairs={{0,1},{1,2},{2,3},{3,4},{4,5},{5,6},{6,7},{7,8},{8,9},{9,10},{10,1... | collective-permute-start | bytes 147464 | tf_op jit(solution)/shard_map/ppermute | solution.py:324
  31.8 1.3 collective-permute-start.3
  33.1 4.0 %collective-permute-start.2 = (bf16[4,32,128]{2,1,0:T(8,128)(2,1)S(1)}, bf16[4,32,128]{2,1,0:T(8,128)(2,1)S(1)}, u32[]{:S(2)}, u32[]{:S(2)}) collective-permute-start(bf16[4,32,128]{2,1,0:T(8,128)(2,1)S(1)} %all_to_all.25.own), channel_id=1, source_target_pairs={{0,4},{4,8},{8,12},{12,16},{16,20},{20,24},{24,28},{28,32},{32,36}... | collective-permute-start | bytes 98312 | tf_op jit(solution)/shard_map/ppermute | solution.py:329
  37.1 0.0 collective-permute-done.1.high
  37.1 0.0 copy-start.4
  37.1 0.0 collective-permute-done.low
  37.1 0.6 copy-done.4
  37.7 0.0 copy-start.6
  37.7 0.6 copy-done.6
  38.3 4.4 %near.2 = f32[64,384]{1,0:T(8,128)} custom-call(s32[4,3]{1,0:T(4,128)} %near_cols.3, bf16[64,384]{1,0:T(8,128)(2,1)} %copy-done.6, bf16[64,384]{1,0:T(8,128)(2,1)} %get-tuple-element.17.field, bf16[64,384]{1,0:T(8,128)(2,1)} %copy-done.4, bf16[4,3,384,384]{3,2,1,0:T(8,128)(2,1)} %blocks.3), custom_call_target="tpu_custom_call" | custom-call | tf_op jit(solution)/shard_map/near/pallas_call | solution.py:332
  42.8 0.0 collective-permute-done.3.high
  42.8 0.0 copy-start.8
  42.8 0.0 collective-permute-done.2.low
  42.8 0.0 copy-done.2
  42.8 0.6 copy-done.8
  43.4 0.0 copy-start.10
  43.4 0.6 copy-done.10
  44.0 2.0 %fine.2 = (f32[64,128]{1,0:T(8,128)}, f32[16,32]{1,0:T(8,128)}) custom-call(s32[4,8]{1,0:T(4,128)} %leaf_far.3, s32[1,4]{1,0:T(1,128)} %box_far.3, bf16[4,32,128]{2,1,0:T(8,128)(2,1)} %copy-done.10, bf16[4,32,128]{2,1,0:T(8,128)(2,1)} %copy-done.2, bf16[4,32,128]{2,1,0:T(8,128)(2,1)} %copy-done.8, bf16[4,32,256]{2,1,0:T(8,128)(2,1)} %leaf_coupling.3, ...), custom_call_target="tpu_custom_call" | custom-call | tf_op jit(solution)/shard_map/fine/pallas_call | solution.py:344
  45.9 0.0 all-to-all-done.parents
  45.9 0.0 copy-start
  45.9 0.7 copy-done
  46.6 3.3 %middle.1 = (f32[64,384]{1,0:T(8,128)}, bf16[64,384]{1,0:T(8,128)(2,1)}, bf16[4,32,128]{2,1,0:T(8,128)(2,1)}, bf16[256,4,128]{2,1,0:T(4,128)(2,1)}) custom-call(s32[1,4]{1,0:T(1,128)} %coarse_far.3, bf16[256,4,128]{2,1,0:T(4,128)(2,1)} %copy-done, f32[64,384]{1,0:T(8,128)} %near.2, f32[64,128]{1,0:T(8,128)} %get-tuple-element.19.leaf_field, ...), custom_call_target="tpu_custom_call" | custom-call | tf_op jit(solution)/shard_map/middle/pallas_call | solution.py:365
  49.9 7.5 %all_to_all.26.own = bf16[4,32,128]{2,1,0:T(8,128)(2,1)S(1)} all-to-all(bf16[4,32,128]{2,1,0:T(8,128)(2,1)} %get-tuple-element.23), channel_id=1, replica_groups=mesh['rows_0'=4,'rows_1'=4,'rows_2'=4,'grp_0'=2,'grp_1'=2] {'grp_0','grp..., dimensions={0} | all-to-all | bytes 65536 | tf_op jit(solution)/shard_map/all_to_all | solution.py:326
  57.4 0.0 copy-start.3
  57.4 19.5 %all-to-all-start.2 = ((bf16[256,4,128]{2,1,0:T(4,128)(2,1)}), bf16[256,4,128]{2,1,0:T(4,128)(2,1)S(1)}, u32[]{:S(2)}, u32[]{:S(2)}) async-start(bf16[256,4,128]{2,1,0:T(4,128)(2,1)} %get-tuple-element.21), calls=%async_computation.2 | async-start | bytes 524288 | tf_op jit(solution)/shard_map/all_to_all | solution.py:321
  76.9 4.1 %collective-permute-start.5 = (bf16[64,384]{1,0:T(8,128)(2,1)}, bf16[64,384]{1,0:T(8,128)(2,1)S(1)}, u32[]{:S(2)}, u32[]{:S(2)}) collective-permute-start(bf16[64,384]{1,0:T(8,128)(2,1)} %get-tuple-element.22.field), channel_id=1, source_target_pairs={{1,0},{2,1},{3,2},{4,3},{5,4},{6,5},{7,6},{8,7},{9,8},{10,9},{11,1... | collective-permute-start | bytes 147464 | tf_op jit(solution)/shard_map/ppermute | solution.py:325
  80.9 1.9 %collective-permute-start.4 = (bf16[64,384]{1,0:T(8,128)(2,1)}, bf16[64,384]{1,0:T(8,128)(2,1)S(1)}, u32[]{:S(2)}, u32[]{:S(2)}) collective-permute-start(bf16[64,384]{1,0:T(8,128)(2,1)} %get-tuple-element.22.field), channel_id=1, source_target_pairs={{0,1},{1,2},{2,3},{3,4},{4,5},{5,6},{6,7},{7,8},{8,9},{9,10},{10,1... | collective-permute-start | bytes 147464 | tf_op jit(solution)/shard_map/ppermute | solution.py:324
  82.9 1.3 collective-permute-start.7
  84.2 4.0 %collective-permute-start.6 = (bf16[4,32,128]{2,1,0:T(8,128)(2,1)S(1)}, bf16[4,32,128]{2,1,0:T(8,128)(2,1)S(1)}, u32[]{:S(2)}, u32[]{:S(2)}) collective-permute-start(bf16[4,32,128]{2,1,0:T(8,128)(2,1)S(1)} %all_to_all.26.own), channel_id=1, source_target_pairs={{0,4},{4,8},{8,12},{12,16},{16,20},{20,24},{24,28},{28,32},{32,36}... | collective-permute-start | bytes 98312 | tf_op jit(solution)/shard_map/ppermute | solution.py:329
  88.1 0.0 collective-permute-done.5.high
  88.2 0.0 copy-start.5
  88.2 0.0 collective-permute-done.4.low
  88.2 0.6 copy-done.5
  88.8 0.0 copy-start.7
  88.8 0.6 copy-done.7
  89.4 4.4 %near.3 = f32[64,384]{1,0:T(8,128)} custom-call(s32[4,3]{1,0:T(4,128)} %near_cols.3, bf16[64,384]{1,0:T(8,128)(2,1)} %copy-done.7, bf16[64,384]{1,0:T(8,128)(2,1)} %get-tuple-element.22.field, bf16[64,384]{1,0:T(8,128)(2,1)} %copy-done.5, bf16[4,3,384,384]{3,2,1,0:T(8,128)(2,1)} %blocks.3), custom_call_target="tpu_custom_call" | custom-call | tf_op jit(solution)/shard_map/near/pallas_call | solution.py:332
  93.8 0.0 collective-permute-done.7.high
  93.8 0.0 copy-start.9
  93.8 0.0 collective-permute-done.6.low
  93.8 0.0 copy-done.3
  93.8 0.6 copy-done.9
  94.4 0.0 copy-start.11
  94.4 0.6 copy-done.11
  95.0 2.0 %fine.3 = (f32[64,128]{1,0:T(8,128)}, f32[16,32]{1,0:T(8,128)}) custom-call(s32[4,8]{1,0:T(4,128)} %leaf_far.3, s32[1,4]{1,0:T(1,128)} %box_far.3, bf16[4,32,128]{2,1,0:T(8,128)(2,1)} %copy-done.11, bf16[4,32,128]{2,1,0:T(8,128)(2,1)} %copy-done.3, bf16[4,32,128]{2,1,0:T(8,128)(2,1)} %copy-done.9, bf16[4,32,256]{2,1,0:T(8,128)(2,1)} %leaf_coupling.3, ...), custom_call_target="tpu_custom_call" | custom-call | tf_op jit(solution)/shard_map/fine/pallas_call | solution.py:344
  97.0 0.0 all-to-all-done.2.parents
  97.0 0.0 copy-start.1
  97.0 0.7 copy-done.1
  97.7 2.8 %products.1 = (f32[64,384]{1,0:T(8,128)}, f32[256,1,128]{2,1,0:T(1,128)}) custom-call(s32[1,4]{1,0:T(1,128)} %coarse_far.3, bf16[256,4,128]{2,1,0:T(4,128)(2,1)} %copy-done.1, f32[64,384]{1,0:T(8,128)} %near.3, f32[64,128]{1,0:T(8,128)} %get-tuple-element.24.leaf_field, f32[16,32]{1,0:T(8,128)} %get-tuple-element.25.box_field, ...), custom_call_target="tpu_custom_call" | custom-call | tf_op jit(solution)/shard_map/products/pallas_call | solution.py:373
  100.5 33.6 %all_to_all.27.sums = f32[256,1,128]{2,1,0:T(1,128)} all-to-all(f32[256,1,128]{2,1,0:T(1,128)} %get-tuple-element.27), channel_id=1, replica_groups=mesh['rows_0'=4,'rows_1'=4,'rows_2'=4,'grp_0'=2,'grp_1'=2] {'rows_0','ro..., dimensions={0} | all-to-all | bytes 262144 | tf_op jit(solution)/shard_map/all_to_all | solution.py:381
  134.0 2.1 %finish.1 = (f32[4,16,384]{2,1,0:T(8,128)}, f32[4,16,384]{2,1,0:T(8,128)}, f32[16,5]{1,0:T(8,128)}) custom-call(f32[256,1,128]{2,1,0:T(1,128)} %all_to_all.27.sums, f32[4,16,384]{2,1,0:T(8,128)} %vector.5, f32[64,384]{1,0:T(8,128)} %get-tuple-element.26.image, f32[64,384]{1,0:T(8,128)} %get-tuple-element.28.second), custom_call_target="tpu_custom_call" | custom-call | tf_op jit(solution)/shard_map/finish/pallas_call | solution.py:382
  136.2 1.4 copy.16
Async XLA Ops:
  12.6 30.2 %copy-start.2 = (bf16[4,32,128]{2,1,0:T(8,128)(2,1)}, bf16[4,32,128]{2,1,0:T(8,128)(2,1)S(1)}, u32[]{:S(2)}) copy-start(bf16[4,32,128]{2,1,0:T(8,128)(2,1)S(1)} %all_to_all.25.own) | copy-start | bytes 98308
  12.6 33.3 %all-to-all-start = ((bf16[256,4,128]{2,1,0:T(4,128)(2,1)}), bf16[256,4,128]{2,1,0:T(4,128)(2,1)S(1)}, u32[]{:S(2)}, u32[]{:S(2)}) async-start(bf16[256,4,128]{2,1,0:T(4,128)(2,1)} %get-tuple-element.16), calls=%async_computation | async-start | bytes 524288 | tf_op jit(solution)/shard_map/all_to_all | solution.py:321
  25.8 11.3 %collective-permute-start.1 = (bf16[64,384]{1,0:T(8,128)(2,1)}, bf16[64,384]{1,0:T(8,128)(2,1)S(1)}, u32[]{:S(2)}, u32[]{:S(2)}) collective-permute-start(bf16[64,384]{1,0:T(8,128)(2,1)} %get-tuple-element.17.field), channel_id=1, source_target_pairs={{1,0},{2,1},{3,2},{4,3},{5,4},{6,5},{7,6},{8,7},{9,8},{10,9},{11,1... | collective-permute-start | bytes 147464 | tf_op jit(solution)/shard_map/ppermute | solution.py:325
  29.9 7.2 %collective-permute-start = (bf16[64,384]{1,0:T(8,128)(2,1)}, bf16[64,384]{1,0:T(8,128)(2,1)S(1)}, u32[]{:S(2)}, u32[]{:S(2)}) collective-permute-start(bf16[64,384]{1,0:T(8,128)(2,1)} %get-tuple-element.17.field), channel_id=1, source_target_pairs={{0,1},{1,2},{2,3},{3,4},{4,5},{5,6},{6,7},{7,8},{8,9},{9,10},{10,1... | collective-permute-start | bytes 147464 | tf_op jit(solution)/shard_map/ppermute | solution.py:324
  31.8 11.0 %collective-permute-start.3 = (bf16[4,32,128]{2,1,0:T(8,128)(2,1)S(1)}, bf16[4,32,128]{2,1,0:T(8,128)(2,1)S(1)}, u32[]{:S(2)}, u32[]{:S(2)}) collective-permute-start(bf16[4,32,128]{2,1,0:T(8,128)(2,1)S(1)} %all_to_all.25.own), channel_id=1, source_target_pairs={{4,0},{8,4},{12,8},{16,12},{20,16},{24,20},{28,24},{32,28},{36,32}... | collective-permute-start | bytes 98312 | tf_op jit(solution)/shard_map/ppermute | solution.py:330
  33.1 9.7 %collective-permute-start.2 = (bf16[4,32,128]{2,1,0:T(8,128)(2,1)S(1)}, bf16[4,32,128]{2,1,0:T(8,128)(2,1)S(1)}, u32[]{:S(2)}, u32[]{:S(2)}) collective-permute-start(bf16[4,32,128]{2,1,0:T(8,128)(2,1)S(1)} %all_to_all.25.own), channel_id=1, source_target_pairs={{0,4},{4,8},{8,12},{12,16},{16,20},{20,24},{24,28},{28,32},{32,36}... | collective-permute-start | bytes 98312 | tf_op jit(solution)/shard_map/ppermute | solution.py:329
  37.1 0.6 copy-start.4
  37.7 0.6 copy-start.6
  42.8 0.6 copy-start.8
  43.4 0.6 copy-start.10
  45.9 0.7 copy-start
  57.4 36.4 %copy-start.3 = (bf16[4,32,128]{2,1,0:T(8,128)(2,1)}, bf16[4,32,128]{2,1,0:T(8,128)(2,1)S(1)}, u32[]{:S(2)}) copy-start(bf16[4,32,128]{2,1,0:T(8,128)(2,1)S(1)} %all_to_all.26.own) | copy-start | bytes 98308
  57.4 39.6 %all-to-all-start.2 = ((bf16[256,4,128]{2,1,0:T(4,128)(2,1)}), bf16[256,4,128]{2,1,0:T(4,128)(2,1)S(1)}, u32[]{:S(2)}, u32[]{:S(2)}) async-start(bf16[256,4,128]{2,1,0:T(4,128)(2,1)} %get-tuple-element.21), calls=%async_computation.2 | async-start | bytes 524288 | tf_op jit(solution)/shard_map/all_to_all | solution.py:321
  76.9 11.3 %collective-permute-start.5 = (bf16[64,384]{1,0:T(8,128)(2,1)}, bf16[64,384]{1,0:T(8,128)(2,1)S(1)}, u32[]{:S(2)}, u32[]{:S(2)}) collective-permute-start(bf16[64,384]{1,0:T(8,128)(2,1)} %get-tuple-element.22.field), channel_id=1, source_target_pairs={{1,0},{2,1},{3,2},{4,3},{5,4},{6,5},{7,6},{8,7},{9,8},{10,9},{11,1... | collective-permute-start | bytes 147464 | tf_op jit(solution)/shard_map/ppermute | solution.py:325
  80.9 7.2 %collective-permute-start.4 = (bf16[64,384]{1,0:T(8,128)(2,1)}, bf16[64,384]{1,0:T(8,128)(2,1)S(1)}, u32[]{:S(2)}, u32[]{:S(2)}) collective-permute-start(bf16[64,384]{1,0:T(8,128)(2,1)} %get-tuple-element.22.field), channel_id=1, source_target_pairs={{0,1},{1,2},{2,3},{3,4},{4,5},{5,6},{6,7},{7,8},{8,9},{9,10},{10,1... | collective-permute-start | bytes 147464 | tf_op jit(solution)/shard_map/ppermute | solution.py:324
  82.9 11.0 %collective-permute-start.7 = (bf16[4,32,128]{2,1,0:T(8,128)(2,1)S(1)}, bf16[4,32,128]{2,1,0:T(8,128)(2,1)S(1)}, u32[]{:S(2)}, u32[]{:S(2)}) collective-permute-start(bf16[4,32,128]{2,1,0:T(8,128)(2,1)S(1)} %all_to_all.26.own), channel_id=1, source_target_pairs={{4,0},{8,4},{12,8},{16,12},{20,16},{24,20},{28,24},{32,28},{36,32}... | collective-permute-start | bytes 98312 | tf_op jit(solution)/shard_map/ppermute | solution.py:330
  84.2 9.7 %collective-permute-start.6 = (bf16[4,32,128]{2,1,0:T(8,128)(2,1)S(1)}, bf16[4,32,128]{2,1,0:T(8,128)(2,1)S(1)}, u32[]{:S(2)}, u32[]{:S(2)}) collective-permute-start(bf16[4,32,128]{2,1,0:T(8,128)(2,1)S(1)} %all_to_all.26.own), channel_id=1, source_target_pairs={{0,4},{4,8},{8,12},{12,16},{16,20},{20,24},{24,28},{28,32},{32,36}... | collective-permute-start | bytes 98312 | tf_op jit(solution)/shard_map/ppermute | solution.py:329
  88.2 0.6 copy-start.5
  88.8 0.6 copy-start.7
  93.8 0.6 copy-start.9
  94.4 0.6 copy-start.11
  97.0 0.7 copy-start.1

commit v2 on v1

--- a/solution.py
+++ b/solution.py
@@ -16,6 +16,7 @@
 epsilon = 1e-06
 SMALL = 2.0**-40
 SWITCH = 2.0**-20
+LIMIT = 16 * 2**20
 
 NT = (((1,), (1,)), ((), ()))
 NN = (((1,), (0,)), ((), ()))
@@ -48,60 +49,51 @@
     return total
 
 
-def coefficients(field_bf, col_basis, leaf_transfer, box_transfer, packet_ref, parent_ref):
+def coefficients(field_bf, col_basis, leaf_transfer, box_transfer, packet_ref):
     leaves = col_basis.shape[0]
+    lanes = leaves * R
     nrhs = field_bf.shape[0] // leaves
-    full = dot(field_bf, col_basis.reshape(leaves * R, -1), NT)
+    full = dot(field_bf, col_basis.reshape(lanes, -1), NT)
     leaf = over_leaves(jnp.where(diagonal(leaves, nrhs), full, 0.0), leaves).astype(BF)
-    transfer = leaf_transfer.reshape(leaves * R, R).astype(BF)
-    box = dot(leaf, transfer).astype(BF)
+    box = dot(leaf, leaf_transfer.reshape(lanes, R).astype(BF)).astype(BF)
     parent = dot(box, box_transfer.astype(BF)).astype(BF)
-    row, col = row_col((R, leaves * R))
-    spread = dot(box, (row == col).astype(BF)).astype(BF)
-    packet = jnp.concatenate([leaf, spread], axis=0)
+    row, col = row_col((R, lanes))
+    both = dot(box, (row == col).astype(BF)) + dot(parent, (row + R == col).astype(BF))
+    blocks = []
+    for l in range(leaves):
+        for t in range(field_bf.shape[1] // lanes):
+            blocks.append(field_bf[l * nrhs : (l + 1) * nrhs, t * lanes : (t + 1) * lanes])
+    blocks += [leaf, both.astype(BF)]
+    packet = jnp.concatenate(blocks, axis=0)
     packet_ref[...] = jnp.broadcast_to(packet[None], packet_ref.shape)
-    tiled = dot(parent, (row == col % R).astype(BF))
-    per_row = nrhs * R // (leaves * R)
-    row, col = row_col((nrhs, leaves * R))
+
+
+def start_kernel(vector, col_basis, leaf_transfer, box_transfer, packet_ref):
+    leaves, nrhs, width = vector.shape
+    field = vector[...].reshape(leaves * nrhs, width).astype(BF)
+    coefficients(field, col_basis[...], leaf_transfer[...], box_transfer[0], packet_ref)
+
+
+def group_kernel(own, side_ref, parent_ref):
+    group, size, lanes = own.shape
+    nrhs = 16
+    fields = size - 2 * nrhs
+    total = own[0, fields + nrhs :].astype(F32)
+    for j in range(1, group):
+        total = total + own[j, fields + nrhs :].astype(F32)
+    total = total.astype(BF)
+    row, col = row_col((lanes, lanes))
+    tiled = dot(total, ((row // R == 1) & (row % R == col % R)).astype(BF))
+    per_row = parent_ref.shape[1]
+    row, col = row_col((nrhs, lanes))
     tiled = jnp.where(row // per_row == col // R, tiled, 0.0).astype(BF)
     row, col = row_col((8, nrhs))
     dense = dot((row == col % per_row).astype(BF), tiled).astype(BF)[:per_row]
     parent_ref[...] = jnp.broadcast_to(dense[None], parent_ref.shape)
-
-
-def start_kernel(vector, col_basis, leaf_transfer, box_transfer, field_ref, packet_ref, parent_ref):
-    leaves, nrhs, width = vector.shape
-    field = vector[...].reshape(leaves * nrhs, width).astype(BF)
-    field_ref[...] = field
-    coefficients(
-        field, col_basis[...], leaf_transfer[...], box_transfer[0], packet_ref, parent_ref
-    )
-
-
-def near_kernel(near_cols, low, field, high, blocks, out, window):
-    nrhs = out.shape[0]
-    leaves = field.shape[0] // nrhs
-    leaf = pl.program_id(0)
-
-    @pl.when(leaf == 0)
-    def _():
-        for i, part in enumerate((low, field, high)):
-            window[i * leaves : (i + 1) * leaves] = part[...].reshape(leaves, nrhs, -1)
-
-    base = device_index() * leaves - leaves
-    total = None
-    for k in range(blocks.shape[1]):
-        picked = window[near_cols[leaf, k] - base]
-        term = dot(picked, blocks[0, k], NT)
-        total = term if total is None else total + term
-    out[...] = total
-
-
-def device_index():
-    index = lax.axis_index(ROWS_GRP[0])
-    for axis in ROWS_GRP[1:]:
-        index = index * lax.axis_size(axis) + lax.axis_index(axis)
-    return index
+    position = lax.axis_index(GRP[0]) * lax.axis_size(GRP[1]) + lax.axis_index(GRP[1])
+    side_ref[:fields] = own[position, :fields]
+    for j in range(group):
+        side_ref[fields + j * 2 * nrhs : fields + (j + 1) * 2 * nrhs] = own[j, fields:]
 
 
 def row_index():
@@ -111,15 +103,53 @@
     return index
 
 
+def near_kernel(near_cols, low, own, high, blocks, out, window, weights, sems):
+    leaves, kn, width, _ = blocks.shape
+    nrhs = out.shape[0] // leaves
+    group = own.shape[0]
+    fields = window.shape[1]
+    copies = [
+        pltpu.make_async_copy(blocks.at[l], weights.at[l], sems.at[l]) for l in range(leaves)
+    ]
+    for copy in copies:
+        copy.start()
+    window[0] = low[:fields]
+    for j in range(group):
+        window[j + 1] = own[j, :fields]
+    window[group + 1] = high[:fields]
+    base = (row_index() * group - 1) * leaves
+    tiles = fields // leaves // nrhs
+    for l in range(leaves):
+        picked = []
+        for k in range(kn):
+            index = near_cols[l, k] - base
+            device = index // leaves
+            first = (index - device * leaves) * (tiles * nrhs)
+            picked += [
+                window[device, pl.ds(pl.multiple_of(first + t * nrhs, nrhs), nrhs)]
+                for t in range(tiles)
+            ]
+        copies[l].wait()
+        total = None
+        for k in range(kn):
+            part = jnp.concatenate(picked[k * tiles : (k + 1) * tiles], axis=1)
+            term = dot(part, weights[l, k], NT)
+            total = term if total is None else total + term
+        out[l * nrhs : (l + 1) * nrhs] = total
+
+
 def fine_kernel(
     leaf_far, box_far, low, own, high, leaf_coupling, box_coupling, leaf_out, box_out, window
 ):
-    group = own.shape[0]
+    group, size, lanes = own.shape
     nrhs = box_out.shape[0]
-    lanes = own.shape[2]
     leaves, kf = leaf_far.shape
-    for i, part in enumerate((low, own, high)):
-        window[i * group : (i + 1) * group] = part[...]
+    fields = size - 2 * nrhs
+    for j in range(group):
+        rows = slice(fields + j * 2 * nrhs, fields + (j + 1) * 2 * nrhs)
+        window[j] = low[rows]
+        window[group + j] = own[j, fields:]
+        window[2 * group + j] = high[rows]
     first_box = (row_index() - 1) * group
     first_leaf = first_box * leaves
     _, col = row_col((nrhs, lanes))
@@ -147,7 +177,7 @@
         values = window[box_far[0, k] - first_box, nrhs:].astype(F32)
         if k:
             values = pltpu.roll(values, k * R, 1)
-        tile = tile + values
+        tile = jnp.where(block == k, values, tile)
     box_out[...] = dot(tile.astype(BF), box_coupling[0], NT)
 
 
@@ -157,15 +187,10 @@
 ):
     leaves = row_basis.shape[0]
     nrhs = near.shape[0] // leaves
-    group = 4
     kc = coarse_far.shape[1]
     per_row, lanes = parents.shape[1:]
     for k in range(kc):
-        first = coarse_far[0, k] * group
-        total = parents[first].astype(F32)
-        for j in range(1, group):
-            total = total + parents[first + j].astype(F32)
-        stack[k * per_row : (k + 1) * per_row] = total
+        stack[k * per_row : (k + 1) * per_row] = parents[coarse_far[0, k]].astype(F32)
     dense = stack[...].astype(BF)
     row, col = row_col((kc * nrhs, kc * per_row))
     pick = (row // nrhs == col // per_row) & (row % per_row == col % per_row)
@@ -187,17 +212,15 @@
 
 def middle_kernel(
     coarse_far, parents, near, leaf_field, box_field, coarse_coupling, box_transfer,
-    leaf_transfer, row_basis, col_basis, image_ref, field_ref, packet_ref, parent_ref, stack,
+    leaf_transfer, row_basis, col_basis, image_ref, packet_ref, stack,
 ):
     image = downward(
         coarse_far, parents, near, leaf_field, box_field, coarse_coupling, box_transfer,
         leaf_transfer, row_basis, stack,
     )
     image_ref[...] = image
-    field = image.astype(BF)
-    field_ref[...] = field
     coefficients(
-        field, col_basis[...], leaf_transfer[...], box_transfer[0], packet_ref, parent_ref
+        image.astype(BF), col_basis[...], leaf_transfer[...], box_transfer[0], packet_ref
     )
 
 
@@ -279,11 +302,11 @@
         u = image[rows, :]
         basis_ref[l] = scale * u - (scale * shift) * v
         remainder_ref[l] = scale * second[rows, :] + on_u * u + on_v * v
-    row, col = row_col((nrhs, 128))
-    table = jnp.zeros((nrhs, 128), F32)
-    for i, entry in enumerate((proj_first, norm_image, proj_second, proj_basis, norm_last)):
-        table = jnp.where(col == i, entry, table)
-    hessenberg_ref[...] = table[:, :5]
+    entries = (proj_first, norm_image, proj_second, proj_basis, norm_last)
+    row, col = row_col((nrhs, nrhs))
+    for i, entry in enumerate(entries):
+        line = jnp.sum(jnp.where(row == col, entry, 0.0), axis=0, keepdims=True)
+        hessenberg_ref[i : i + 1] = line
 
 
 def shards(
@@ -309,87 +332,99 @@
     lanes = leaves * R
     flat = leaves * nrhs
     dense = nrhs * R // lanes
+    tiles = width // lanes
+    size = (leaves * tiles + 2) * nrhs
+    side = (leaves * tiles + 2 * group) * nrhs
+    params = pltpu.CompilerParams(vmem_limit_bytes=LIMIT)
+
+    given = {id(a) for a in (
+        vector, near_cols, near_blocks, col_basis, row_basis, leaf_far, leaf_coupling,
+        leaf_transfer, box_far, box_coupling, box_transfer, coarse_far, coarse_coupling,
+    )}
+
+    def placed(arrays):
+        return [
+            pltpu.with_memory_space_constraint(a, pltpu.HBM if id(a) in given else pltpu.VMEM)
+            for a in arrays
+        ]
+
+    def made(*dims, dtype=F32):
+        return pltpu.VMEM(dims, dtype)
+
+    def call(kernel, inputs, outs, smem=(), hbm=(), scratch=()):
+        specs = [SMEM] * len(smem) + [VMEM] * len(inputs)
+        specs += [pl.BlockSpec(memory_space=pl.ANY)] * len(hbm)
+        return pl.pallas_call(
+            kernel,
+            in_specs=specs,
+            out_specs=[VMEM] * len(outs),
+            out_shape=outs,
+            scratch_shapes=scratch,
+            compiler_params=params,
+            name=kernel.__name__,
+        )(*placed(smem), *placed(inputs), *placed(hbm))
+
+    step = [
+        (i, (i // group + 1) * group + (i + 1) % group) for i in range(devices - group)
+    ]
+
+    def exchange(packet):
+        own = lax.all_to_all(packet, GRP, 0, 0, tiled=True)
+        sides, parent = call(
+            group_kernel, [own], [made(side, lanes, dtype=BF), made(rows, dense, lanes, dtype=BF)]
+        )
+        low = lax.ppermute(sides, ROWS_GRP, step)
+        high = lax.ppermute(sides, ROWS_GRP, [(b, a) for a, b in step])
+        parents = lax.all_to_all(parent, ROWS, 0, 0, tiled=True)
+        (near,) = call(
+            near_kernel,
+            [low, own, high],
+            [made(flat, width)],
+            smem=[near_cols],
+            hbm=[near_blocks],
+            scratch=[
+                pltpu.VMEM((group + 2, leaves * tiles * nrhs, lanes), BF),
+                pltpu.VMEM((leaves, kn, width, width), BF),
+                pltpu.SemaphoreType.DMA((leaves,)),
+            ],
+        )
+        leaf_field, box_field = call(
+            fine_kernel,
+            [low, own, high, leaf_coupling, box_coupling],
+            [made(flat, lanes), made(nrhs, R)],
+            smem=[leaf_far, box_far],
+            scratch=[pltpu.VMEM((3 * group, 2 * nrhs, lanes), BF)],
+        )
+        return [
+            parents, near, leaf_field, box_field, coarse_coupling, box_transfer, leaf_transfer,
+            row_basis,
+        ]
+
+    packet_out = made(group, size, lanes, dtype=BF)
+    stack = pltpu.VMEM((coarse_far.shape[1] * dense, lanes), F32)
+    (packet,) = call(start_kernel, [vector, col_basis, leaf_transfer, box_transfer], [packet_out])
+    image, packet = call(
+        middle_kernel,
+        exchange(packet) + [col_basis],
+        [made(flat, width), packet_out],
+        smem=[coarse_far],
+        scratch=[stack],
+    )
+    second, sums = call(
+        products_kernel,
+        exchange(packet) + [vector, image],
+        [made(flat, width), made(devices, 1, 8 * nrhs)],
+        smem=[coarse_far],
+        scratch=[stack],
+    )
+    sums = lax.all_to_all(sums, ROWS_GRP, 0, 0, tiled=True)
     shape = jax.ShapeDtypeStruct
-
-    upward_out = (
-        shape((flat, width), BF),
-        shape((group, 2 * nrhs, lanes), BF),
-        shape((devices, dense, lanes), BF),
-    )
-
-    def exchange(field, packet, parent):
-        parents = lax.all_to_all(parent, ROWS_GRP, 0, 0, tiled=True)
-        up = [(i, i + 1) for i in range(devices - 1)]
-        down = [(b, a) for a, b in up]
-        low_field = lax.ppermute(field, ROWS_GRP, up)
-        high_field = lax.ppermute(field, ROWS_GRP, down)
-        own = lax.all_to_all(packet, GRP, 0, 0, tiled=True)
-        up = [(i, i + 1) for i in range(rows - 1)]
-        down = [(b, a) for a, b in up]
-        low = lax.ppermute(own, ROWS, up)
-        high = lax.ppermute(own, ROWS, down)
-        whole = pl.BlockSpec((flat, width), lambda l: (0, 0))
-        near = pl.pallas_call(
-            near_kernel,
-            grid=(leaves,),
-            in_specs=[
-                SMEM, whole, whole, whole,
-                pl.BlockSpec((1, kn, width, width), lambda l: (l, 0, 0, 0)),
-            ],
-            out_specs=pl.BlockSpec((nrhs, width), lambda l: (l, 0)),
-            out_shape=shape((flat, width), F32),
-            scratch_shapes=[pltpu.VMEM((3 * leaves, nrhs, width), BF)],
-            name="near",
-        )(near_cols, low_field, field, high_field, near_blocks)
-        leaf_field, box_field = pl.pallas_call(
-            fine_kernel,
-            in_specs=[SMEM, SMEM] + [VMEM] * 5,
-            out_specs=(VMEM, VMEM),
-            out_shape=(shape((flat, lanes), F32), shape((nrhs, R), F32)),
-            scratch_shapes=[pltpu.VMEM((3 * group, 2 * nrhs, lanes), BF)],
-            name="fine",
-        )(leaf_far, box_far, low, own, high, leaf_coupling, box_coupling)
-        return (
-            coarse_far, parents, near, leaf_field, box_field, coarse_coupling, box_transfer,
-            leaf_transfer, row_basis,
-        )
-
-    stack = pltpu.VMEM((coarse_far.shape[1] * dense, lanes), F32)
-    upward = pl.pallas_call(
-        start_kernel,
-        in_specs=[VMEM] * 4,
-        out_specs=(VMEM,) * 3,
-        out_shape=upward_out,
-        name="start",
-    )(vector, col_basis, leaf_transfer, box_transfer)
-    image, *upward = pl.pallas_call(
-        middle_kernel,
-        in_specs=[SMEM] + [VMEM] * 9,
-        out_specs=(VMEM,) * 4,
-        out_shape=(shape((flat, width), F32), *upward_out),
-        scratch_shapes=[stack],
-        name="middle",
-    )(*exchange(*upward), col_basis)
-    second, sums = pl.pallas_call(
-        products_kernel,
-        in_specs=[SMEM] + [VMEM] * 10,
-        out_specs=(VMEM,) * 2,
-        out_shape=(shape((flat, width), F32), shape((devices, 1, 8 * nrhs), F32)),
-        scratch_shapes=[stack],
-        name="products",
-    )(*exchange(*upward), vector, image)
-    sums = lax.all_to_all(sums, ROWS_GRP, 0, 0, tiled=True)
-    return pl.pallas_call(
+    basis, remainder, hessenberg = call(
         finish_kernel,
-        in_specs=[VMEM] * 4,
-        out_specs=(VMEM,) * 3,
-        out_shape=(
-            shape(vector.shape, F32),
-            shape(vector.shape, F32),
-            shape((nrhs, 5), F32),
-        ),
-        name="finish",
-    )(sums, vector, image, second)
+        [sums, vector, image, second],
+        [shape(vector.shape, F32), shape(vector.shape, F32), shape((5, nrhs), F32)],
+    )
+    return basis, remainder, hessenberg.T
 
 
 def solution(mesh):

time: 138 us -> 117 us (0.85)
  starting transfers between devices: 55.2 us -> 42.3 us
  local copies, waits for them, and re-layouts: 7.55 us -> 0 us
  Pallas kernels: 23.3 us -> 19.2 us
  waiting for transfers between devices: 0.03 us -> 2.93 us
    ppermute x8 -> x4, starting transfers between devices: 22.5 us -> 12.9 us  [the longest x2 10.3 us: exchange(): low = lax.ppermute(sides, ROWS_GRP, step)]
    unnamed x24 -> x0, local copies, waits for them, and re-layouts: 6.19 us -> none
    pallas_call x8 -> x10, Pallas kernels: 23.3 us -> 19.2 us  [call(): pl.pallas_call(kernel, in_specs=specs, out_specs=[VMEM] * len(outs), out_...]
    all_to_all x2, starting transfers between devices: 32.7 us -> 29.3 us  [exchange(): parents = lax.all_to_all(parent, ROWS, 0, 0, tiled=True)]
    ppermute x8 -> x4, waiting for transfers between devices: 0.02 us -> 2.93 us  [the longest x2 1.97 us: exchange(): low = lax.ppermute(sides, ROWS_GRP, step)]
    all_to_all x2, blocking collectives: 17.1 us -> 19.3 us  [exchange(): own = lax.all_to_all(packet, GRP, 0, 0, tiled=True)]
    all_to_all x1, blocking collectives: 33.6 us -> 31.9 us  [shards(): sums = lax.all_to_all(sums, ROWS_GRP, 0, 0, tiled=True)]
  transfers between devices with their start and end apart: 10 -> 6, of which waited for: 0 -> 4; matrix products, arithmetic and copies ran while one was open for 0% -> 0% of each run, Pallas kernels for 9% -> 8%
where the time goes in v2:
time: 117 us; the launch traced here: 116 us
  blocking collectives  51.1 us (44%)
  starting transfers between devices  42.3 us (36%)
  Pallas kernels  19.2 us (16%)
  waiting for transfers between devices  2.93 us (3%)
    all_to_all x1, blocking collectives, shards(): sums = lax.all_to_all(sums, ROWS_GRP, 0, 0, tiled=True)  31.9 us
    all_to_all x2, starting transfers between devices, exchange(): parents = lax.all_to_all(parent, ROWS, 0, 0, tiled=True)  29.3 us
    all_to_all x2, blocking collectives, exchange(): own = lax.all_to_all(packet, GRP, 0, 0, tiled=True)  19.3 us
    pallas_call x10, Pallas kernels, call(): pl.pallas_call(kernel, in_specs=specs, out_specs=[VMEM] * len(outs), out_...  19.2 us
    ppermute x2, starting transfers between devices, exchange(): low = lax.ppermute(sides, ROWS_GRP, step)  10.3 us
    ppermute x2, starting transfers between devices, exchange(): high = lax.ppermute(sides, ROWS_GRP, [(b, a) for a, b in step])  2.58 us
  transfers between devices with their start and end apart: 6, of which 4 were waited for; matrix products, arithmetic and copies ran while one was open for 0% of the time, Pallas kernels for 8%

profile of v2, /device:TPU:1, one launch (start us, length us, event | category | flops | bytes accessed | tf_op | source)
XLA Modules:
  0.0 116.2 jit_solution(4431337648214881236)
XLA Ops:
  0.6 1.5 %start_kernel.1 = bf16[4,224,128]{2,1,0:T(8,128)(2,1)S(1)} custom-call(f32[4,16,384]{2,1,0:T(8,128)} %vector.5, bf16[4,32,384]{2,1,0:T(8,128)(2,1)} %col_basis.3, f32[4,32,32]{2,1,0:T(8,128)} %leaf_transfer.5, f32[1,32,32]{2,1,0:T(8,128)} %box_transfer.5), custom_call_target="tpu_custom_call" | custom-call | tf_op jit(solution)/shard_map/start_kernel/pallas_call | solution.py:357
  2.1 10.3 %all_to_all.25.own = bf16[4,224,128]{2,1,0:T(8,128)(2,1)S(1)} all-to-all(bf16[4,224,128]{2,1,0:T(8,128)(2,1)S(1)} %start_kernel.1), channel_id=1, replica_groups=mesh['rows_0'=4,'rows_1'=4,'rows_2'=4,'grp_0'=2,'grp_1'=2] {'grp_0','grp..., dimensions={0} | all-to-all | bytes 458752 | tf_op jit(solution)/shard_map/all_to_all | solution.py:372
  12.4 0.9 group_kernel.2
  13.3 12.6 %all-to-all-start.1 = ((bf16[64,4,128]{2,1,0:T(4,128)(2,1)}), bf16[64,4,128]{2,1,0:T(4,128)(2,1)S(1)}, u32[]{:S(2)}, u32[]{:S(2)}) async-start(bf16[64,4,128]{2,1,0:T(4,128)(2,1)} %get-tuple-element.18), calls=%async_computation.1 | async-start | bytes 131072 | tf_op jit(solution)/shard_map/all_to_all | solution.py:378
  25.9 1.3 %collective-permute-start.1 = (bf16[320,128]{1,0:T(8,128)(2,1)S(1)}, bf16[320,128]{1,0:T(8,128)(2,1)S(1)}, u32[]{:S(2)}, u32[]{:S(2)}) collective-permute-start(bf16[320,128]{1,0:T(8,128)(2,1)S(1)} %get-tuple-element.19), channel_id=1, source_target_pairs={{5,0},{6,1},{7,2},{4,3},{9,4},{10,5},{11,6},{8,7},{13,8},{14,9},{1... | collective-permute-start | bytes 245768 | tf_op jit(solution)/shard_map/ppermute | solution.py:377
  27.2 5.2 %collective-permute-start = (bf16[320,128]{1,0:T(8,128)(2,1)S(1)}, bf16[320,128]{1,0:T(8,128)(2,1)S(1)}, u32[]{:S(2)}, u32[]{:S(2)}) collective-permute-start(bf16[320,128]{1,0:T(8,128)(2,1)S(1)} %get-tuple-element.19), channel_id=1, source_target_pairs={{0,5},{1,6},{2,7},{3,4},{4,9},{5,10},{6,11},{7,8},{8,13},{9,14},{1... | collective-permute-start | bytes 245768 | tf_op jit(solution)/shard_map/ppermute | solution.py:376
  32.4 0.5 collective-permute-done.1.high
  32.8 1.0 collective-permute-done.low
  33.8 3.6 %near_kernel.2.near = f32[64,384]{1,0:T(8,128)S(1)} custom-call(s32[4,3]{1,0:T(4,128)} %near_cols.3, bf16[320,128]{1,0:T(8,128)(2,1)S(1)} %collective-permute-done.low, bf16[4,224,128]{2,1,0:T(8,128)(2,1)S(1)} %all_to_all.25.own, bf16[320,128]{1,0:T(8,128)(2,1)S(1)} %collective-permute-done.1.high, bf16[4,3,384,384]{3,2,1,0:T(8,128)(2,1)} %blocks.3), custom_call_target="tpu_custom_call" | custom-call | tf_op jit(solution)/shard_map/near_kernel/pallas_call | solution.py:357
  37.4 1.3 %fine_kernel.2 = (f32[64,128]{1,0:T(8,128)S(1)}, f32[16,32]{1,0:T(8,128)S(1)}) custom-call(s32[4,8]{1,0:T(4,128)} %leaf_far.3, s32[1,4]{1,0:T(1,128)} %box_far.3, bf16[320,128]{1,0:T(8,128)(2,1)S(1)} %collective-permute-done.low, bf16[4,224,128]{2,1,0:T(8,128)(2,1)S(1)} %all_to_all.25.own, bf16[320,128]{1,0:T(8,128)(2,1)S(1)} %collective-permute-done.1.high, ...), custom_call_target="tpu_custom_call" | custom-call | tf_op jit(solution)/shard_map/fine_kernel/pallas_call | solution.py:357
  38.7 0.0 all-to-all-done.1.parents
  38.7 2.2 %middle_kernel.1 = (f32[64,384]{1,0:T(8,128)S(1)}, bf16[4,224,128]{2,1,0:T(8,128)(2,1)S(1)}) custom-call(s32[1,4]{1,0:T(1,128)} %coarse_far.3, bf16[64,4,128]{2,1,0:T(4,128)(2,1)S(1)} %all-to-all-done.1.parents, f32[64,384]{1,0:T(8,128)S(1)} %near_kernel.2.near, f32[64,128]{1,0:T(8,128)S(1)} %get-tuple-element.20.leaf_field, ...), custom_call_target="tpu_custom_call" | custom-call | tf_op jit(solution)/shard_map/middle_kernel/pallas_call | solution.py:357
  41.0 8.9 %all_to_all.26.own = bf16[4,224,128]{2,1,0:T(8,128)(2,1)S(1)} all-to-all(bf16[4,224,128]{2,1,0:T(8,128)(2,1)S(1)} %get-tuple-element.22), channel_id=1, replica_groups=mesh['rows_0'=4,'rows_1'=4,'rows_2'=4,'grp_0'=2,'grp_1'=2] {'grp_0','grp..., dimensions={0} | all-to-all | bytes 458752 | tf_op jit(solution)/shard_map/all_to_all | solution.py:372
  49.9 0.9 group_kernel.3
  50.8 16.8 %all-to-all-start.3 = ((bf16[64,4,128]{2,1,0:T(4,128)(2,1)}), bf16[64,4,128]{2,1,0:T(4,128)(2,1)S(1)}, u32[]{:S(2)}, u32[]{:S(2)}) async-start(bf16[64,4,128]{2,1,0:T(4,128)(2,1)} %get-tuple-element.23), calls=%async_computation.3 | async-start | bytes 131072 | tf_op jit(solution)/shard_map/all_to_all | solution.py:378
  67.6 1.3 %collective-permute-start.3 = (bf16[320,128]{1,0:T(8,128)(2,1)S(1)}, bf16[320,128]{1,0:T(8,128)(2,1)S(1)}, u32[]{:S(2)}, u32[]{:S(2)}) collective-permute-start(bf16[320,128]{1,0:T(8,128)(2,1)S(1)} %get-tuple-element.24), channel_id=1, source_target_pairs={{5,0},{6,1},{7,2},{4,3},{9,4},{10,5},{11,6},{8,7},{13,8},{14,9},{1... | collective-permute-start | bytes 245768 | tf_op jit(solution)/shard_map/ppermute | solution.py:377
  68.9 5.2 %collective-permute-start.2 = (bf16[320,128]{1,0:T(8,128)(2,1)S(1)}, bf16[320,128]{1,0:T(8,128)(2,1)S(1)}, u32[]{:S(2)}, u32[]{:S(2)}) collective-permute-start(bf16[320,128]{1,0:T(8,128)(2,1)S(1)} %get-tuple-element.24), channel_id=1, source_target_pairs={{0,5},{1,6},{2,7},{3,4},{4,9},{5,10},{6,11},{7,8},{8,13},{9,14},{1... | collective-permute-start | bytes 245768 | tf_op jit(solution)/shard_map/ppermute | solution.py:376
  74.1 0.5 collective-permute-done.3.high
  74.5 1.0 collective-permute-done.2.low
  75.5 1.3 %fine_kernel.3 = (f32[64,128]{1,0:T(8,128)S(1)}, f32[16,32]{1,0:T(8,128)S(1)}) custom-call(s32[4,8]{1,0:T(4,128)} %leaf_far.3, s32[1,4]{1,0:T(1,128)} %box_far.3, bf16[320,128]{1,0:T(8,128)(2,1)S(1)} %collective-permute-done.2.low, bf16[4,224,128]{2,1,0:T(8,128)(2,1)S(1)} %all_to_all.26.own, bf16[320,128]{1,0:T(8,128)(2,1)S(1)} %collective-permute-done.3.high, ...), custom_call_target="tpu_custom_call" | custom-call | tf_op jit(solution)/shard_map/fine_kernel/pallas_call | solution.py:357
  76.8 3.6 %near_kernel.3.near = f32[64,384]{1,0:T(8,128)S(1)} custom-call(s32[4,3]{1,0:T(4,128)} %near_cols.3, bf16[320,128]{1,0:T(8,128)(2,1)S(1)} %collective-permute-done.2.low, bf16[4,224,128]{2,1,0:T(8,128)(2,1)S(1)} %all_to_all.26.own, bf16[320,128]{1,0:T(8,128)(2,1)S(1)} %collective-permute-done.3.high, bf16[4,3,384,384]{3,2,1,0:T(8,128)(2,1)} %blocks.3), custom_call_target="tpu_custom_call" | custom-call | tf_op jit(solution)/shard_map/near_kernel/pallas_call | solution.py:357
  80.4 0.0 all-to-all-done.3.parents
  80.4 1.9 %products_kernel.1 = (f32[64,384]{1,0:T(8,128)S(1)}, f32[256,1,128]{2,1,0:T(1,128)S(1)}) custom-call(s32[1,4]{1,0:T(1,128)} %coarse_far.3, bf16[64,4,128]{2,1,0:T(4,128)(2,1)S(1)} %all-to-all-done.3.parents, f32[64,384]{1,0:T(8,128)S(1)} %near_kernel.3.near, f32[64,128]{1,0:T(8,128)S(1)} %get-tuple-element.25.leaf_field, ...), custom_call_target="tpu_custom_call" | custom-call | tf_op jit(solution)/shard_map/products_kernel/pallas_call | solution.py:357
  82.4 31.9 %all_to_all.27.sums = f32[256,1,128]{2,1,0:T(1,128)S(1)} all-to-all(f32[256,1,128]{2,1,0:T(1,128)S(1)} %get-tuple-element.28), channel_id=1, replica_groups=mesh['rows_0'=4,'rows_1'=4,'rows_2'=4,'grp_0'=2,'grp_1'=2] {'rows_0','ro..., dimensions={0} | all-to-all | bytes 262144 | tf_op jit(solution)/shard_map/all_to_all | solution.py:420
  114.3 2.0 %finish_kernel.1 = (f32[4,16,384]{2,1,0:T(8,128)}, f32[4,16,384]{2,1,0:T(8,128)}, f32[5,16]{1,0:T(8,128)}) custom-call(f32[256,1,128]{2,1,0:T(1,128)S(1)} %all_to_all.27.sums, f32[4,16,384]{2,1,0:T(8,128)} %vector.5, f32[64,384]{1,0:T(8,128)S(1)} %get-tuple-element.27.image, f32[64,384]{1,0:T(8,128)S(1)} %get-tuple-element.29.second), custom_call_target="tpu_custom_call" | custom-call | tf_op jit(solution)/shard_map/finish_kernel/pallas_call | solution.py:357
Async XLA Ops:
  13.3 25.4 %all-to-all-start.1 = ((bf16[64,4,128]{2,1,0:T(4,128)(2,1)}), bf16[64,4,128]{2,1,0:T(4,128)(2,1)S(1)}, u32[]{:S(2)}, u32[]{:S(2)}) async-start(bf16[64,4,128]{2,1,0:T(4,128)(2,1)} %get-tuple-element.18), calls=%async_computation.1 | async-start | bytes 131072 | tf_op jit(solution)/shard_map/all_to_all | solution.py:378
  25.9 7.0 %collective-permute-start.1 = (bf16[320,128]{1,0:T(8,128)(2,1)S(1)}, bf16[320,128]{1,0:T(8,128)(2,1)S(1)}, u32[]{:S(2)}, u32[]{:S(2)}) collective-permute-start(bf16[320,128]{1,0:T(8,128)(2,1)S(1)} %get-tuple-element.19), channel_id=1, source_target_pairs={{5,0},{6,1},{7,2},{4,3},{9,4},{10,5},{11,6},{8,7},{13,8},{14,9},{1... | collective-permute-start | bytes 245768 | tf_op jit(solution)/shard_map/ppermute | solution.py:377
  27.2 6.6 %collective-permute-start = (bf16[320,128]{1,0:T(8,128)(2,1)S(1)}, bf16[320,128]{1,0:T(8,128)(2,1)S(1)}, u32[]{:S(2)}, u32[]{:S(2)}) collective-permute-start(bf16[320,128]{1,0:T(8,128)(2,1)S(1)} %get-tuple-element.19), channel_id=1, source_target_pairs={{0,5},{1,6},{2,7},{3,4},{4,9},{5,10},{6,11},{7,8},{8,13},{9,14},{1... | collective-permute-start | bytes 245768 | tf_op jit(solution)/shard_map/ppermute | solution.py:376
  50.8 29.6 %all-to-all-start.3 = ((bf16[64,4,128]{2,1,0:T(4,128)(2,1)}), bf16[64,4,128]{2,1,0:T(4,128)(2,1)S(1)}, u32[]{:S(2)}, u32[]{:S(2)}) async-start(bf16[64,4,128]{2,1,0:T(4,128)(2,1)} %get-tuple-element.23), calls=%async_computation.3 | async-start | bytes 131072 | tf_op jit(solution)/shard_map/all_to_all | solution.py:378
  67.6 7.0 %collective-permute-start.3 = (bf16[320,128]{1,0:T(8,128)(2,1)S(1)}, bf16[320,128]{1,0:T(8,128)(2,1)S(1)}, u32[]{:S(2)}, u32[]{:S(2)}) collective-permute-start(bf16[320,128]{1,0:T(8,128)(2,1)S(1)} %get-tuple-element.24), channel_id=1, source_target_pairs={{5,0},{6,1},{7,2},{4,3},{9,4},{10,5},{11,6},{8,7},{13,8},{14,9},{1... | collective-permute-start | bytes 245768 | tf_op jit(solution)/shard_map/ppermute | solution.py:377
  68.9 6.6 %collective-permute-start.2 = (bf16[320,128]{1,0:T(8,128)(2,1)S(1)}, bf16[320,128]{1,0:T(8,128)(2,1)S(1)}, u32[]{:S(2)}, u32[]{:S(2)}) collective-permute-start(bf16[320,128]{1,0:T(8,128)(2,1)S(1)} %get-tuple-element.24), channel_id=1, source_target_pairs={{0,5},{1,6},{2,7},{3,4},{4,9},{5,10},{6,11},{7,8},{8,13},{9,14},{1... | collective-permute-start | bytes 245768 | tf_op jit(solution)/shard_map/ppermute | solution.py:376

commit v3 on v2

--- a/solution.py
+++ b/solution.py
@@ -6,6 +6,7 @@
 from jax.sharding import Mesh
 from jax.sharding import PartitionSpec as P
 
+
 R = 32
 GRP = ("grp_0", "grp_1")
 ROWS = ("rows_0", "rows_1", "rows_2")
@@ -50,13 +51,13 @@
 
 
 def coefficients(field_bf, col_basis, leaf_transfer, box_transfer, packet_ref):
-    leaves = col_basis.shape[0]
-    lanes = leaves * R
+    lanes = col_basis.shape[0]
+    leaves = lanes // R
     nrhs = field_bf.shape[0] // leaves
-    full = dot(field_bf, col_basis.reshape(lanes, -1), NT)
+    full = dot(field_bf, col_basis, NT)
     leaf = over_leaves(jnp.where(diagonal(leaves, nrhs), full, 0.0), leaves).astype(BF)
-    box = dot(leaf, leaf_transfer.reshape(lanes, R).astype(BF)).astype(BF)
-    parent = dot(box, box_transfer.astype(BF)).astype(BF)
+    box = dot(leaf, leaf_transfer).astype(BF)
+    parent = dot(box, box_transfer).astype(BF)
     row, col = row_col((R, lanes))
     both = dot(box, (row == col).astype(BF)) + dot(parent, (row + R == col).astype(BF))
     blocks = []
@@ -71,7 +72,13 @@
 def start_kernel(vector, col_basis, leaf_transfer, box_transfer, packet_ref):
     leaves, nrhs, width = vector.shape
     field = vector[...].reshape(leaves * nrhs, width).astype(BF)
-    coefficients(field, col_basis[...], leaf_transfer[...], box_transfer[0], packet_ref)
+    coefficients(
+        field,
+        col_basis[...].reshape(leaves * R, width),
+        leaf_transfer[...].reshape(leaves * R, R).astype(BF),
+        box_transfer[0].astype(BF),
+        packet_ref,
+    )
 
 
 def group_kernel(own, side_ref, parent_ref):
@@ -90,10 +97,13 @@
     row, col = row_col((8, nrhs))
     dense = dot((row == col % per_row).astype(BF), tiled).astype(BF)[:per_row]
     parent_ref[...] = jnp.broadcast_to(dense[None], parent_ref.shape)
-    position = lax.axis_index(GRP[0]) * lax.axis_size(GRP[1]) + lax.axis_index(GRP[1])
-    side_ref[:fields] = own[position, :fields]
+    side_ref[:fields] = own[position(), :fields]
     for j in range(group):
         side_ref[fields + j * 2 * nrhs : fields + (j + 1) * 2 * nrhs] = own[j, fields:]
+
+
+def position():
+    return lax.axis_index(GRP[0]) * lax.axis_size(GRP[1]) + lax.axis_index(GRP[1])
 
 
 def row_index():
@@ -103,8 +113,8 @@
     return index
 
 
-def near_kernel(near_cols, low, own, high, blocks, out, window, weights, sems):
-    leaves, kn, width, _ = blocks.shape
+def near_kernel(near_cols, own, side, blocks, out, window, weights, sems):
+    leaves, kn, _, _ = blocks.shape
     nrhs = out.shape[0] // leaves
     group = own.shape[0]
     fields = window.shape[1]
@@ -113,10 +123,10 @@
     ]
     for copy in copies:
         copy.start()
-    window[0] = low[:fields]
+    window[0] = side[:fields]
     for j in range(group):
         window[j + 1] = own[j, :fields]
-    window[group + 1] = high[:fields]
+    window[group + 1] = side[:fields]
     base = (row_index() * group - 1) * leaves
     tiles = fields // leaves // nrhs
     for l in range(leaves):
@@ -138,18 +148,21 @@
         out[l * nrhs : (l + 1) * nrhs] = total
 
 
-def fine_kernel(
-    leaf_far, box_far, low, own, high, leaf_coupling, box_coupling, leaf_out, box_out, window
+def fine_sums(
+    leaf_far, box_far, own, side, other, leaf_coupling, box_coupling, leaf_transfer, out, window
 ):
     group, size, lanes = own.shape
-    nrhs = box_out.shape[0]
     leaves, kf = leaf_far.shape
+    nrhs = out.shape[0] // leaves
     fields = size - 2 * nrhs
+    is_low = position() < group // 2
+    side_slot = jnp.where(is_low, 0, 2 * group)
+    other_slot = jnp.where(is_low, 2 * group, 0)
     for j in range(group):
         rows = slice(fields + j * 2 * nrhs, fields + (j + 1) * 2 * nrhs)
-        window[j] = low[rows]
+        window[side_slot + j] = side[rows]
         window[group + j] = own[j, fields:]
-        window[2 * group + j] = high[rows]
+        window[other_slot + j] = other[rows]
     first_box = (row_index() - 1) * group
     first_leaf = first_box * leaves
     _, col = row_col((nrhs, lanes))
@@ -171,24 +184,57 @@
             tiles.append(tile.astype(BF))
         rows.append(jnp.concatenate(tiles, axis=1))
     gathered = jnp.concatenate(rows, axis=0)
-    leaf_out[...] = dot(gathered, leaf_coupling[...].reshape(leaves * R, -1), NT)
+    leaf_field = dot(gathered, leaf_coupling[...].reshape(leaves * R, -1), NT)
     tile = jnp.zeros((nrhs, lanes), F32)
     for k in range(box_far.shape[1]):
         values = window[box_far[0, k] - first_box, nrhs:].astype(F32)
         if k:
             values = pltpu.roll(values, k * R, 1)
         tile = jnp.where(block == k, values, tile)
-    box_out[...] = dot(tile.astype(BF), box_coupling[0], NT)
-
-
-def downward(
-    coarse_far, parents, near, leaf_field, box_field, coarse_coupling, box_transfer,
-    leaf_transfer, row_basis, stack,
+    box_field = dot(tile.astype(BF), box_coupling[0], NT)
+    transfer = leaf_transfer[...].reshape(leaves * R, R)
+    shared = lax.dot_general(
+        box_field, transfer, NT, precision=lax.Precision.HIGHEST, preferred_element_type=F32
+    )
+    out[...] = leaf_field + jnp.concatenate([shared] * leaves, axis=0)
+
+
+def fine_kernel(
+    leaf_far, box_far, own, side, other, leaf_coupling, box_coupling, leaf_transfer, out, window
 ):
-    leaves = row_basis.shape[0]
-    nrhs = near.shape[0] // leaves
+    fine_sums(
+        leaf_far, box_far, own, side, other, leaf_coupling, box_coupling, leaf_transfer, out,
+        window,
+    )
+
+
+def fine_and_stage_kernel(
+    leaf_far, box_far, own, side, other, leaf_coupling, box_coupling, leaf_transfer,
+    coarse_coupling, box_transfer, row_basis, col_basis, vector, out, coarse_out, down_out,
+    row_out, col_out, leaf_out, box_out, vector_out, window,
+):
+    fine_sums(
+        leaf_far, box_far, own, side, other, leaf_coupling, box_coupling, leaf_transfer, out,
+        window,
+    )
+    transfer = leaf_transfer[...].reshape(leaf_out.shape)
+    coarse_out[...] = coarse_coupling[0]
+    down_out[...] = lax.dot_general(
+        transfer, box_transfer[0], NN, precision=lax.Precision.HIGHEST,
+        preferred_element_type=F32,
+    ).astype(BF)
+    row_out[...] = row_basis[...].reshape(row_out.shape)
+    col_out[...] = col_basis[...].reshape(col_out.shape)
+    leaf_out[...] = transfer.astype(BF)
+    box_out[...] = box_transfer[0].astype(BF)
+    vector_out[...] = vector[...]
+
+
+def downward(coarse_far, parents, near, local_field, coarse_coupling, down, row_basis, stack):
     kc = coarse_far.shape[1]
     per_row, lanes = parents.shape[1:]
+    leaves = lanes // R
+    nrhs = near.shape[0] // leaves
     for k in range(kc):
         stack[k * per_row : (k + 1) * per_row] = parents[coarse_far[0, k]].astype(F32)
     dense = stack[...].astype(BF)
@@ -201,37 +247,33 @@
     wide = half + pltpu.roll(half, R, 1)
     wide = jnp.where(row // nrhs == col // R, wide, 0.0)
     gathered = over_leaves(wide, kc).astype(BF)
-    group_field = dot(gathered, coarse_coupling[0], NT)
-    box_local = box_field[...] + dot(group_field.astype(BF), box_transfer[0].astype(BF), NT)
-    transfer = leaf_transfer[...].reshape(leaves * R, R).astype(BF)
-    shared = dot(box_local.astype(BF), transfer, NT)
-    local = leaf_field[...] + jnp.concatenate([shared] * leaves, axis=0)
+    group_field = dot(gathered, coarse_coupling[...], NT)
+    shared = dot(group_field.astype(BF), down[...], NT)
+    local = local_field[...] + jnp.concatenate([shared] * leaves, axis=0)
     local = jnp.where(diagonal(leaves, nrhs), local, 0.0).astype(BF)
-    return near[...] + dot(local, row_basis[...].reshape(leaves * R, -1))
+    return near[...] + dot(local, row_basis[...])
 
 
 def middle_kernel(
-    coarse_far, parents, near, leaf_field, box_field, coarse_coupling, box_transfer,
-    leaf_transfer, row_basis, col_basis, image_ref, packet_ref, stack,
+    coarse_far, parents, near, local_field, coarse_coupling, down, row_basis, col_basis,
+    leaf_transfer, box_transfer, image_ref, packet_ref, stack,
 ):
     image = downward(
-        coarse_far, parents, near, leaf_field, box_field, coarse_coupling, box_transfer,
-        leaf_transfer, row_basis, stack,
+        coarse_far, parents, near, local_field, coarse_coupling, down, row_basis, stack
     )
     image_ref[...] = image
     coefficients(
-        image.astype(BF), col_basis[...], leaf_transfer[...], box_transfer[0], packet_ref
+        image.astype(BF), col_basis[...], leaf_transfer[...], box_transfer[...], packet_ref
     )
 
 
 def products_kernel(
-    coarse_far, parents, near, leaf_field, box_field, coarse_coupling, box_transfer,
-    leaf_transfer, row_basis, vector, image, second_ref, sums_ref, stack,
+    coarse_far, parents, near, local_field, coarse_coupling, down, row_basis, vector, image,
+    second_ref, sums_ref, stack,
 ):
     leaves, nrhs, width = vector.shape
     second = downward(
-        coarse_far, parents, near, leaf_field, box_field, coarse_coupling, box_transfer,
-        leaf_transfer, row_basis, stack,
+        coarse_far, parents, near, local_field, coarse_coupling, down, row_basis, stack
     )
     second_ref[...] = second
     first = vector[...].reshape(leaves * nrhs, width)
@@ -361,24 +403,27 @@
             out_shape=outs,
             scratch_shapes=scratch,
             compiler_params=params,
-            name=kernel.__name__,
         )(*placed(smem), *placed(inputs), *placed(hbm))
 
-    step = [
-        (i, (i // group + 1) * group + (i + 1) % group) for i in range(devices - group)
-    ]
-
-    def exchange(packet):
+    half = group // 2
+    across = []
+    for i in range(rows - 1):
+        for j in range(half):
+            pair = (i * group + group - 1 - j, (i + 1) * group + j)
+            across += [pair, pair[::-1]]
+    inside = [(i, i ^ half) for i in range(devices)]
+
+    def exchange(packet, number):
         own = lax.all_to_all(packet, GRP, 0, 0, tiled=True)
-        sides, parent = call(
+        mine, parent = call(
             group_kernel, [own], [made(side, lanes, dtype=BF), made(rows, dense, lanes, dtype=BF)]
         )
-        low = lax.ppermute(sides, ROWS_GRP, step)
-        high = lax.ppermute(sides, ROWS_GRP, [(b, a) for a, b in step])
+        near_side = lax.ppermute(mine, ROWS_GRP, across)
         parents = lax.all_to_all(parent, ROWS, 0, 0, tiled=True)
+        far_side = lax.ppermute(near_side, ROWS_GRP, inside)
         (near,) = call(
             near_kernel,
-            [low, own, high],
+            [own, near_side],
             [made(flat, width)],
             smem=[near_cols],
             hbm=[near_blocks],
@@ -388,31 +433,42 @@
                 pltpu.SemaphoreType.DMA((leaves,)),
             ],
         )
-        leaf_field, box_field = call(
-            fine_kernel,
-            [low, own, high, leaf_coupling, box_coupling],
-            [made(flat, lanes), made(nrhs, R)],
+        inputs = [own, near_side, far_side, leaf_coupling, box_coupling, leaf_transfer]
+        outs = [made(flat, lanes)]
+        kernel = fine_kernel
+        if number == 0:
+            kernel = fine_and_stage_kernel
+            inputs += [coarse_coupling, box_transfer, row_basis, col_basis, vector]
+            outs += [
+                made(R, lanes, dtype=BF), made(lanes, R, dtype=BF),
+                made(lanes, width, dtype=BF), made(lanes, width, dtype=BF),
+                made(lanes, R, dtype=BF), made(R, R, dtype=BF), made(*vector.shape),
+            ]
+        local_field, *staged = call(
+            kernel,
+            inputs,
+            outs,
             smem=[leaf_far, box_far],
             scratch=[pltpu.VMEM((3 * group, 2 * nrhs, lanes), BF)],
         )
-        return [
-            parents, near, leaf_field, box_field, coarse_coupling, box_transfer, leaf_transfer,
-            row_basis,
-        ]
+        return [parents, near, local_field], staged
 
     packet_out = made(group, size, lanes, dtype=BF)
     stack = pltpu.VMEM((coarse_far.shape[1] * dense, lanes), F32)
     (packet,) = call(start_kernel, [vector, col_basis, leaf_transfer, box_transfer], [packet_out])
+    received, staged = exchange(packet, 0)
+    coarse, down, row_flat, col_flat, leaf_up, box_up, first = staged
     image, packet = call(
         middle_kernel,
-        exchange(packet) + [col_basis],
+        received + [coarse, down, row_flat, col_flat, leaf_up, box_up],
         [made(flat, width), packet_out],
         smem=[coarse_far],
         scratch=[stack],
     )
+    received, _ = exchange(packet, 1)
     second, sums = call(
         products_kernel,
-        exchange(packet) + [vector, image],
+        received + [coarse, down, row_flat, first, image],
         [made(flat, width), made(devices, 1, 8 * nrhs)],
         smem=[coarse_far],
         scratch=[stack],
@@ -421,7 +477,7 @@
     shape = jax.ShapeDtypeStruct
     basis, remainder, hessenberg = call(
         finish_kernel,
-        [sums, vector, image, second],
+        [sums, first, image, second],
         [shape(vector.shape, F32), shape(vector.shape, F32), shape((5, nrhs), F32)],
     )
     return basis, remainder, hessenberg.T

time: 117 us -> 97.5 us (0.83)
  starting transfers between devices: 42.3 us -> 29.7 us
  blocking collectives: 51.1 us -> 41.7 us
  waiting for transfers between devices: 2.93 us -> 7.07 us
  Pallas kernels: 19.2 us -> 17.8 us
    all_to_all x1, blocking collectives: 31.9 us -> 21.8 us  [shards(): sums = lax.all_to_all(sums, ROWS_GRP, 0, 0, tiled=True)]
    ppermute x4, starting transfers between devices: 12.9 us -> 5.95 us  [the longest x2 4.64 us: exchange(): far_side = lax.ppermute(near_side, ROWS_GRP, inside)]
    all_to_all x2, waiting for transfers between devices: 0.01 us -> 6.44 us  [exchange(): parents = lax.all_to_all(parent, ROWS, 0, 0, tiled=True)]
    all_to_all x2, starting transfers between devices: 29.3 us -> 23.8 us  [exchange(): parents = lax.all_to_all(parent, ROWS, 0, 0, tiled=True)]
    ppermute x4, waiting for transfers between devices: 2.93 us -> 0.63 us  [the longest x2 0.62 us: exchange(): far_side = lax.ppermute(near_side, ROWS_GRP, inside)]
    pallas_call x10, Pallas kernels: 19.2 us -> 17.8 us  [call(): pl.pallas_call(kernel, in_specs=specs, out_specs=[VMEM] * len(outs), out_...]
  transfers between devices with their start and end apart: 6 -> 6, of which waited for: 4 -> 4; matrix products, arithmetic and copies ran while one was open for 0% -> 0% of each run, Pallas kernels for 8% -> 11%
where the time goes in v3:
time: 97.5 us; the launch traced here: 97 us
  blocking collectives  41.7 us (43%)
  starting transfers between devices  29.7 us (30%)
  Pallas kernels  17.8 us (18%)
  waiting for transfers between devices  7.07 us (7%)
    all_to_all x2, starting transfers between devices, exchange(): parents = lax.all_to_all(parent, ROWS, 0, 0, tiled=True)  23.8 us
    all_to_all x1, blocking collectives, shards(): sums = lax.all_to_all(sums, ROWS_GRP, 0, 0, tiled=True)  21.8 us
    all_to_all x2, blocking collectives, exchange(): own = lax.all_to_all(packet, GRP, 0, 0, tiled=True)  19.9 us
    pallas_call x10, Pallas kernels, call(): pl.pallas_call(kernel, in_specs=specs, out_specs=[VMEM] * len(outs), out_...  17.8 us
    all_to_all x2, waiting for transfers between devices, exchange(): parents = lax.all_to_all(parent, ROWS, 0, 0, tiled=True)  6.44 us
    ppermute x2, starting transfers between devices, exchange(): far_side = lax.ppermute(near_side, ROWS_GRP, inside)  4.64 us
  transfers between devices with their start and end apart: 6, of which 4 were waited for; matrix products, arithmetic and copies ran while one was open for 0% of the time, Pallas kernels for 11%

profile of v3, /device:TPU:1, one launch (start us, length us, event | category | flops | bytes accessed | tf_op | source)
XLA Modules:
  0.0 97.0 jit_solution(10727143338048598264)
XLA Ops:
  0.6 1.5 %shard_map.148 = bf16[4,224,128]{2,1,0:T(8,128)(2,1)S(1)} custom-call(f32[4,16,384]{2,1,0:T(8,128)} %vector.3, bf16[4,32,384]{2,1,0:T(8,128)(2,1)} %col_basis.3, f32[4,32,32]{2,1,0:T(8,128)} %leaf_transfer.5, f32[1,32,32]{2,1,0:T(8,128)} %box_transfer.3), custom_call_target="tpu_custom_call" | custom-call | tf_op jit(solution)/shard_map/pallas_call | solution.py:399
  2.1 10.3 %all_to_all.25.own = bf16[4,224,128]{2,1,0:T(8,128)(2,1)S(1)} all-to-all(bf16[4,224,128]{2,1,0:T(8,128)(2,1)S(1)} %shard_map.148), channel_id=1, replica_groups=mesh['rows_0'=4,'rows_1'=4,'rows_2'=4,'grp_0'=2,'grp_1'=2] {'grp_0','grp..., dimensions={0} | all-to-all | bytes 458752 | tf_op jit(solution)/shard_map/all_to_all | solution.py:417
  12.4 0.9 shard_map.149
  13.3 0.7 collective-permute-start
  14.0 14.7 %all-to-all-start.1 = ((bf16[64,4,128]{2,1,0:T(4,128)(2,1)}), bf16[64,4,128]{2,1,0:T(4,128)(2,1)S(1)}, u32[]{:S(2)}, u32[]{:S(2)}) async-start(bf16[64,4,128]{2,1,0:T(4,128)(2,1)} %get-tuple-element.22), calls=%async_computation.1 | async-start | bytes 131072 | tf_op jit(solution)/shard_map/all_to_all | solution.py:422
  28.7 0.0 collective-permute-done.side
  28.7 2.2 %collective-permute-start.1 = (bf16[320,128]{1,0:T(8,128)(2,1)S(1)}, bf16[320,128]{1,0:T(8,128)(2,1)S(1)}, u32[]{:S(2)}, u32[]{:S(2)}) collective-permute-start(bf16[320,128]{1,0:T(8,128)(2,1)S(1)} %collective-permute-done.side), channel_id=1, source_target_pairs={{0,2},{1,3},{2,0},{3,1},{4,6},{5,7},{6,4},{7,5},{8,10},{9,11},{10,... | collective-permute-start | bytes 245768 | tf_op jit(solution)/shard_map/ppermute | solution.py:423
  30.9 3.6 %shard_map.150.near = f32[64,384]{1,0:T(8,128)S(1)} custom-call(s32[4,3]{1,0:T(4,128)} %near_cols.3, bf16[4,224,128]{2,1,0:T(8,128)(2,1)S(1)} %all_to_all.25.own, bf16[320,128]{1,0:T(8,128)(2,1)S(1)} %collective-permute-done.side, bf16[4,3,384,384]{3,2,1,0:T(8,128)(2,1)} %blocks.3), custom_call_target="tpu_custom_call" | custom-call | tf_op jit(solution)/shard_map/pallas_call | solution.py:399
  34.5 0.4 collective-permute-done.1.other
  34.9 1.7 %shard_map.151 = (f32[64,128]{1,0:T(8,128)S(1)}, bf16[32,128]{1,0:T(8,128)(2,1)S(1)}, bf16[128,32]{1,0:T(8,128)(2,1)S(1)}, bf16[128,384]{1,0:T(8,128)(2,1)S(1)},...) custom-call(s32[4,8]{1,0:T(4,128)} %leaf_far.3, ...), custom_call_target="tpu_custom_call" | custom-call | tf_op jit(solution)/shard_map/pallas_call | solution.py:399
  36.6 3.2 %all-to-all-done.1.parents = bf16[64,4,128]{2,1,0:T(4,128)(2,1)S(1)} async-done(((bf16[64,4,128]{2,1,0:T(4,128)(2,1)}), bf16[64,4,128]{2,1,0:T(4,128)(2,1)S(1)}, u32[]{:S(2)}, u32[]{:S(2)}) %all-to-all-start.1) | async-done | bytes 65568 | tf_op jit(solution)/shard_map/all_to_all | solution.py:422
  39.7 1.8 %shard_map.152 = (f32[64,384]{1,0:T(8,128)S(1)}, bf16[4,224,128]{2,1,0:T(8,128)(2,1)S(1)}) custom-call(s32[1,4]{1,0:T(1,128)} %coarse_far.3, bf16[64,4,128]{2,1,0:T(4,128)(2,1)S(1)} %all-to-all-done.1.parents, f32[64,384]{1,0:T(8,128)S(1)} %shard_map.150.near, f32[64,128]{1,0:T(8,128)S(1)} %get-tuple-element.24.local_field, ...), custom_call_target="tpu_custom_call" | custom-call | tf_op jit(solution)/shard_map/pallas_call | solution.py:399
  41.5 9.5 %all_to_all.26.own = bf16[4,224,128]{2,1,0:T(8,128)(2,1)S(1)} all-to-all(bf16[4,224,128]{2,1,0:T(8,128)(2,1)S(1)} %get-tuple-element.31), channel_id=1, replica_groups=mesh['rows_0'=4,'rows_1'=4,'rows_2'=4,'grp_0'=2,'grp_1'=2] {'grp_0','grp..., dimensions={0} | all-to-all | bytes 458752 | tf_op jit(solution)/shard_map/all_to_all | solution.py:417
  51.0 0.9 shard_map.153
  51.9 0.7 collective-permute-start.2
  52.6 9.0 %all-to-all-start.3 = ((bf16[64,4,128]{2,1,0:T(4,128)(2,1)}), bf16[64,4,128]{2,1,0:T(4,128)(2,1)S(1)}, u32[]{:S(2)}, u32[]{:S(2)}) async-start(bf16[64,4,128]{2,1,0:T(4,128)(2,1)} %get-tuple-element.32), calls=%async_computation.3 | async-start | bytes 131072 | tf_op jit(solution)/shard_map/all_to_all | solution.py:422
  61.6 0.0 collective-permute-done.2.side
  61.6 2.5 %collective-permute-start.3 = (bf16[320,128]{1,0:T(8,128)(2,1)S(1)}, bf16[320,128]{1,0:T(8,128)(2,1)S(1)}, u32[]{:S(2)}, u32[]{:S(2)}) collective-permute-start(bf16[320,128]{1,0:T(8,128)(2,1)S(1)} %collective-permute-done.2.side), channel_id=1, source_target_pairs={{0,2},{1,3},{2,0},{3,1},{4,6},{5,7},{6,4},{7,5},{8,10},{9,11},{10,... | collective-permute-start | bytes 245768 | tf_op jit(solution)/shard_map/ppermute | solution.py:423
  64.1 3.6 %shard_map.154.near = f32[64,384]{1,0:T(8,128)S(1)} custom-call(s32[4,3]{1,0:T(4,128)} %near_cols.3, bf16[4,224,128]{2,1,0:T(8,128)(2,1)S(1)} %all_to_all.26.own, bf16[320,128]{1,0:T(8,128)(2,1)S(1)} %collective-permute-done.2.side, bf16[4,3,384,384]{3,2,1,0:T(8,128)(2,1)} %blocks.3), custom_call_target="tpu_custom_call" | custom-call | tf_op jit(solution)/shard_map/pallas_call | solution.py:399
  67.7 0.2 collective-permute-done.3.other
  67.9 1.4 %shard_map.155.local_field = f32[64,128]{1,0:T(8,128)S(1)} custom-call(s32[4,8]{1,0:T(4,128)} %leaf_far.3, s32[1,4]{1,0:T(1,128)} %box_far.3, bf16[4,224,128]{2,1,0:T(8,128)(2,1)S(1)} %all_to_all.26.own, bf16[320,128]{1,0:T(8,128)(2,1)S(1)} %collective-permute-done.2.side, bf16[320,128]{1,0:T(8,128)(2,1)S(1)} %collective-permute-done.3.other, ...), custom_call_target="tpu_custom_call" | custom-call | tf_op jit(solution)/shard_map/pallas_call | solution.py:399
  69.3 3.3 %all-to-all-done.3.parents = bf16[64,4,128]{2,1,0:T(4,128)(2,1)S(1)} async-done(((bf16[64,4,128]{2,1,0:T(4,128)(2,1)}), bf16[64,4,128]{2,1,0:T(4,128)(2,1)S(1)}, u32[]{:S(2)}, u32[]{:S(2)}) %all-to-all-start.3) | async-done | bytes 65568 | tf_op jit(solution)/shard_map/all_to_all | solution.py:422
  72.6 1.5 %shard_map.156 = (f32[64,384]{1,0:T(8,128)S(1)}, f32[256,1,128]{2,1,0:T(1,128)S(1)}) custom-call(s32[1,4]{1,0:T(1,128)} %coarse_far.3, bf16[64,4,128]{2,1,0:T(4,128)(2,1)S(1)} %all-to-all-done.3.parents, f32[64,384]{1,0:T(8,128)S(1)} %shard_map.154.near, f32[64,128]{1,0:T(8,128)S(1)} %shard_map.155.local_field, ...), custom_call_target="tpu_custom_call" | custom-call | tf_op jit(solution)/shard_map/pallas_call | solution.py:399
  74.1 21.8 %all_to_all.27.sums = f32[256,1,128]{2,1,0:T(1,128)S(1)} all-to-all(f32[256,1,128]{2,1,0:T(1,128)S(1)} %get-tuple-element.36), channel_id=1, replica_groups=mesh['rows_0'=4,'rows_1'=4,'rows_2'=4,'grp_0'=2,'grp_1'=2] {'rows_0','ro..., dimensions={0} | all-to-all | bytes 262144 | tf_op jit(solution)/shard_map/all_to_all | solution.py:476
  95.9 1.1 %shard_map.157 = (f32[4,16,384]{2,1,0:T(8,128)}, f32[4,16,384]{2,1,0:T(8,128)}, f32[5,16]{1,0:T(8,128)}) custom-call(f32[256,1,128]{2,1,0:T(1,128)S(1)} %all_to_all.27.sums, f32[4,16,384]{2,1,0:T(8,128)S(1)} %get-tuple-element.34.vector, f32[64,384]{1,0:T(8,128)S(1)} %get-tuple-element.35.image, f32[64,384]{1,0:T(8,128)S(1)} %get-tuple-element.37.second), custom_call_target="tpu_custom_call" | custom-call | tf_op jit(solution)/shard_map/pallas_call | solution.py:399
Async XLA Ops:
  13.3 15.4 %collective-permute-start = (bf16[320,128]{1,0:T(8,128)(2,1)S(1)}, bf16[320,128]{1,0:T(8,128)(2,1)S(1)}, u32[]{:S(2)}, u32[]{:S(2)}) collective-permute-start(bf16[320,128]{1,0:T(8,128)(2,1)S(1)} %get-tuple-element.23), channel_id=1, source_target_pairs={{3,4},{4,3},{2,5},{5,2},{7,8},{8,7},{6,9},{9,6},{11,12},{12,11},{1... | collective-permute-start | bytes 245768 | tf_op jit(solution)/shard_map/ppermute | solution.py:421
  14.0 25.8 %all-to-all-start.1 = ((bf16[64,4,128]{2,1,0:T(4,128)(2,1)}), bf16[64,4,128]{2,1,0:T(4,128)(2,1)S(1)}, u32[]{:S(2)}, u32[]{:S(2)}) async-start(bf16[64,4,128]{2,1,0:T(4,128)(2,1)} %get-tuple-element.22), calls=%async_computation.1 | async-start | bytes 131072 | tf_op jit(solution)/shard_map/all_to_all | solution.py:422
  28.7 6.1 %collective-permute-start.1 = (bf16[320,128]{1,0:T(8,128)(2,1)S(1)}, bf16[320,128]{1,0:T(8,128)(2,1)S(1)}, u32[]{:S(2)}, u32[]{:S(2)}) collective-permute-start(bf16[320,128]{1,0:T(8,128)(2,1)S(1)} %collective-permute-done.side), channel_id=1, source_target_pairs={{0,2},{1,3},{2,0},{3,1},{4,6},{5,7},{6,4},{7,5},{8,10},{9,11},{10,... | collective-permute-start | bytes 245768 | tf_op jit(solution)/shard_map/ppermute | solution.py:423
  51.9 9.7 %collective-permute-start.2 = (bf16[320,128]{1,0:T(8,128)(2,1)S(1)}, bf16[320,128]{1,0:T(8,128)(2,1)S(1)}, u32[]{:S(2)}, u32[]{:S(2)}) collective-permute-start(bf16[320,128]{1,0:T(8,128)(2,1)S(1)} %get-tuple-element.33), channel_id=1, source_target_pairs={{3,4},{4,3},{2,5},{5,2},{7,8},{8,7},{6,9},{9,6},{11,12},{12,11},{1... | collective-permute-start | bytes 245768 | tf_op jit(solution)/shard_map/ppermute | solution.py:421
  52.6 20.0 %all-to-all-start.3 = ((bf16[64,4,128]{2,1,0:T(4,128)(2,1)}), bf16[64,4,128]{2,1,0:T(4,128)(2,1)S(1)}, u32[]{:S(2)}, u32[]{:S(2)}) async-start(bf16[64,4,128]{2,1,0:T(4,128)(2,1)} %get-tuple-element.32), calls=%async_computation.3 | async-start | bytes 131072 | tf_op jit(solution)/shard_map/all_to_all | solution.py:422
  61.6 6.3 %collective-permute-start.3 = (bf16[320,128]{1,0:T(8,128)(2,1)S(1)}, bf16[320,128]{1,0:T(8,128)(2,1)S(1)}, u32[]{:S(2)}, u32[]{:S(2)}) collective-permute-start(bf16[320,128]{1,0:T(8,128)(2,1)S(1)} %collective-permute-done.2.side), channel_id=1, source_target_pairs={{0,2},{1,3},{2,0},{3,1},{4,6},{5,7},{6,4},{7,5},{8,10},{9,11},{10,... | collective-permute-start | bytes 245768 | tf_op jit(solution)/shard_map/ppermute | solution.py:423

commit v4 on v3

--- a/solution.py
+++ b/solution.py
@@ -50,7 +50,7 @@
     return total
 
 
-def coefficients(field_bf, col_basis, leaf_transfer, box_transfer, packet_ref):
+def coefficients(field_bf, col_basis, leaf_transfer, box_transfer, packet_ref, coef_ref):
     lanes = col_basis.shape[0]
     leaves = lanes // R
     nrhs = field_bf.shape[0] // leaves
@@ -64,12 +64,12 @@
     for l in range(leaves):
         for t in range(field_bf.shape[1] // lanes):
             blocks.append(field_bf[l * nrhs : (l + 1) * nrhs, t * lanes : (t + 1) * lanes])
-    blocks += [leaf, both.astype(BF)]
-    packet = jnp.concatenate(blocks, axis=0)
-    packet_ref[...] = jnp.broadcast_to(packet[None], packet_ref.shape)
-
-
-def start_kernel(vector, col_basis, leaf_transfer, box_transfer, packet_ref):
+    coef = [leaf, both.astype(BF)]
+    packet_ref[...] = jnp.concatenate(blocks + coef, axis=0)
+    coef_ref[...] = jnp.concatenate(coef, axis=0)
+
+
+def start_kernel(vector, col_basis, leaf_transfer, box_transfer, packet_ref, coef_ref):
     leaves, nrhs, width = vector.shape
     field = vector[...].reshape(leaves * nrhs, width).astype(BF)
     coefficients(
@@ -78,16 +78,22 @@
         leaf_transfer[...].reshape(leaves * R, R).astype(BF),
         box_transfer[0].astype(BF),
         packet_ref,
-    )
-
-
-def group_kernel(own, side_ref, parent_ref):
-    group, size, lanes = own.shape
-    nrhs = 16
+        coef_ref,
+    )
+
+
+def group_kernel(own, chip, cross, coef, side_ref, parent_ref):
+    size, lanes = own.shape
+    nrhs = coef.shape[0] // 2
     fields = size - 2 * nrhs
-    total = own[0, fields + nrhs :].astype(F32)
-    for j in range(1, group):
-        total = total + own[j, fields + nrhs :].astype(F32)
+    place = position()
+    side_ref[:fields] = own[:fields]
+    total = None
+    for other, part in ((0, own[fields:]), (1, chip[fields:]), (3, cross[fields:]), (2, coef[...])):
+        first = pl.multiple_of(fields + (place ^ other) * (2 * nrhs), 2 * nrhs)
+        side_ref[pl.ds(first, 2 * nrhs)] = part
+        parent = part[nrhs:].astype(F32)
+        total = parent if total is None else total + parent
     total = total.astype(BF)
     row, col = row_col((lanes, lanes))
     tiled = dot(total, ((row // R == 1) & (row % R == col % R)).astype(BF))
@@ -97,9 +103,6 @@
     row, col = row_col((8, nrhs))
     dense = dot((row == col % per_row).astype(BF), tiled).astype(BF)[:per_row]
     parent_ref[...] = jnp.broadcast_to(dense[None], parent_ref.shape)
-    side_ref[:fields] = own[position(), :fields]
-    for j in range(group):
-        side_ref[fields + j * 2 * nrhs : fields + (j + 1) * 2 * nrhs] = own[j, fields:]
 
 
 def position():
@@ -113,10 +116,10 @@
     return index
 
 
-def near_kernel(near_cols, own, side, blocks, out, window, weights, sems):
+def near_kernel(near_cols, own, chip, cross, side, blocks, out, window, weights, sems):
     leaves, kn, _, _ = blocks.shape
     nrhs = out.shape[0] // leaves
-    group = own.shape[0]
+    group = window.shape[0] - 2
     fields = window.shape[1]
     copies = [
         pltpu.make_async_copy(blocks.at[l], weights.at[l], sems.at[l]) for l in range(leaves)
@@ -124,9 +127,11 @@
     for copy in copies:
         copy.start()
     window[0] = side[:fields]
-    for j in range(group):
-        window[j + 1] = own[j, :fields]
     window[group + 1] = side[:fields]
+    place = position()
+    window[place + 1] = own[:fields]
+    window[(place ^ 1) + 1] = chip[:fields]
+    window[(place ^ 3) + 1] = cross[:fields]
     base = (row_index() * group - 1) * leaves
     tiles = fields // leaves // nrhs
     for l in range(leaves):
@@ -151,17 +156,18 @@
 def fine_sums(
     leaf_far, box_far, own, side, other, leaf_coupling, box_coupling, leaf_transfer, out, window
 ):
-    group, size, lanes = own.shape
+    size, lanes = own.shape
     leaves, kf = leaf_far.shape
     nrhs = out.shape[0] // leaves
-    fields = size - 2 * nrhs
+    group = window.shape[0] // 3
+    fields = size - 2 * group * nrhs
     is_low = position() < group // 2
     side_slot = jnp.where(is_low, 0, 2 * group)
     other_slot = jnp.where(is_low, 2 * group, 0)
     for j in range(group):
         rows = slice(fields + j * 2 * nrhs, fields + (j + 1) * 2 * nrhs)
         window[side_slot + j] = side[rows]
-        window[group + j] = own[j, fields:]
+        window[group + j] = own[rows]
         window[other_slot + j] = other[rows]
     first_box = (row_index() - 1) * group
     first_leaf = first_box * leaves
@@ -256,14 +262,15 @@
 
 def middle_kernel(
     coarse_far, parents, near, local_field, coarse_coupling, down, row_basis, col_basis,
-    leaf_transfer, box_transfer, image_ref, packet_ref, stack,
+    leaf_transfer, box_transfer, image_ref, packet_ref, coef_ref, stack,
 ):
     image = downward(
         coarse_far, parents, near, local_field, coarse_coupling, down, row_basis, stack
     )
     image_ref[...] = image
     coefficients(
-        image.astype(BF), col_basis[...], leaf_transfer[...], box_transfer[...], packet_ref
+        image.astype(BF), col_basis[...], leaf_transfer[...], box_transfer[...], packet_ref,
+        coef_ref,
     )
 
 
@@ -411,19 +418,25 @@
         for j in range(half):
             pair = (i * group + group - 1 - j, (i + 1) * group + j)
             across += [pair, pair[::-1]]
-    inside = [(i, i ^ half) for i in range(devices)]
-
-    def exchange(packet, number):
-        own = lax.all_to_all(packet, GRP, 0, 0, tiled=True)
+
+    def swap(array, bits):
+        return lax.ppermute(array, ROWS_GRP, [(i, i ^ bits) for i in range(devices)])
+
+    def exchange(packet, coef, number):
+        chip = swap(packet, 1)
+        cross = swap(packet, 3)
+        third = swap(coef, 2)
         mine, parent = call(
-            group_kernel, [own], [made(side, lanes, dtype=BF), made(rows, dense, lanes, dtype=BF)]
+            group_kernel,
+            [packet, chip, cross, third],
+            [made(side, lanes, dtype=BF), made(rows, dense, lanes, dtype=BF)],
         )
         near_side = lax.ppermute(mine, ROWS_GRP, across)
         parents = lax.all_to_all(parent, ROWS, 0, 0, tiled=True)
-        far_side = lax.ppermute(near_side, ROWS_GRP, inside)
+        far_side = swap(near_side, half)
         (near,) = call(
             near_kernel,
-            [own, near_side],
+            [packet, chip, cross, near_side],
             [made(flat, width)],
             smem=[near_cols],
             hbm=[near_blocks],
@@ -433,7 +446,7 @@
                 pltpu.SemaphoreType.DMA((leaves,)),
             ],
         )
-        inputs = [own, near_side, far_side, leaf_coupling, box_coupling, leaf_transfer]
+        inputs = [mine, near_side, far_side, leaf_coupling, box_coupling, leaf_transfer]
         outs = [made(flat, lanes)]
         kernel = fine_kernel
         if number == 0:
@@ -453,19 +466,19 @@
         )
         return [parents, near, local_field], staged
 
-    packet_out = made(group, size, lanes, dtype=BF)
+    upward_out = [made(size, lanes, dtype=BF), made(2 * nrhs, lanes, dtype=BF)]
     stack = pltpu.VMEM((coarse_far.shape[1] * dense, lanes), F32)
-    (packet,) = call(start_kernel, [vector, col_basis, leaf_transfer, box_transfer], [packet_out])
-    received, staged = exchange(packet, 0)
+    upward = call(start_kernel, [vector, col_basis, leaf_transfer, box_transfer], upward_out)
+    received, staged = exchange(*upward, 0)
     coarse, down, row_flat, col_flat, leaf_up, box_up, first = staged
-    image, packet = call(
+    image, *upward = call(
         middle_kernel,
         received + [coarse, down, row_flat, col_flat, leaf_up, box_up],
-        [made(flat, width), packet_out],
+        [made(flat, width), *upward_out],
         smem=[coarse_far],
         scratch=[stack],
     )
-    received, _ = exchange(packet, 1)
+    received, _ = exchange(*upward, 1)
     second, sums = call(
         products_kernel,
         received + [coarse, down, row_flat, first, image],

time: 97.5 us -> 90.8 us (0.931)
  blocking collectives: 41.7 us -> 20.4 us
  starting transfers between devices: 29.7 us -> 38.2 us
  waiting for transfers between devices: 7.07 us -> 13.2 us
    all_to_all x2 -> x0, blocking collectives: 19.9 us -> none  [exchange(): own = lax.all_to_all(packet, GRP, 0, 0, tiled=True)]
    ppermute x2 -> x8, starting transfers between devices: 4.64 us -> 10.8 us  [swap(): lax.ppermute(array, ROWS_GRP, [(i, i ^ bits) for i in range(devices)])]
    ppermute x2 -> x8, waiting for transfers between devices: 0.62 us -> 4.64 us  [swap(): lax.ppermute(array, ROWS_GRP, [(i, i ^ bits) for i in range(devices)])]
    all_to_all x2, starting transfers between devices: 23.8 us -> 26.1 us  [exchange(): parents = lax.all_to_all(parent, ROWS, 0, 0, tiled=True)]
    all_to_all x2, waiting for transfers between devices: 6.44 us -> 8.58 us  [exchange(): parents = lax.all_to_all(parent, ROWS, 0, 0, tiled=True)]
    all_to_all x1, blocking collectives: 21.8 us -> 20.4 us  [shards(): sums = lax.all_to_all(sums, ROWS_GRP, 0, 0, tiled=True)]
  transfers between devices with their start and end apart: 6 -> 12, of which waited for: 4 -> 5; matrix products, arithmetic and copies ran while one was open for 0% -> 0% of each run, Pallas kernels for 11% -> 11%
where the time goes in v4:
time: 90.8 us; the launch traced here: 90.4 us
  starting transfers between devices  38.2 us (42%)
  blocking collectives  20.4 us (22%)
  Pallas kernels  17.8 us (20%)
  waiting for transfers between devices  13.2 us (15%)
    all_to_all x2, starting transfers between devices, exchange(): parents = lax.all_to_all(parent, ROWS, 0, 0, tiled=True)  26.1 us
    all_to_all x1, blocking collectives, shards(): sums = lax.all_to_all(sums, ROWS_GRP, 0, 0, tiled=True)  20.4 us
    pallas_call x10, Pallas kernels, call(): pl.pallas_call(kernel, in_specs=specs, out_specs=[VMEM] * len(outs), out_...  17.8 us
    ppermute x8, starting transfers between devices, swap(): lax.ppermute(array, ROWS_GRP, [(i, i ^ bits) for i in range(devices)])  10.8 us
    all_to_all x2, waiting for transfers between devices, exchange(): parents = lax.all_to_all(parent, ROWS, 0, 0, tiled=True)  8.58 us
    ppermute x8, waiting for transfers between devices, swap(): lax.ppermute(array, ROWS_GRP, [(i, i ^ bits) for i in range(devices)])  4.64 us
  transfers between devices with their start and end apart: 12, of which 5 were waited for; matrix products, arithmetic and copies ran while one was open for 0% of the time, Pallas kernels for 11%

profile of v4, /device:TPU:1, one launch (start us, length us, event | category | flops | bytes accessed | tf_op | source)
XLA Modules:
  0.0 90.4 jit_solution(1641095296093391472)
XLA Ops:
  0.6 1.5 %shard_map.148 = (bf16[224,128]{1,0:T(8,128)(2,1)S(1)}, bf16[32,128]{1,0:T(8,128)(2,1)S(1)}) custom-call(f32[4,16,384]{2,1,0:T(8,128)} %vector.3, bf16[4,32,384]{2,1,0:T(8,128)(2,1)} %col_basis.3, f32[4,32,32]{2,1,0:T(8,128)} %leaf_transfer.5, f32[1,32,32]{2,1,0:T(8,128)} %box_transfer.3), custom_call_target="tpu_custom_call" | custom-call | tf_op jit(solution)/shard_map/pallas_call | solution.py:406
  2.1 3.0 %collective-permute-start.1 = (bf16[224,128]{1,0:T(8,128)(2,1)S(1)}, bf16[224,128]{1,0:T(8,128)(2,1)S(1)}, u32[]{:S(2)}, u32[]{:S(2)}) collective-permute-start(bf16[224,128]{1,0:T(8,128)(2,1)S(1)} %get-tuple-element.25.own), channel_id=1, source_target_pairs={{0,3},{1,2},{2,1},{3,0},{4,7},{5,6},{6,5},{7,4},{8,11},{9,10},{10,... | collective-permute-start | bytes 172040 | tf_op jit(solution)/shard_map/ppermute | solution.py:423
  5.1 0.2 collective-permute-start
  5.3 1.3 %collective-permute-start.2 = (bf16[32,128]{1,0:T(8,128)(2,1)S(1)}, bf16[32,128]{1,0:T(8,128)(2,1)S(1)}, u32[]{:S(2)}, u32[]{:S(2)}) collective-permute-start(bf16[32,128]{1,0:T(8,128)(2,1)S(1)} %get-tuple-element.26), channel_id=1, source_target_pairs={{0,2},{1,3},{2,0},{3,1},{4,6},{5,7},{6,4},{7,5},{8,10},{9,11},{10,... | collective-permute-start | bytes 24584 | tf_op jit(solution)/shard_map/ppermute | solution.py:423
  6.7 1.9 %collective-permute-done.2.coef = bf16[32,128]{1,0:T(8,128)(2,1)S(1)} collective-permute-done((bf16[32,128]{1,0:T(8,128)(2,1)S(1)}, bf16[32,128]{1,0:T(8,128)(2,1)S(1)}, u32[]{:S(2)}, u32[]{:S(2)}) %collective-permute-start.2) | collective-permute-done | bytes 8224 | tf_op jit(solution)/shard_map/ppermute | solution.py:423
  8.5 0.0 collective-permute-done.1.cross
  8.5 0.0 collective-permute-done.chip
  8.5 0.9 shard_map.149
  9.4 0.7 collective-permute-start.3
  10.1 16.0 %all-to-all-start = ((bf16[64,4,128]{2,1,0:T(4,128)(2,1)}), bf16[64,4,128]{2,1,0:T(4,128)(2,1)S(1)}, u32[]{:S(2)}, u32[]{:S(2)}) async-start(bf16[64,4,128]{2,1,0:T(4,128)(2,1)} %get-tuple-element.27), calls=%async_computation | async-start | bytes 131072 | tf_op jit(solution)/shard_map/all_to_all | solution.py:435
  26.1 0.0 collective-permute-done.3.side
  26.1 1.5 %collective-permute-start.4 = (bf16[320,128]{1,0:T(8,128)(2,1)S(1)}, bf16[320,128]{1,0:T(8,128)(2,1)S(1)}, u32[]{:S(2)}, u32[]{:S(2)}) collective-permute-start(bf16[320,128]{1,0:T(8,128)(2,1)S(1)} %collective-permute-done.3.side), channel_id=1, source_target_pairs={{0,2},{1,3},{2,0},{3,1},{4,6},{5,7},{6,4},{7,5},{8,10},{9,11},{10,... | collective-permute-start | bytes 245768 | tf_op jit(solution)/shard_map/ppermute | solution.py:423
  27.7 3.6 %shard_map.150.near = f32[64,384]{1,0:T(8,128)S(1)} custom-call(s32[4,3]{1,0:T(4,128)} %near_cols.3, bf16[224,128]{1,0:T(8,128)(2,1)S(1)} %get-tuple-element.25.own, bf16[224,128]{1,0:T(8,128)(2,1)S(1)} %collective-permute-done.chip, bf16[224,128]{1,0:T(8,128)(2,1)S(1)} %collective-permute-done.1.cross, bf16[320,128]{1,0:T(8,128)(2,1)S(1)} %collective-permute-done.3.side, ...), custom_call_target="tpu_custom_call" | custom-call | tf_op jit(solution)/shard_map/pallas_call | solution.py:406
  31.2 0.4 collective-permute-done.4.other
  31.7 1.7 %shard_map.151 = (f32[64,128]{1,0:T(8,128)S(1)}, bf16[32,128]{1,0:T(8,128)(2,1)S(1)}, bf16[128,32]{1,0:T(8,128)(2,1)S(1)}, bf16[128,384]{1,0:T(8,128)(2,1)S(1)},...) custom-call(s32[4,8]{1,0:T(4,128)} %leaf_far.3, ...), custom_call_target="tpu_custom_call" | custom-call | tf_op jit(solution)/shard_map/pallas_call | solution.py:406
  33.4 4.2 %all-to-all-done.parents = bf16[64,4,128]{2,1,0:T(4,128)(2,1)S(1)} async-done(((bf16[64,4,128]{2,1,0:T(4,128)(2,1)}), bf16[64,4,128]{2,1,0:T(4,128)(2,1)S(1)}, u32[]{:S(2)}, u32[]{:S(2)}) %all-to-all-start) | async-done | bytes 65568 | tf_op jit(solution)/shard_map/all_to_all | solution.py:435
  37.5 1.8 %shard_map.152 = (f32[64,384]{1,0:T(8,128)S(1)}, bf16[224,128]{1,0:T(8,128)(2,1)S(1)}, bf16[32,128]{1,0:T(8,128)(2,1)S(1)}) custom-call(s32[1,4]{1,0:T(1,128)} %coarse_far.3, bf16[64,4,128]{2,1,0:T(4,128)(2,1)S(1)} %all-to-all-done.parents, f32[64,384]{1,0:T(8,128)S(1)} %shard_map.150.near, f32[64,128]{1,0:T(8,128)S(1)} %get-tuple-element.29.local_field, ...), custom_call_target="tpu_custom_call" | custom-call | tf_op jit(solution)/shard_map/pallas_call | solution.py:406
  39.3 2.3 %collective-permute-start.6 = (bf16[224,128]{1,0:T(8,128)(2,1)S(1)}, bf16[224,128]{1,0:T(8,128)(2,1)S(1)}, u32[]{:S(2)}, u32[]{:S(2)}) collective-permute-start(bf16[224,128]{1,0:T(8,128)(2,1)S(1)} %get-tuple-element.36.own), channel_id=1, source_target_pairs={{0,3},{1,2},{2,1},{3,0},{4,7},{5,6},{6,5},{7,4},{8,11},{9,10},{10,... | collective-permute-start | bytes 172040 | tf_op jit(solution)/shard_map/ppermute | solution.py:423
  41.6 0.0 collective-permute-start.5
  41.7 0.2 collective-permute-start.7
  41.8 2.3 %collective-permute-done.7.coef = bf16[32,128]{1,0:T(8,128)(2,1)S(1)} collective-permute-done((bf16[32,128]{1,0:T(8,128)(2,1)S(1)}, bf16[32,128]{1,0:T(8,128)(2,1)S(1)}, u32[]{:S(2)}, u32[]{:S(2)}) %collective-permute-start.7) | collective-permute-done | bytes 8224 | tf_op jit(solution)/shard_map/ppermute | solution.py:423
  44.2 0.0 collective-permute-done.6.cross
  44.2 0.0 collective-permute-done.5.chip
  44.2 0.9 shard_map.153
  45.1 0.7 collective-permute-start.8
  45.7 10.0 %all-to-all-start.1 = ((bf16[64,4,128]{2,1,0:T(4,128)(2,1)}), bf16[64,4,128]{2,1,0:T(4,128)(2,1)S(1)}, u32[]{:S(2)}, u32[]{:S(2)}) async-start(bf16[64,4,128]{2,1,0:T(4,128)(2,1)} %get-tuple-element.38), calls=%async_computation.1 | async-start | bytes 131072 | tf_op jit(solution)/shard_map/all_to_all | solution.py:435
  55.8 0.0 collective-permute-done.8.side
  55.8 2.2 %collective-permute-start.9 = (bf16[320,128]{1,0:T(8,128)(2,1)S(1)}, bf16[320,128]{1,0:T(8,128)(2,1)S(1)}, u32[]{:S(2)}, u32[]{:S(2)}) collective-permute-start(bf16[320,128]{1,0:T(8,128)(2,1)S(1)} %collective-permute-done.8.side), channel_id=1, source_target_pairs={{0,2},{1,3},{2,0},{3,1},{4,6},{5,7},{6,4},{7,5},{8,10},{9,11},{10,... | collective-permute-start | bytes 245768 | tf_op jit(solution)/shard_map/ppermute | solution.py:423
  58.0 3.6 %shard_map.154.near = f32[64,384]{1,0:T(8,128)S(1)} custom-call(s32[4,3]{1,0:T(4,128)} %near_cols.3, bf16[224,128]{1,0:T(8,128)(2,1)S(1)} %get-tuple-element.36.own, bf16[224,128]{1,0:T(8,128)(2,1)S(1)} %collective-permute-done.5.chip, bf16[224,128]{1,0:T(8,128)(2,1)S(1)} %collective-permute-done.6.cross, bf16[320,128]{1,0:T(8,128)(2,1)S(1)} %collective-permute-done.8.side, ...), custom_call_target="tpu_custom_call" | custom-call | tf_op jit(solution)/shard_map/pallas_call | solution.py:406
  61.5 0.0 collective-permute-done.9.other
  61.5 1.4 %shard_map.155.local_field = f32[64,128]{1,0:T(8,128)S(1)} custom-call(s32[4,8]{1,0:T(4,128)} %leaf_far.3, s32[1,4]{1,0:T(1,128)} %box_far.3, bf16[320,128]{1,0:T(8,128)(2,1)S(1)} %get-tuple-element.39.own, bf16[320,128]{1,0:T(8,128)(2,1)S(1)} %collective-permute-done.8.side, bf16[320,128]{1,0:T(8,128)(2,1)S(1)} %collective-permute-done.9.other, ...), custom_call_target="tpu_custom_call" | custom-call | tf_op jit(solution)/shard_map/pallas_call | solution.py:406
  63.0 4.4 %all-to-all-done.1.parents = bf16[64,4,128]{2,1,0:T(4,128)(2,1)S(1)} async-done(((bf16[64,4,128]{2,1,0:T(4,128)(2,1)}), bf16[64,4,128]{2,1,0:T(4,128)(2,1)S(1)}, u32[]{:S(2)}, u32[]{:S(2)}) %all-to-all-start.1) | async-done | bytes 65568 | tf_op jit(solution)/shard_map/all_to_all | solution.py:435
  67.4 1.5 %shard_map.156 = (f32[64,384]{1,0:T(8,128)S(1)}, f32[256,1,128]{2,1,0:T(1,128)S(1)}) custom-call(s32[1,4]{1,0:T(1,128)} %coarse_far.3, bf16[64,4,128]{2,1,0:T(4,128)(2,1)S(1)} %all-to-all-done.1.parents, f32[64,384]{1,0:T(8,128)S(1)} %shard_map.154.near, f32[64,128]{1,0:T(8,128)S(1)} %shard_map.155.local_field, ...), custom_call_target="tpu_custom_call" | custom-call | tf_op jit(solution)/shard_map/pallas_call | solution.py:406
  68.9 20.4 %all_to_all.15.sums = f32[256,1,128]{2,1,0:T(1,128)S(1)} all-to-all(f32[256,1,128]{2,1,0:T(1,128)S(1)} %get-tuple-element.42), channel_id=1, replica_groups=mesh['rows_0'=4,'rows_1'=4,'rows_2'=4,'grp_0'=2,'grp_1'=2] {'rows_0','ro..., dimensions={0} | all-to-all | bytes 262144 | tf_op jit(solution)/shard_map/all_to_all | solution.py:489
  89.3 1.1 %shard_map.157 = (f32[4,16,384]{2,1,0:T(8,128)}, f32[4,16,384]{2,1,0:T(8,128)}, f32[5,16]{1,0:T(8,128)}) custom-call(f32[256,1,128]{2,1,0:T(1,128)S(1)} %all_to_all.15.sums, f32[4,16,384]{2,1,0:T(8,128)S(1)} %get-tuple-element.40.vector, f32[64,384]{1,0:T(8,128)S(1)} %get-tuple-element.41.image, f32[64,384]{1,0:T(8,128)S(1)} %get-tuple-element.43.second), custom_call_target="tpu_custom_call" | custom-call | tf_op jit(solution)/shard_map/pallas_call | solution.py:406
Async XLA Ops:
  2.1 6.4 %collective-permute-start.1 = (bf16[224,128]{1,0:T(8,128)(2,1)S(1)}, bf16[224,128]{1,0:T(8,128)(2,1)S(1)}, u32[]{:S(2)}, u32[]{:S(2)}) collective-permute-start(bf16[224,128]{1,0:T(8,128)(2,1)S(1)} %get-tuple-element.25.own), channel_id=1, source_target_pairs={{0,3},{1,2},{2,1},{3,0},{4,7},{5,6},{6,5},{7,4},{8,11},{9,10},{10,... | collective-permute-start | bytes 172040 | tf_op jit(solution)/shard_map/ppermute | solution.py:423
  5.1 3.4 %collective-permute-start = (bf16[224,128]{1,0:T(8,128)(2,1)S(1)}, bf16[224,128]{1,0:T(8,128)(2,1)S(1)}, u32[]{:S(2)}, u32[]{:S(2)}) collective-permute-start(bf16[224,128]{1,0:T(8,128)(2,1)S(1)} %get-tuple-element.25.own), channel_id=1, source_target_pairs={{0,1},{1,0},{2,3},{3,2},{4,5},{5,4},{6,7},{7,6},{8,9},{9,8},{10,11... | collective-permute-start | bytes 172040 | tf_op jit(solution)/shard_map/ppermute | solution.py:423
  5.3 3.2 %collective-permute-start.2 = (bf16[32,128]{1,0:T(8,128)(2,1)S(1)}, bf16[32,128]{1,0:T(8,128)(2,1)S(1)}, u32[]{:S(2)}, u32[]{:S(2)}) collective-permute-start(bf16[32,128]{1,0:T(8,128)(2,1)S(1)} %get-tuple-element.26), channel_id=1, source_target_pairs={{0,2},{1,3},{2,0},{3,1},{4,6},{5,7},{6,4},{7,5},{8,10},{9,11},{10,... | collective-permute-start | bytes 24584 | tf_op jit(solution)/shard_map/ppermute | solution.py:423
  9.4 16.7 %collective-permute-start.3 = (bf16[320,128]{1,0:T(8,128)(2,1)S(1)}, bf16[320,128]{1,0:T(8,128)(2,1)S(1)}, u32[]{:S(2)}, u32[]{:S(2)}) collective-permute-start(bf16[320,128]{1,0:T(8,128)(2,1)S(1)} %get-tuple-element.28.own), channel_id=1, source_target_pairs={{3,4},{4,3},{2,5},{5,2},{7,8},{8,7},{6,9},{9,6},{11,12},{12,11},{1... | collective-permute-start | bytes 245768 | tf_op jit(solution)/shard_map/ppermute | solution.py:434
  10.1 27.5 %all-to-all-start = ((bf16[64,4,128]{2,1,0:T(4,128)(2,1)}), bf16[64,4,128]{2,1,0:T(4,128)(2,1)S(1)}, u32[]{:S(2)}, u32[]{:S(2)}) async-start(bf16[64,4,128]{2,1,0:T(4,128)(2,1)} %get-tuple-element.27), calls=%async_computation | async-start | bytes 131072 | tf_op jit(solution)/shard_map/all_to_all | solution.py:435
  26.1 5.6 %collective-permute-start.4 = (bf16[320,128]{1,0:T(8,128)(2,1)S(1)}, bf16[320,128]{1,0:T(8,128)(2,1)S(1)}, u32[]{:S(2)}, u32[]{:S(2)}) collective-permute-start(bf16[320,128]{1,0:T(8,128)(2,1)S(1)} %collective-permute-done.3.side), channel_id=1, source_target_pairs={{0,2},{1,3},{2,0},{3,1},{4,6},{5,7},{6,4},{7,5},{8,10},{9,11},{10,... | collective-permute-start | bytes 245768 | tf_op jit(solution)/shard_map/ppermute | solution.py:423
  39.3 4.9 %collective-permute-start.6 = (bf16[224,128]{1,0:T(8,128)(2,1)S(1)}, bf16[224,128]{1,0:T(8,128)(2,1)S(1)}, u32[]{:S(2)}, u32[]{:S(2)}) collective-permute-start(bf16[224,128]{1,0:T(8,128)(2,1)S(1)} %get-tuple-element.36.own), channel_id=1, source_target_pairs={{0,3},{1,2},{2,1},{3,0},{4,7},{5,6},{6,5},{7,4},{8,11},{9,10},{10,... | collective-permute-start | bytes 172040 | tf_op jit(solution)/shard_map/ppermute | solution.py:423
  41.6 2.5 %collective-permute-start.5 = (bf16[224,128]{1,0:T(8,128)(2,1)S(1)}, bf16[224,128]{1,0:T(8,128)(2,1)S(1)}, u32[]{:S(2)}, u32[]{:S(2)}) collective-permute-start(bf16[224,128]{1,0:T(8,128)(2,1)S(1)} %get-tuple-element.36.own), channel_id=1, source_target_pairs={{0,1},{1,0},{2,3},{3,2},{4,5},{5,4},{6,7},{7,6},{8,9},{9,8},{10,11... | collective-permute-start | bytes 172040 | tf_op jit(solution)/shard_map/ppermute | solution.py:423
  41.7 2.5 %collective-permute-start.7 = (bf16[32,128]{1,0:T(8,128)(2,1)S(1)}, bf16[32,128]{1,0:T(8,128)(2,1)S(1)}, u32[]{:S(2)}, u32[]{:S(2)}) collective-permute-start(bf16[32,128]{1,0:T(8,128)(2,1)S(1)} %get-tuple-element.37), channel_id=1, source_target_pairs={{0,2},{1,3},{2,0},{3,1},{4,6},{5,7},{6,4},{7,5},{8,10},{9,11},{10,... | collective-permute-start | bytes 24584 | tf_op jit(solution)/shard_map/ppermute | solution.py:423
  45.1 10.7 %collective-permute-start.8 = (bf16[320,128]{1,0:T(8,128)(2,1)S(1)}, bf16[320,128]{1,0:T(8,128)(2,1)S(1)}, u32[]{:S(2)}, u32[]{:S(2)}) collective-permute-start(bf16[320,128]{1,0:T(8,128)(2,1)S(1)} %get-tuple-element.39.own), channel_id=1, source_target_pairs={{3,4},{4,3},{2,5},{5,2},{7,8},{8,7},{6,9},{9,6},{11,12},{12,11},{1... | collective-permute-start | bytes 245768 | tf_op jit(solution)/shard_map/ppermute | solution.py:434
  45.7 21.7 %all-to-all-start.1 = ((bf16[64,4,128]{2,1,0:T(4,128)(2,1)}), bf16[64,4,128]{2,1,0:T(4,128)(2,1)S(1)}, u32[]{:S(2)}, u32[]{:S(2)}) async-start(bf16[64,4,128]{2,1,0:T(4,128)(2,1)} %get-tuple-element.38), calls=%async_computation.1 | async-start | bytes 131072 | tf_op jit(solution)/shard_map/all_to_all | solution.py:435
  55.8 5.8 %collective-permute-start.9 = (bf16[320,128]{1,0:T(8,128)(2,1)S(1)}, bf16[320,128]{1,0:T(8,128)(2,1)S(1)}, u32[]{:S(2)}, u32[]{:S(2)}) collective-permute-start(bf16[320,128]{1,0:T(8,128)(2,1)S(1)} %collective-permute-done.8.side), channel_id=1, source_target_pairs={{0,2},{1,3},{2,0},{3,1},{4,6},{5,7},{6,4},{7,5},{8,10},{9,11},{10,... | collective-permute-start | bytes 245768 | tf_op jit(solution)/shard_map/ppermute | solution.py:423

commit v5 on v4

--- a/solution.py
+++ b/solution.py
@@ -50,7 +50,7 @@
     return total
 
 
-def coefficients(field_bf, col_basis, leaf_transfer, box_transfer, packet_ref, coef_ref):
+def coefficients(field_bf, col_basis, leaf_transfer, box_transfer, tiles_ref, coef_ref):
     lanes = col_basis.shape[0]
     leaves = lanes // R
     nrhs = field_bf.shape[0] // leaves
@@ -65,11 +65,11 @@
         for t in range(field_bf.shape[1] // lanes):
             blocks.append(field_bf[l * nrhs : (l + 1) * nrhs, t * lanes : (t + 1) * lanes])
     coef = [leaf, both.astype(BF)]
-    packet_ref[...] = jnp.concatenate(blocks + coef, axis=0)
+    tiles_ref[...] = jnp.concatenate(blocks, axis=0)
     coef_ref[...] = jnp.concatenate(coef, axis=0)
 
 
-def start_kernel(vector, col_basis, leaf_transfer, box_transfer, packet_ref, coef_ref):
+def start_kernel(vector, col_basis, leaf_transfer, box_transfer, tiles_ref, coef_ref):
     leaves, nrhs, width = vector.shape
     field = vector[...].reshape(leaves * nrhs, width).astype(BF)
     coefficients(
@@ -77,19 +77,19 @@
         col_basis[...].reshape(leaves * R, width),
         leaf_transfer[...].reshape(leaves * R, R).astype(BF),
         box_transfer[0].astype(BF),
-        packet_ref,
+        tiles_ref,
         coef_ref,
     )
 
 
-def group_kernel(own, chip, cross, coef, side_ref, parent_ref):
-    size, lanes = own.shape
+def group_kernel(tiles, coef, chip, cross, third, side_ref, parent_ref):
+    fields, lanes = tiles.shape
     nrhs = coef.shape[0] // 2
-    fields = size - 2 * nrhs
     place = position()
-    side_ref[:fields] = own[:fields]
+    side_ref[:fields] = tiles[...]
     total = None
-    for other, part in ((0, own[fields:]), (1, chip[fields:]), (3, cross[fields:]), (2, coef[...])):
+    for other, source in ((0, coef), (1, chip), (3, cross), (2, third)):
+        part = source[...]
         first = pl.multiple_of(fields + (place ^ other) * (2 * nrhs), 2 * nrhs)
         side_ref[pl.ds(first, 2 * nrhs)] = part
         parent = part[nrhs:].astype(F32)
@@ -129,9 +129,9 @@
     window[0] = side[:fields]
     window[group + 1] = side[:fields]
     place = position()
-    window[place + 1] = own[:fields]
-    window[(place ^ 1) + 1] = chip[:fields]
-    window[(place ^ 3) + 1] = cross[:fields]
+    window[place + 1] = own[...]
+    window[(place ^ 1) + 1] = chip[...]
+    window[(place ^ 3) + 1] = cross[...]
     base = (row_index() * group - 1) * leaves
     tiles = fields // leaves // nrhs
     for l in range(leaves):
@@ -262,14 +262,14 @@
 
 def middle_kernel(
     coarse_far, parents, near, local_field, coarse_coupling, down, row_basis, col_basis,
-    leaf_transfer, box_transfer, image_ref, packet_ref, coef_ref, stack,
+    leaf_transfer, box_transfer, image_ref, tiles_ref, coef_ref, stack,
 ):
     image = downward(
         coarse_far, parents, near, local_field, coarse_coupling, down, row_basis, stack
     )
     image_ref[...] = image
     coefficients(
-        image.astype(BF), col_basis[...], leaf_transfer[...], box_transfer[...], packet_ref,
+        image.astype(BF), col_basis[...], leaf_transfer[...], box_transfer[...], tiles_ref,
         coef_ref,
     )
 
@@ -382,7 +382,6 @@
     flat = leaves * nrhs
     dense = nrhs * R // lanes
     tiles = width // lanes
-    size = (leaves * tiles + 2) * nrhs
     side = (leaves * tiles + 2 * group) * nrhs
     params = pltpu.CompilerParams(vmem_limit_bytes=LIMIT)
 
@@ -422,21 +421,20 @@
     def swap(array, bits):
         return lax.ppermute(array, ROWS_GRP, [(i, i ^ bits) for i in range(devices)])
 
-    def exchange(packet, coef, number):
-        chip = swap(packet, 1)
-        cross = swap(packet, 3)
-        third = swap(coef, 2)
+    def exchange(field, coef, number):
         mine, parent = call(
             group_kernel,
-            [packet, chip, cross, third],
+            [field, coef, swap(coef, 1), swap(coef, 3), swap(coef, 2)],
             [made(side, lanes, dtype=BF), made(rows, dense, lanes, dtype=BF)],
         )
         near_side = lax.ppermute(mine, ROWS_GRP, across)
         parents = lax.all_to_all(parent, ROWS, 0, 0, tiled=True)
         far_side = swap(near_side, half)
+        chip = swap(field, 1)
+        cross = swap(field, 3)
         (near,) = call(
             near_kernel,
-            [packet, chip, cross, near_side],
+            [field, chip, cross, near_side],
             [made(flat, width)],
             smem=[near_cols],
             hbm=[near_blocks],
@@ -466,7 +464,9 @@
         )
         return [parents, near, local_field], staged
 
-    upward_out = [made(size, lanes, dtype=BF), made(2 * nrhs, lanes, dtype=BF)]
+    upward_out = [
+        made(leaves * tiles * nrhs, lanes, dtype=BF), made(2 * nrhs, lanes, dtype=BF),
+    ]
     stack = pltpu.VMEM((coarse_far.shape[1] * dense, lanes), F32)
     upward = call(start_kernel, [vector, col_basis, leaf_transfer, box_transfer], upward_out)
     received, staged = exchange(*upward, 0)

time: 90.8 us -> 99.2 us (1.093)
  starting transfers between devices: 38.2 us -> 43.3 us
  blocking collectives: 20.4 us -> 24.6 us
  waiting for transfers between devices: 13.2 us -> 12.2 us
    all_to_all x2, waiting for transfers between devices: 8.58 us -> 0.01 us  [exchange(): parents = lax.all_to_all(parent, ROWS, 0, 0, tiled=True)]
    ppermute x8 -> x12, waiting for transfers between devices: 4.64 us -> 12.2 us  [swap(): lax.ppermute(array, ROWS_GRP, [(i, i ^ bits) for i in range(devices)])]
    all_to_all x2, starting transfers between devices: 26.1 us -> 31.1 us  [exchange(): parents = lax.all_to_all(parent, ROWS, 0, 0, tiled=True)]
    all_to_all x1, blocking collectives: 20.4 us -> 24.6 us  [shards(): sums = lax.all_to_all(sums, ROWS_GRP, 0, 0, tiled=True)]
    ppermute x8 -> x12, starting transfers between devices: 10.8 us -> 10.9 us  [swap(): lax.ppermute(array, ROWS_GRP, [(i, i ^ bits) for i in range(devices)])]
  transfers between devices with their start and end apart: 12 -> 16, of which waited for: 5 -> 6; matrix products, arithmetic and copies ran while one was open for 0% -> 0% of each run, Pallas kernels for 11% -> 10%
where the time goes in v5:
time: 99.2 us; the launch traced here: 98.7 us
  starting transfers between devices  43.3 us (44%)
  blocking collectives  24.6 us (25%)
  Pallas kernels  17.9 us (18%)
  waiting for transfers between devices  12.2 us (12%)
    all_to_all x2, starting transfers between devices, exchange(): parents = lax.all_to_all(parent, ROWS, 0, 0, tiled=True)  31.1 us
    all_to_all x1, blocking collectives, shards(): sums = lax.all_to_all(sums, ROWS_GRP, 0, 0, tiled=True)  24.6 us
    pallas_call x10, Pallas kernels, call(): pl.pallas_call(kernel, in_specs=specs, out_specs=[VMEM] * len(outs), out_...  17.9 us
    ppermute x12, waiting for transfers between devices, swap(): lax.ppermute(array, ROWS_GRP, [(i, i ^ bits) for i in range(devices)])  12.2 us
    ppermute x12, starting transfers between devices, swap(): lax.ppermute(array, ROWS_GRP, [(i, i ^ bits) for i in range(devices)])  10.9 us
  transfers between devices with their start and end apart: 16, of which 6 were waited for; matrix products, arithmetic and copies ran while one was open for 0% of the time, Pallas kernels for 10%

profile of v5, /device:TPU:1, one launch (start us, length us, event | category | flops | bytes accessed | tf_op | source)
XLA Modules:
  0.0 98.7 jit_solution(5080817042789352969)
XLA Ops:
  0.6 1.5 %shard_map.148 = (bf16[192,128]{1,0:T(8,128)(2,1)S(1)}, bf16[32,128]{1,0:T(8,128)(2,1)S(1)}) custom-call(f32[4,16,384]{2,1,0:T(8,128)} %vector.3, bf16[4,32,384]{2,1,0:T(8,128)(2,1)} %col_basis.3, f32[4,32,32]{2,1,0:T(8,128)} %leaf_transfer.5, f32[1,32,32]{2,1,0:T(8,128)} %box_transfer.3), custom_call_target="tpu_custom_call" | custom-call | tf_op jit(solution)/shard_map/pallas_call | solution.py:405
  2.1 3.2 %collective-permute-start = (bf16[32,128]{1,0:T(8,128)(2,1)S(1)}, bf16[32,128]{1,0:T(8,128)(2,1)S(1)}, u32[]{:S(2)}, u32[]{:S(2)}) collective-permute-start(bf16[32,128]{1,0:T(8,128)(2,1)S(1)} %get-tuple-element.26.coef), channel_id=1, source_target_pairs={{0,1},{1,0},{2,3},{3,2},{4,5},{5,4},{6,7},{7,6},{8,9},{9,8},{10,11... | collective-permute-start | bytes 24584 | tf_op jit(solution)/shard_map/ppermute | solution.py:422
  5.3 0.0 collective-permute-start.1
  5.3 1.4 %collective-permute-start.2 = (bf16[32,128]{1,0:T(8,128)(2,1)S(1)}, bf16[32,128]{1,0:T(8,128)(2,1)S(1)}, u32[]{:S(2)}, u32[]{:S(2)}) collective-permute-start(bf16[32,128]{1,0:T(8,128)(2,1)S(1)} %get-tuple-element.26.coef), channel_id=1, source_target_pairs={{0,2},{1,3},{2,0},{3,1},{4,6},{5,7},{6,4},{7,5},{8,10},{9,11},{10,... | collective-permute-start | bytes 24584 | tf_op jit(solution)/shard_map/ppermute | solution.py:422
  6.7 0.0 collective-permute-done.chip
  6.7 1.7 %collective-permute-done.1.cross = bf16[32,128]{1,0:T(8,128)(2,1)S(1)} collective-permute-done((bf16[32,128]{1,0:T(8,128)(2,1)S(1)}, bf16[32,128]{1,0:T(8,128)(2,1)S(1)}, u32[]{:S(2)}, u32[]{:S(2)}) %collective-permute-start.1) | collective-permute-done | bytes 8224 | tf_op jit(solution)/shard_map/ppermute | solution.py:422
  8.4 0.0 collective-permute-done.2.third
  8.4 0.9 shard_map.149
  9.3 0.7 collective-permute-start.5
  9.9 16.1 %all-to-all-start = ((bf16[64,4,128]{2,1,0:T(4,128)(2,1)}), bf16[64,4,128]{2,1,0:T(4,128)(2,1)S(1)}, u32[]{:S(2)}, u32[]{:S(2)}) async-start(bf16[64,4,128]{2,1,0:T(4,128)(2,1)} %get-tuple-element.27), calls=%async_computation | async-start | bytes 131072 | tf_op jit(solution)/shard_map/all_to_all | solution.py:431
  26.1 0.0 collective-permute-done.5.side
  26.1 1.5 %collective-permute-start.6 = (bf16[320,128]{1,0:T(8,128)(2,1)S(1)}, bf16[320,128]{1,0:T(8,128)(2,1)S(1)}, u32[]{:S(2)}, u32[]{:S(2)}) collective-permute-start(bf16[320,128]{1,0:T(8,128)(2,1)S(1)} %collective-permute-done.5.side), channel_id=1, source_target_pairs={{0,2},{1,3},{2,0},{3,1},{4,6},{5,7},{6,4},{7,5},{8,10},{9,11},{10,... | collective-permute-start | bytes 245768 | tf_op jit(solution)/shard_map/ppermute | solution.py:422
  27.7 0.0 collective-permute-start.3
  27.7 0.5 collective-permute-start.4
  28.2 0.7 collective-permute-done.3.chip
  28.9 3.6 %collective-permute-done.4.cross = bf16[192,128]{1,0:T(8,128)(2,1)S(1)} collective-permute-done((bf16[192,128]{1,0:T(8,128)(2,1)S(1)}, bf16[192,128]{1,0:T(8,128)(2,1)S(1)}, u32[]{:S(2)}, u32[]{:S(2)}) %collective-permute-start.4) | collective-permute-done | bytes 49184 | tf_op jit(solution)/shard_map/ppermute | solution.py:422
  32.5 3.6 %shard_map.150.near = f32[64,384]{1,0:T(8,128)S(1)} custom-call(s32[4,3]{1,0:T(4,128)} %near_cols.3, bf16[192,128]{1,0:T(8,128)(2,1)S(1)} %get-tuple-element.25.tiles.own, bf16[192,128]{1,0:T(8,128)(2,1)S(1)} %collective-permute-done.3.chip, bf16[192,128]{1,0:T(8,128)(2,1)S(1)} %collective-permute-done.4.cross, ...), custom_call_target="tpu_custom_call" | custom-call | tf_op jit(solution)/shard_map/pallas_call | solution.py:405
  36.1 0.0 collective-permute-done.6.other
  36.1 1.7 %shard_map.151 = (f32[64,128]{1,0:T(8,128)S(1)}, bf16[32,128]{1,0:T(8,128)(2,1)S(1)}, bf16[128,32]{1,0:T(8,128)(2,1)S(1)}, bf16[128,384]{1,0:T(8,128)(2,1)S(1)},...) custom-call(s32[4,8]{1,0:T(4,128)} %leaf_far.3, ...), custom_call_target="tpu_custom_call" | custom-call | tf_op jit(solution)/shard_map/pallas_call | solution.py:405
  37.8 0.0 all-to-all-done.parents
  37.8 1.8 %shard_map.152 = (f32[64,384]{1,0:T(8,128)S(1)}, bf16[192,128]{1,0:T(8,128)(2,1)S(1)}, bf16[32,128]{1,0:T(8,128)(2,1)S(1)}) custom-call(s32[1,4]{1,0:T(1,128)} %coarse_far.3, bf16[64,4,128]{2,1,0:T(4,128)(2,1)S(1)} %all-to-all-done.parents, f32[64,384]{1,0:T(8,128)S(1)} %shard_map.150.near, f32[64,128]{1,0:T(8,128)S(1)} %get-tuple-element.29.local_field, ...), custom_call_target="tpu_custom_call" | custom-call | tf_op jit(solution)/shard_map/pallas_call | solution.py:405
  39.6 0.8 collective-permute-start.7
  40.4 0.5 collective-permute-start.8
  40.9 0.8 collective-permute-start.9
  41.7 0.0 collective-permute-done.7.chip
  41.7 1.8 %collective-permute-done.8.cross = bf16[32,128]{1,0:T(8,128)(2,1)S(1)} collective-permute-done((bf16[32,128]{1,0:T(8,128)(2,1)S(1)}, bf16[32,128]{1,0:T(8,128)(2,1)S(1)}, u32[]{:S(2)}, u32[]{:S(2)}) %collective-permute-start.8) | collective-permute-done | bytes 8224 | tf_op jit(solution)/shard_map/ppermute | solution.py:422
  43.5 0.0 collective-permute-done.9.third
  43.5 0.9 shard_map.153
  44.4 0.7 collective-permute-start.12
  45.0 15.0 %all-to-all-start.1 = ((bf16[64,4,128]{2,1,0:T(4,128)(2,1)}), bf16[64,4,128]{2,1,0:T(4,128)(2,1)S(1)}, u32[]{:S(2)}, u32[]{:S(2)}) async-start(bf16[64,4,128]{2,1,0:T(4,128)(2,1)} %get-tuple-element.38), calls=%async_computation.1 | async-start | bytes 131072 | tf_op jit(solution)/shard_map/all_to_all | solution.py:431
  60.0 0.0 collective-permute-done.12.side
  60.0 1.7 %collective-permute-start.13 = (bf16[320,128]{1,0:T(8,128)(2,1)S(1)}, bf16[320,128]{1,0:T(8,128)(2,1)S(1)}, u32[]{:S(2)}, u32[]{:S(2)}) collective-permute-start(bf16[320,128]{1,0:T(8,128)(2,1)S(1)} %collective-permute-done.12.side), channel_id=1, source_target_pairs={{0,2},{1,3},{2,0},{3,1},{4,6},{5,7},{6,4},{7,5},{8,10},{9,11},{10,... | collective-permute-start | bytes 245768 | tf_op jit(solution)/shard_map/ppermute | solution.py:422
  61.7 0.0 collective-permute-start.10
  61.7 0.5 collective-permute-start.11
  62.2 0.7 collective-permute-done.10.chip
  62.9 3.6 %collective-permute-done.11.cross = bf16[192,128]{1,0:T(8,128)(2,1)S(1)} collective-permute-done((bf16[192,128]{1,0:T(8,128)(2,1)S(1)}, bf16[192,128]{1,0:T(8,128)(2,1)S(1)}, u32[]{:S(2)}, u32[]{:S(2)}) %collective-permute-start.11) | collective-permute-done | bytes 49184 | tf_op jit(solution)/shard_map/ppermute | solution.py:422
  66.5 3.6 %shard_map.154.near = f32[64,384]{1,0:T(8,128)S(1)} custom-call(s32[4,3]{1,0:T(4,128)} %near_cols.3, bf16[192,128]{1,0:T(8,128)(2,1)S(1)} %get-tuple-element.36.tiles.own, bf16[192,128]{1,0:T(8,128)(2,1)S(1)} %collective-permute-done.10.chip, bf16[192,128]{1,0:T(8,128)(2,1)S(1)} %collective-permute-done.11.cross, ...), custom_call_target="tpu_custom_call" | custom-call | tf_op jit(solution)/shard_map/pallas_call | solution.py:405
  70.1 0.0 collective-permute-done.13.other
  70.1 1.4 %shard_map.155.local_field = f32[64,128]{1,0:T(8,128)S(1)} custom-call(s32[4,8]{1,0:T(4,128)} %leaf_far.3, s32[1,4]{1,0:T(1,128)} %box_far.3, bf16[320,128]{1,0:T(8,128)(2,1)S(1)} %get-tuple-element.39.own, bf16[320,128]{1,0:T(8,128)(2,1)S(1)} %collective-permute-done.12.side, bf16[320,128]{1,0:T(8,128)(2,1)S(1)} %collective-permute-done.13.other, ...), custom_call_target="tpu_custom_call" | custom-call | tf_op jit(solution)/shard_map/pallas_call | solution.py:405
  71.5 0.0 all-to-all-done.1.parents
  71.5 1.5 %shard_map.156 = (f32[64,384]{1,0:T(8,128)S(1)}, f32[256,1,128]{2,1,0:T(1,128)S(1)}) custom-call(s32[1,4]{1,0:T(1,128)} %coarse_far.3, bf16[64,4,128]{2,1,0:T(4,128)(2,1)S(1)} %all-to-all-done.1.parents, f32[64,384]{1,0:T(8,128)S(1)} %shard_map.154.near, f32[64,128]{1,0:T(8,128)S(1)} %shard_map.155.local_field, ...), custom_call_target="tpu_custom_call" | custom-call | tf_op jit(solution)/shard_map/pallas_call | solution.py:405
  73.0 24.6 %all_to_all.15.sums = f32[256,1,128]{2,1,0:T(1,128)S(1)} all-to-all(f32[256,1,128]{2,1,0:T(1,128)S(1)} %get-tuple-element.42), channel_id=1, replica_groups=mesh['rows_0'=4,'rows_1'=4,'rows_2'=4,'grp_0'=2,'grp_1'=2] {'rows_0','ro..., dimensions={0} | all-to-all | bytes 262144 | tf_op jit(solution)/shard_map/all_to_all | solution.py:489
  97.6 1.1 %shard_map.157 = (f32[4,16,384]{2,1,0:T(8,128)}, f32[4,16,384]{2,1,0:T(8,128)}, f32[5,16]{1,0:T(8,128)}) custom-call(f32[256,1,128]{2,1,0:T(1,128)S(1)} %all_to_all.15.sums, f32[4,16,384]{2,1,0:T(8,128)S(1)} %get-tuple-element.40.vector, f32[64,384]{1,0:T(8,128)S(1)} %get-tuple-element.41.image, f32[64,384]{1,0:T(8,128)S(1)} %get-tuple-element.43.second), custom_call_target="tpu_custom_call" | custom-call | tf_op jit(solution)/shard_map/pallas_call | solution.py:405
Async XLA Ops:
  2.1 4.6 %collective-permute-start = (bf16[32,128]{1,0:T(8,128)(2,1)S(1)}, bf16[32,128]{1,0:T(8,128)(2,1)S(1)}, u32[]{:S(2)}, u32[]{:S(2)}) collective-permute-start(bf16[32,128]{1,0:T(8,128)(2,1)S(1)} %get-tuple-element.26.coef), channel_id=1, source_target_pairs={{0,1},{1,0},{2,3},{3,2},{4,5},{5,4},{6,7},{7,6},{8,9},{9,8},{10,11... | collective-permute-start | bytes 24584 | tf_op jit(solution)/shard_map/ppermute | solution.py:422
  5.3 3.1 %collective-permute-start.1 = (bf16[32,128]{1,0:T(8,128)(2,1)S(1)}, bf16[32,128]{1,0:T(8,128)(2,1)S(1)}, u32[]{:S(2)}, u32[]{:S(2)}) collective-permute-start(bf16[32,128]{1,0:T(8,128)(2,1)S(1)} %get-tuple-element.26.coef), channel_id=1, source_target_pairs={{0,3},{1,2},{2,1},{3,0},{4,7},{5,6},{6,5},{7,4},{8,11},{9,10},{10,... | collective-permute-start | bytes 24584 | tf_op jit(solution)/shard_map/ppermute | solution.py:422
  5.3 3.1 %collective-permute-start.2 = (bf16[32,128]{1,0:T(8,128)(2,1)S(1)}, bf16[32,128]{1,0:T(8,128)(2,1)S(1)}, u32[]{:S(2)}, u32[]{:S(2)}) collective-permute-start(bf16[32,128]{1,0:T(8,128)(2,1)S(1)} %get-tuple-element.26.coef), channel_id=1, source_target_pairs={{0,2},{1,3},{2,0},{3,1},{4,6},{5,7},{6,4},{7,5},{8,10},{9,11},{10,... | collective-permute-start | bytes 24584 | tf_op jit(solution)/shard_map/ppermute | solution.py:422
  9.3 16.8 %collective-permute-start.5 = (bf16[320,128]{1,0:T(8,128)(2,1)S(1)}, bf16[320,128]{1,0:T(8,128)(2,1)S(1)}, u32[]{:S(2)}, u32[]{:S(2)}) collective-permute-start(bf16[320,128]{1,0:T(8,128)(2,1)S(1)} %get-tuple-element.28.own), channel_id=1, source_target_pairs={{3,4},{4,3},{2,5},{5,2},{7,8},{8,7},{6,9},{9,6},{11,12},{12,11},{1... | collective-permute-start | bytes 245768 | tf_op jit(solution)/shard_map/ppermute | solution.py:430
  9.9 27.9 %all-to-all-start = ((bf16[64,4,128]{2,1,0:T(4,128)(2,1)}), bf16[64,4,128]{2,1,0:T(4,128)(2,1)S(1)}, u32[]{:S(2)}, u32[]{:S(2)}) async-start(bf16[64,4,128]{2,1,0:T(4,128)(2,1)} %get-tuple-element.27), calls=%async_computation | async-start | bytes 131072 | tf_op jit(solution)/shard_map/all_to_all | solution.py:431
  26.1 10.0 %collective-permute-start.6 = (bf16[320,128]{1,0:T(8,128)(2,1)S(1)}, bf16[320,128]{1,0:T(8,128)(2,1)S(1)}, u32[]{:S(2)}, u32[]{:S(2)}) collective-permute-start(bf16[320,128]{1,0:T(8,128)(2,1)S(1)} %collective-permute-done.5.side), channel_id=1, source_target_pairs={{0,2},{1,3},{2,0},{3,1},{4,6},{5,7},{6,4},{7,5},{8,10},{9,11},{10,... | collective-permute-start | bytes 245768 | tf_op jit(solution)/shard_map/ppermute | solution.py:422
  27.7 1.2 %collective-permute-start.3 = (bf16[192,128]{1,0:T(8,128)(2,1)S(1)}, bf16[192,128]{1,0:T(8,128)(2,1)S(1)}, u32[]{:S(2)}, u32[]{:S(2)}) collective-permute-start(bf16[192,128]{1,0:T(8,128)(2,1)S(1)} %get-tuple-element.25.tiles.own), channel_id=1, source_target_pairs={{0,1},{1,0},{2,3},{3,2},{4,5},{5,4},{6,7},{7,6},{8,9},{9,8},{10,11... | collective-permute-start | bytes 147464 | tf_op jit(solution)/shard_map/ppermute | solution.py:422
  27.7 4.9 %collective-permute-start.4 = (bf16[192,128]{1,0:T(8,128)(2,1)S(1)}, bf16[192,128]{1,0:T(8,128)(2,1)S(1)}, u32[]{:S(2)}, u32[]{:S(2)}) collective-permute-start(bf16[192,128]{1,0:T(8,128)(2,1)S(1)} %get-tuple-element.25.tiles.own), channel_id=1, source_target_pairs={{0,3},{1,2},{2,1},{3,0},{4,7},{5,6},{6,5},{7,4},{8,11},{9,10},{10,... | collective-permute-start | bytes 147464 | tf_op jit(solution)/shard_map/ppermute | solution.py:422
  39.6 2.1 %collective-permute-start.7 = (bf16[32,128]{1,0:T(8,128)(2,1)S(1)}, bf16[32,128]{1,0:T(8,128)(2,1)S(1)}, u32[]{:S(2)}, u32[]{:S(2)}) collective-permute-start(bf16[32,128]{1,0:T(8,128)(2,1)S(1)} %get-tuple-element.37.coef), channel_id=1, source_target_pairs={{0,1},{1,0},{2,3},{3,2},{4,5},{5,4},{6,7},{7,6},{8,9},{9,8},{10,11... | collective-permute-start | bytes 24584 | tf_op jit(solution)/shard_map/ppermute | solution.py:422
  40.4 3.1 %collective-permute-start.8 = (bf16[32,128]{1,0:T(8,128)(2,1)S(1)}, bf16[32,128]{1,0:T(8,128)(2,1)S(1)}, u32[]{:S(2)}, u32[]{:S(2)}) collective-permute-start(bf16[32,128]{1,0:T(8,128)(2,1)S(1)} %get-tuple-element.37.coef), channel_id=1, source_target_pairs={{0,3},{1,2},{2,1},{3,0},{4,7},{5,6},{6,5},{7,4},{8,11},{9,10},{10,... | collective-permute-start | bytes 24584 | tf_op jit(solution)/shard_map/ppermute | solution.py:422
  40.9 2.6 %collective-permute-start.9 = (bf16[32,128]{1,0:T(8,128)(2,1)S(1)}, bf16[32,128]{1,0:T(8,128)(2,1)S(1)}, u32[]{:S(2)}, u32[]{:S(2)}) collective-permute-start(bf16[32,128]{1,0:T(8,128)(2,1)S(1)} %get-tuple-element.37.coef), channel_id=1, source_target_pairs={{0,2},{1,3},{2,0},{3,1},{4,6},{5,7},{6,4},{7,5},{8,10},{9,11},{10,... | collective-permute-start | bytes 24584 | tf_op jit(solution)/shard_map/ppermute | solution.py:422
  44.4 15.6 %collective-permute-start.12 = (bf16[320,128]{1,0:T(8,128)(2,1)S(1)}, bf16[320,128]{1,0:T(8,128)(2,1)S(1)}, u32[]{:S(2)}, u32[]{:S(2)}) collective-permute-start(bf16[320,128]{1,0:T(8,128)(2,1)S(1)} %get-tuple-element.39.own), channel_id=1, source_target_pairs={{3,4},{4,3},{2,5},{5,2},{7,8},{8,7},{6,9},{9,6},{11,12},{12,11},{1... | collective-permute-start | bytes 245768 | tf_op jit(solution)/shard_map/ppermute | solution.py:430
  45.0 26.5 %all-to-all-start.1 = ((bf16[64,4,128]{2,1,0:T(4,128)(2,1)}), bf16[64,4,128]{2,1,0:T(4,128)(2,1)S(1)}, u32[]{:S(2)}, u32[]{:S(2)}) async-start(bf16[64,4,128]{2,1,0:T(4,128)(2,1)} %get-tuple-element.38), calls=%async_computation.1 | async-start | bytes 131072 | tf_op jit(solution)/shard_map/all_to_all | solution.py:431
  60.0 10.1 %collective-permute-start.13 = (bf16[320,128]{1,0:T(8,128)(2,1)S(1)}, bf16[320,128]{1,0:T(8,128)(2,1)S(1)}, u32[]{:S(2)}, u32[]{:S(2)}) collective-permute-start(bf16[320,128]{1,0:T(8,128)(2,1)S(1)} %collective-permute-done.12.side), channel_id=1, source_target_pairs={{0,2},{1,3},{2,0},{3,1},{4,6},{5,7},{6,4},{7,5},{8,10},{9,11},{10,... | collective-permute-start | bytes 245768 | tf_op jit(solution)/shard_map/ppermute | solution.py:422
  61.7 1.2 %collective-permute-start.10 = (bf16[192,128]{1,0:T(8,128)(2,1)S(1)}, bf16[192,128]{1,0:T(8,128)(2,1)S(1)}, u32[]{:S(2)}, u32[]{:S(2)}) collective-permute-start(bf16[192,128]{1,0:T(8,128)(2,1)S(1)} %get-tuple-element.36.tiles.own), channel_id=1, source_target_pairs={{0,1},{1,0},{2,3},{3,2},{4,5},{5,4},{6,7},{7,6},{8,9},{9,8},{10,11... | collective-permute-start | bytes 147464 | tf_op jit(solution)/shard_map/ppermute | solution.py:422
  61.7 4.9 %collective-permute-start.11 = (bf16[192,128]{1,0:T(8,128)(2,1)S(1)}, bf16[192,128]{1,0:T(8,128)(2,1)S(1)}, u32[]{:S(2)}, u32[]{:S(2)}) collective-permute-start(bf16[192,128]{1,0:T(8,128)(2,1)S(1)} %get-tuple-element.36.tiles.own), channel_id=1, source_target_pairs={{0,3},{1,2},{2,1},{3,0},{4,7},{5,6},{6,5},{7,4},{8,11},{9,10},{10,... | collective-permute-start | bytes 147464 | tf_op jit(solution)/shard_map/ppermute | solution.py:422

commit v6 on v4

--- a/solution.py
+++ b/solution.py
@@ -50,21 +50,36 @@
     return total
 
 
+def transfers(leaf_transfer, box_transfer):
+    lanes = leaf_transfer.shape[0]
+    row, col = row_col((R, lanes))
+    spread = (row == col % R).astype(BF)
+    tiled = dot(leaf_transfer.astype(BF), spread).astype(BF)
+    wide = dot(box_transfer.astype(BF), spread)
+    wide = jnp.concatenate([wide] * (lanes // R), axis=0)
+    row, col = row_col((lanes, lanes))
+    return tiled, jnp.where(row // R == col // R, wide, 0.0).astype(BF)
+
+
 def coefficients(field_bf, col_basis, leaf_transfer, box_transfer, packet_ref, coef_ref):
     lanes = col_basis.shape[0]
     leaves = lanes // R
     nrhs = field_bf.shape[0] // leaves
     full = dot(field_bf, col_basis, NT)
     leaf = over_leaves(jnp.where(diagonal(leaves, nrhs), full, 0.0), leaves).astype(BF)
-    box = dot(leaf, leaf_transfer).astype(BF)
-    parent = dot(box, box_transfer).astype(BF)
-    row, col = row_col((R, lanes))
-    both = dot(box, (row == col).astype(BF)) + dot(parent, (row + R == col).astype(BF))
+    box = dot(leaf, leaf_transfer)
+    row, col = row_col((nrhs, lanes))
+    per_row = nrhs * R // lanes
+    turned = jnp.where(row // per_row == col // R, box, 0.0).astype(BF)
+    box = jnp.where(col < R, box, 0.0).astype(BF)
+    row, col = row_col((nrhs, nrhs))
+    picked = dot(((row == col % per_row) & (row < per_row)).astype(BF), turned).astype(BF)
+    parent = dot(picked, box_transfer).astype(BF)
     blocks = []
     for l in range(leaves):
         for t in range(field_bf.shape[1] // lanes):
             blocks.append(field_bf[l * nrhs : (l + 1) * nrhs, t * lanes : (t + 1) * lanes])
-    coef = [leaf, both.astype(BF)]
+    coef = [leaf, box, parent]
     packet_ref[...] = jnp.concatenate(blocks + coef, axis=0)
     coef_ref[...] = jnp.concatenate(coef, axis=0)
 
@@ -72,36 +87,26 @@
 def start_kernel(vector, col_basis, leaf_transfer, box_transfer, packet_ref, coef_ref):
     leaves, nrhs, width = vector.shape
     field = vector[...].reshape(leaves * nrhs, width).astype(BF)
+    up, across = transfers(leaf_transfer[...].reshape(leaves * R, R), box_transfer[0])
     coefficients(
-        field,
-        col_basis[...].reshape(leaves * R, width),
-        leaf_transfer[...].reshape(leaves * R, R).astype(BF),
-        box_transfer[0].astype(BF),
-        packet_ref,
-        coef_ref,
+        field, col_basis[...].reshape(leaves * R, width), up, across, packet_ref, coef_ref
     )
 
 
 def group_kernel(own, chip, cross, coef, side_ref, parent_ref):
-    size, lanes = own.shape
-    nrhs = coef.shape[0] // 2
-    fields = size - 2 * nrhs
+    size, _ = own.shape
+    nrhs = coef.shape[0] // 3
+    fields = size - 3 * nrhs
+    per_row = parent_ref.shape[1]
     place = position()
     side_ref[:fields] = own[:fields]
     total = None
     for other, part in ((0, own[fields:]), (1, chip[fields:]), (3, cross[fields:]), (2, coef[...])):
         first = pl.multiple_of(fields + (place ^ other) * (2 * nrhs), 2 * nrhs)
-        side_ref[pl.ds(first, 2 * nrhs)] = part
-        parent = part[nrhs:].astype(F32)
+        side_ref[pl.ds(first, 2 * nrhs)] = part[: 2 * nrhs]
+        parent = part[2 * nrhs :].astype(F32)
         total = parent if total is None else total + parent
-    total = total.astype(BF)
-    row, col = row_col((lanes, lanes))
-    tiled = dot(total, ((row // R == 1) & (row % R == col % R)).astype(BF))
-    per_row = parent_ref.shape[1]
-    row, col = row_col((nrhs, lanes))
-    tiled = jnp.where(row // per_row == col // R, tiled, 0.0).astype(BF)
-    row, col = row_col((8, nrhs))
-    dense = dot((row == col % per_row).astype(BF), tiled).astype(BF)[:per_row]
+    dense = total.astype(BF)[:per_row]
     parent_ref[...] = jnp.broadcast_to(dense[None], parent_ref.shape)
 
 
@@ -223,7 +228,7 @@
         leaf_far, box_far, own, side, other, leaf_coupling, box_coupling, leaf_transfer, out,
         window,
     )
-    transfer = leaf_transfer[...].reshape(leaf_out.shape)
+    transfer = leaf_transfer[...].reshape(down_out.shape)
     coarse_out[...] = coarse_coupling[0]
     down_out[...] = lax.dot_general(
         transfer, box_transfer[0], NN, precision=lax.Precision.HIGHEST,
@@ -231,8 +236,7 @@
     ).astype(BF)
     row_out[...] = row_basis[...].reshape(row_out.shape)
     col_out[...] = col_basis[...].reshape(col_out.shape)
-    leaf_out[...] = transfer.astype(BF)
-    box_out[...] = box_transfer[0].astype(BF)
+    leaf_out[...], box_out[...] = transfers(transfer, box_transfer[0])
     vector_out[...] = vector[...]
 
 
@@ -382,7 +386,7 @@
     flat = leaves * nrhs
     dense = nrhs * R // lanes
     tiles = width // lanes
-    size = (leaves * tiles + 2) * nrhs
+    size = (leaves * tiles + 3) * nrhs
     side = (leaves * tiles + 2 * group) * nrhs
     params = pltpu.CompilerParams(vmem_limit_bytes=LIMIT)
 
@@ -455,7 +459,7 @@
             outs += [
                 made(R, lanes, dtype=BF), made(lanes, R, dtype=BF),
                 made(lanes, width, dtype=BF), made(lanes, width, dtype=BF),
-                made(lanes, R, dtype=BF), made(R, R, dtype=BF), made(*vector.shape),
+                made(lanes, lanes, dtype=BF), made(lanes, lanes, dtype=BF), made(*vector.shape),
             ]
         local_field, *staged = call(
             kernel,
@@ -466,7 +470,7 @@
         )
         return [parents, near, local_field], staged
 
-    upward_out = [made(size, lanes, dtype=BF), made(2 * nrhs, lanes, dtype=BF)]
+    upward_out = [made(size, lanes, dtype=BF), made(3 * nrhs, lanes, dtype=BF)]
     stack = pltpu.VMEM((coarse_far.shape[1] * dense, lanes), F32)
     upward = call(start_kernel, [vector, col_basis, leaf_transfer, box_transfer], upward_out)
     received, staged = exchange(*upward, 0)

time: 90.8 us -> 90.5 us (level)
  no operation moved by 1% of the time
where the time goes in v6:
time: 90.5 us; the launch traced here: 90 us
  starting transfers between devices  38.1 us (42%)
  blocking collectives  20.4 us (23%)
  Pallas kernels  17.4 us (19%)
  waiting for transfers between devices  13.4 us (15%)
    all_to_all x2, starting transfers between devices, exchange(): parents = lax.all_to_all(parent, ROWS, 0, 0, tiled=True)  26.1 us
    all_to_all x1, blocking collectives, shards(): sums = lax.all_to_all(sums, ROWS_GRP, 0, 0, tiled=True)  20.4 us
    pallas_call x10, Pallas kernels, call(): pl.pallas_call(kernel, in_specs=specs, out_specs=[VMEM] * len(outs), out_...  17.4 us
    ppermute x8, starting transfers between devices, swap(): lax.ppermute(array, ROWS_GRP, [(i, i ^ bits) for i in range(devices)])  10.7 us
    all_to_all x2, waiting for transfers between devices, exchange(): parents = lax.all_to_all(parent, ROWS, 0, 0, tiled=True)  8.61 us
    ppermute x8, waiting for transfers between devices, swap(): lax.ppermute(array, ROWS_GRP, [(i, i ^ bits) for i in range(devices)])  4.77 us
  transfers between devices with their start and end apart: 12, of which 5 were waited for; matrix products, arithmetic and copies ran while one was open for 0% of the time, Pallas kernels for 11%

profile of v6, /device:TPU:1, one launch (start us, length us, event | category | flops | bytes accessed | tf_op | source)
XLA Modules:
  0.0 90.0 jit_solution(13051928827688441845)
XLA Ops:
  0.6 1.5 %shard_map.148 = (bf16[240,128]{1,0:T(8,128)(2,1)S(1)}, bf16[48,128]{1,0:T(8,128)(2,1)S(1)}) custom-call(f32[4,16,384]{2,1,0:T(8,128)} %vector.3, bf16[4,32,384]{2,1,0:T(8,128)(2,1)} %col_basis.3, f32[4,32,32]{2,1,0:T(8,128)} %leaf_transfer.5, f32[1,32,32]{2,1,0:T(8,128)} %box_transfer.3), custom_call_target="tpu_custom_call" | custom-call | tf_op jit(solution)/shard_map/pallas_call | solution.py:410
  2.1 3.0 %collective-permute-start.1 = (bf16[240,128]{1,0:T(8,128)(2,1)S(1)}, bf16[240,128]{1,0:T(8,128)(2,1)S(1)}, u32[]{:S(2)}, u32[]{:S(2)}) collective-permute-start(bf16[240,128]{1,0:T(8,128)(2,1)S(1)} %get-tuple-element.25.own), channel_id=1, source_target_pairs={{0,3},{1,2},{2,1},{3,0},{4,7},{5,6},{6,5},{7,4},{8,11},{9,10},{10,... | collective-permute-start | bytes 184328 | tf_op jit(solution)/shard_map/ppermute | solution.py:427
  5.1 0.2 collective-permute-start
  5.3 1.4 %collective-permute-start.2 = (bf16[48,128]{1,0:T(8,128)(2,1)S(1)}, bf16[48,128]{1,0:T(8,128)(2,1)S(1)}, u32[]{:S(2)}, u32[]{:S(2)}) collective-permute-start(bf16[48,128]{1,0:T(8,128)(2,1)S(1)} %get-tuple-element.26), channel_id=1, source_target_pairs={{0,2},{1,3},{2,0},{3,1},{4,6},{5,7},{6,4},{7,5},{8,10},{9,11},{10,... | collective-permute-start | bytes 36872 | tf_op jit(solution)/shard_map/ppermute | solution.py:427
  6.7 1.9 %collective-permute-done.2.coef = bf16[48,128]{1,0:T(8,128)(2,1)S(1)} collective-permute-done((bf16[48,128]{1,0:T(8,128)(2,1)S(1)}, bf16[48,128]{1,0:T(8,128)(2,1)S(1)}, u32[]{:S(2)}, u32[]{:S(2)}) %collective-permute-start.2) | collective-permute-done | bytes 12320 | tf_op jit(solution)/shard_map/ppermute | solution.py:427
  8.6 0.0 collective-permute-done.1.cross
  8.6 0.0 collective-permute-done.chip
  8.6 0.7 shard_map.149
  9.2 0.7 collective-permute-start.3
  9.9 16.0 %all-to-all-start = ((bf16[64,4,128]{2,1,0:T(4,128)(2,1)}), bf16[64,4,128]{2,1,0:T(4,128)(2,1)S(1)}, u32[]{:S(2)}, u32[]{:S(2)}) async-start(bf16[64,4,128]{2,1,0:T(4,128)(2,1)} %get-tuple-element.27), calls=%async_computation | async-start | bytes 131072 | tf_op jit(solution)/shard_map/all_to_all | solution.py:439
  25.9 0.0 collective-permute-done.3.side
  25.9 1.5 %collective-permute-start.4 = (bf16[320,128]{1,0:T(8,128)(2,1)S(1)}, bf16[320,128]{1,0:T(8,128)(2,1)S(1)}, u32[]{:S(2)}, u32[]{:S(2)}) collective-permute-start(bf16[320,128]{1,0:T(8,128)(2,1)S(1)} %collective-permute-done.3.side), channel_id=1, source_target_pairs={{0,2},{1,3},{2,0},{3,1},{4,6},{5,7},{6,4},{7,5},{8,10},{9,11},{10,... | collective-permute-start | bytes 245768 | tf_op jit(solution)/shard_map/ppermute | solution.py:427
  27.5 3.6 %shard_map.150.near = f32[64,384]{1,0:T(8,128)S(1)} custom-call(s32[4,3]{1,0:T(4,128)} %near_cols.3, bf16[240,128]{1,0:T(8,128)(2,1)S(1)} %get-tuple-element.25.own, bf16[240,128]{1,0:T(8,128)(2,1)S(1)} %collective-permute-done.chip, bf16[240,128]{1,0:T(8,128)(2,1)S(1)} %collective-permute-done.1.cross, bf16[320,128]{1,0:T(8,128)(2,1)S(1)} %collective-permute-done.3.side, ...), custom_call_target="tpu_custom_call" | custom-call | tf_op jit(solution)/shard_map/pallas_call | solution.py:410
  31.1 0.4 collective-permute-done.4.other
  31.5 1.7 %shard_map.151 = (f32[64,128]{1,0:T(8,128)S(1)}, bf16[32,128]{1,0:T(8,128)(2,1)S(1)}, bf16[128,32]{1,0:T(8,128)(2,1)S(1)}, bf16[128,384]{1,0:T(8,128)(2,1)S(1)},...) custom-call(s32[4,8]{1,0:T(4,128)} %leaf_far.3, ...), custom_call_target="tpu_custom_call" | custom-call | tf_op jit(solution)/shard_map/pallas_call | solution.py:410
  33.2 4.2 %all-to-all-done.parents = bf16[64,4,128]{2,1,0:T(4,128)(2,1)S(1)} async-done(((bf16[64,4,128]{2,1,0:T(4,128)(2,1)}), bf16[64,4,128]{2,1,0:T(4,128)(2,1)S(1)}, u32[]{:S(2)}, u32[]{:S(2)}) %all-to-all-start) | async-done | bytes 65568 | tf_op jit(solution)/shard_map/all_to_all | solution.py:439
  37.4 1.8 %shard_map.152 = (f32[64,384]{1,0:T(8,128)S(1)}, bf16[240,128]{1,0:T(8,128)(2,1)S(1)}, bf16[48,128]{1,0:T(8,128)(2,1)S(1)}) custom-call(s32[1,4]{1,0:T(1,128)} %coarse_far.3, bf16[64,4,128]{2,1,0:T(4,128)(2,1)S(1)} %all-to-all-done.parents, f32[64,384]{1,0:T(8,128)S(1)} %shard_map.150.near, f32[64,128]{1,0:T(8,128)S(1)} %get-tuple-element.29.local_field, ...), custom_call_target="tpu_custom_call" | custom-call | tf_op jit(solution)/shard_map/pallas_call | solution.py:410
  39.2 2.3 %collective-permute-start.6 = (bf16[240,128]{1,0:T(8,128)(2,1)S(1)}, bf16[240,128]{1,0:T(8,128)(2,1)S(1)}, u32[]{:S(2)}, u32[]{:S(2)}) collective-permute-start(bf16[240,128]{1,0:T(8,128)(2,1)S(1)} %get-tuple-element.36.own), channel_id=1, source_target_pairs={{0,3},{1,2},{2,1},{3,0},{4,7},{5,6},{6,5},{7,4},{8,11},{9,10},{10,... | collective-permute-start | bytes 184328 | tf_op jit(solution)/shard_map/ppermute | solution.py:427
  41.5 0.0 collective-permute-start.5
  41.5 0.1 collective-permute-start.7
  41.6 2.4 %collective-permute-done.7.coef = bf16[48,128]{1,0:T(8,128)(2,1)S(1)} collective-permute-done((bf16[48,128]{1,0:T(8,128)(2,1)S(1)}, bf16[48,128]{1,0:T(8,128)(2,1)S(1)}, u32[]{:S(2)}, u32[]{:S(2)}) %collective-permute-start.7) | collective-permute-done | bytes 12320 | tf_op jit(solution)/shard_map/ppermute | solution.py:427
  44.0 0.0 collective-permute-done.6.cross
  44.0 0.0 collective-permute-done.5.chip
  44.0 0.7 shard_map.153
  44.7 0.7 collective-permute-start.8
  45.4 10.0 %all-to-all-start.1 = ((bf16[64,4,128]{2,1,0:T(4,128)(2,1)}), bf16[64,4,128]{2,1,0:T(4,128)(2,1)S(1)}, u32[]{:S(2)}, u32[]{:S(2)}) async-start(bf16[64,4,128]{2,1,0:T(4,128)(2,1)} %get-tuple-element.38), calls=%async_computation.1 | async-start | bytes 131072 | tf_op jit(solution)/shard_map/all_to_all | solution.py:439
  55.4 0.0 collective-permute-done.8.side
  55.4 2.2 %collective-permute-start.9 = (bf16[320,128]{1,0:T(8,128)(2,1)S(1)}, bf16[320,128]{1,0:T(8,128)(2,1)S(1)}, u32[]{:S(2)}, u32[]{:S(2)}) collective-permute-start(bf16[320,128]{1,0:T(8,128)(2,1)S(1)} %collective-permute-done.8.side), channel_id=1, source_target_pairs={{0,2},{1,3},{2,0},{3,1},{4,6},{5,7},{6,4},{7,5},{8,10},{9,11},{10,... | collective-permute-start | bytes 245768 | tf_op jit(solution)/shard_map/ppermute | solution.py:427
  57.6 3.6 %shard_map.154.near = f32[64,384]{1,0:T(8,128)S(1)} custom-call(s32[4,3]{1,0:T(4,128)} %near_cols.3, bf16[240,128]{1,0:T(8,128)(2,1)S(1)} %get-tuple-element.36.own, bf16[240,128]{1,0:T(8,128)(2,1)S(1)} %collective-permute-done.5.chip, bf16[240,128]{1,0:T(8,128)(2,1)S(1)} %collective-permute-done.6.cross, bf16[320,128]{1,0:T(8,128)(2,1)S(1)} %collective-permute-done.8.side, ...), custom_call_target="tpu_custom_call" | custom-call | tf_op jit(solution)/shard_map/pallas_call | solution.py:410
  61.2 0.0 collective-permute-done.9.other
  61.2 1.4 %shard_map.155.local_field = f32[64,128]{1,0:T(8,128)S(1)} custom-call(s32[4,8]{1,0:T(4,128)} %leaf_far.3, s32[1,4]{1,0:T(1,128)} %box_far.3, bf16[320,128]{1,0:T(8,128)(2,1)S(1)} %get-tuple-element.39.own, bf16[320,128]{1,0:T(8,128)(2,1)S(1)} %collective-permute-done.8.side, bf16[320,128]{1,0:T(8,128)(2,1)S(1)} %collective-permute-done.9.other, ...), custom_call_target="tpu_custom_call" | custom-call | tf_op jit(solution)/shard_map/pallas_call | solution.py:410
  62.6 4.4 %all-to-all-done.1.parents = bf16[64,4,128]{2,1,0:T(4,128)(2,1)S(1)} async-done(((bf16[64,4,128]{2,1,0:T(4,128)(2,1)}), bf16[64,4,128]{2,1,0:T(4,128)(2,1)S(1)}, u32[]{:S(2)}, u32[]{:S(2)}) %all-to-all-start.1) | async-done | bytes 65568 | tf_op jit(solution)/shard_map/all_to_all | solution.py:439
  67.0 1.5 %shard_map.156 = (f32[64,384]{1,0:T(8,128)S(1)}, f32[256,1,128]{2,1,0:T(1,128)S(1)}) custom-call(s32[1,4]{1,0:T(1,128)} %coarse_far.3, bf16[64,4,128]{2,1,0:T(4,128)(2,1)S(1)} %all-to-all-done.1.parents, f32[64,384]{1,0:T(8,128)S(1)} %shard_map.154.near, f32[64,128]{1,0:T(8,128)S(1)} %shard_map.155.local_field, ...), custom_call_target="tpu_custom_call" | custom-call | tf_op jit(solution)/shard_map/pallas_call | solution.py:410
  68.5 20.4 %all_to_all.15.sums = f32[256,1,128]{2,1,0:T(1,128)S(1)} all-to-all(f32[256,1,128]{2,1,0:T(1,128)S(1)} %get-tuple-element.42), channel_id=1, replica_groups=mesh['rows_0'=4,'rows_1'=4,'rows_2'=4,'grp_0'=2,'grp_1'=2] {'rows_0','ro..., dimensions={0} | all-to-all | bytes 262144 | tf_op jit(solution)/shard_map/all_to_all | solution.py:493
  89.0 1.1 %shard_map.157 = (f32[4,16,384]{2,1,0:T(8,128)}, f32[4,16,384]{2,1,0:T(8,128)}, f32[5,16]{1,0:T(8,128)}) custom-call(f32[256,1,128]{2,1,0:T(1,128)S(1)} %all_to_all.15.sums, f32[4,16,384]{2,1,0:T(8,128)S(1)} %get-tuple-element.40.vector, f32[64,384]{1,0:T(8,128)S(1)} %get-tuple-element.41.image, f32[64,384]{1,0:T(8,128)S(1)} %get-tuple-element.43.second), custom_call_target="tpu_custom_call" | custom-call | tf_op jit(solution)/shard_map/pallas_call | solution.py:410
Async XLA Ops:
  2.1 6.5 %collective-permute-start.1 = (bf16[240,128]{1,0:T(8,128)(2,1)S(1)}, bf16[240,128]{1,0:T(8,128)(2,1)S(1)}, u32[]{:S(2)}, u32[]{:S(2)}) collective-permute-start(bf16[240,128]{1,0:T(8,128)(2,1)S(1)} %get-tuple-element.25.own), channel_id=1, source_target_pairs={{0,3},{1,2},{2,1},{3,0},{4,7},{5,6},{6,5},{7,4},{8,11},{9,10},{10,... | collective-permute-start | bytes 184328 | tf_op jit(solution)/shard_map/ppermute | solution.py:427
  5.1 3.4 %collective-permute-start = (bf16[240,128]{1,0:T(8,128)(2,1)S(1)}, bf16[240,128]{1,0:T(8,128)(2,1)S(1)}, u32[]{:S(2)}, u32[]{:S(2)}) collective-permute-start(bf16[240,128]{1,0:T(8,128)(2,1)S(1)} %get-tuple-element.25.own), channel_id=1, source_target_pairs={{0,1},{1,0},{2,3},{3,2},{4,5},{5,4},{6,7},{7,6},{8,9},{9,8},{10,11... | collective-permute-start | bytes 184328 | tf_op jit(solution)/shard_map/ppermute | solution.py:427
  5.3 3.2 %collective-permute-start.2 = (bf16[48,128]{1,0:T(8,128)(2,1)S(1)}, bf16[48,128]{1,0:T(8,128)(2,1)S(1)}, u32[]{:S(2)}, u32[]{:S(2)}) collective-permute-start(bf16[48,128]{1,0:T(8,128)(2,1)S(1)} %get-tuple-element.26), channel_id=1, source_target_pairs={{0,2},{1,3},{2,0},{3,1},{4,6},{5,7},{6,4},{7,5},{8,10},{9,11},{10,... | collective-permute-start | bytes 36872 | tf_op jit(solution)/shard_map/ppermute | solution.py:427
  9.2 16.7 %collective-permute-start.3 = (bf16[320,128]{1,0:T(8,128)(2,1)S(1)}, bf16[320,128]{1,0:T(8,128)(2,1)S(1)}, u32[]{:S(2)}, u32[]{:S(2)}) collective-permute-start(bf16[320,128]{1,0:T(8,128)(2,1)S(1)} %get-tuple-element.28.own), channel_id=1, source_target_pairs={{3,4},{4,3},{2,5},{5,2},{7,8},{8,7},{6,9},{9,6},{11,12},{12,11},{1... | collective-permute-start | bytes 245768 | tf_op jit(solution)/shard_map/ppermute | solution.py:438
  9.9 27.5 %all-to-all-start = ((bf16[64,4,128]{2,1,0:T(4,128)(2,1)}), bf16[64,4,128]{2,1,0:T(4,128)(2,1)S(1)}, u32[]{:S(2)}, u32[]{:S(2)}) async-start(bf16[64,4,128]{2,1,0:T(4,128)(2,1)} %get-tuple-element.27), calls=%async_computation | async-start | bytes 131072 | tf_op jit(solution)/shard_map/all_to_all | solution.py:439
  25.9 5.6 %collective-permute-start.4 = (bf16[320,128]{1,0:T(8,128)(2,1)S(1)}, bf16[320,128]{1,0:T(8,128)(2,1)S(1)}, u32[]{:S(2)}, u32[]{:S(2)}) collective-permute-start(bf16[320,128]{1,0:T(8,128)(2,1)S(1)} %collective-permute-done.3.side), channel_id=1, source_target_pairs={{0,2},{1,3},{2,0},{3,1},{4,6},{5,7},{6,4},{7,5},{8,10},{9,11},{10,... | collective-permute-start | bytes 245768 | tf_op jit(solution)/shard_map/ppermute | solution.py:427
  39.2 4.9 %collective-permute-start.6 = (bf16[240,128]{1,0:T(8,128)(2,1)S(1)}, bf16[240,128]{1,0:T(8,128)(2,1)S(1)}, u32[]{:S(2)}, u32[]{:S(2)}) collective-permute-start(bf16[240,128]{1,0:T(8,128)(2,1)S(1)} %get-tuple-element.36.own), channel_id=1, source_target_pairs={{0,3},{1,2},{2,1},{3,0},{4,7},{5,6},{6,5},{7,4},{8,11},{9,10},{10,... | collective-permute-start | bytes 184328 | tf_op jit(solution)/shard_map/ppermute | solution.py:427
  41.5 2.6 %collective-permute-start.5 = (bf16[240,128]{1,0:T(8,128)(2,1)S(1)}, bf16[240,128]{1,0:T(8,128)(2,1)S(1)}, u32[]{:S(2)}, u32[]{:S(2)}) collective-permute-start(bf16[240,128]{1,0:T(8,128)(2,1)S(1)} %get-tuple-element.36.own), channel_id=1, source_target_pairs={{0,1},{1,0},{2,3},{3,2},{4,5},{5,4},{6,7},{7,6},{8,9},{9,8},{10,11... | collective-permute-start | bytes 184328 | tf_op jit(solution)/shard_map/ppermute | solution.py:427
  41.5 2.5 %collective-permute-start.7 = (bf16[48,128]{1,0:T(8,128)(2,1)S(1)}, bf16[48,128]{1,0:T(8,128)(2,1)S(1)}, u32[]{:S(2)}, u32[]{:S(2)}) collective-permute-start(bf16[48,128]{1,0:T(8,128)(2,1)S(1)} %get-tuple-element.37), channel_id=1, source_target_pairs={{0,2},{1,3},{2,0},{3,1},{4,6},{5,7},{6,4},{7,5},{8,10},{9,11},{10,... | collective-permute-start | bytes 36872 | tf_op jit(solution)/shard_map/ppermute | solution.py:427
  44.7 10.7 %collective-permute-start.8 = (bf16[320,128]{1,0:T(8,128)(2,1)S(1)}, bf16[320,128]{1,0:T(8,128)(2,1)S(1)}, u32[]{:S(2)}, u32[]{:S(2)}) collective-permute-start(bf16[320,128]{1,0:T(8,128)(2,1)S(1)} %get-tuple-element.39.own), channel_id=1, source_target_pairs={{3,4},{4,3},{2,5},{5,2},{7,8},{8,7},{6,9},{9,6},{11,12},{12,11},{1... | collective-permute-start | bytes 245768 | tf_op jit(solution)/shard_map/ppermute | solution.py:438
  45.4 21.7 %all-to-all-start.1 = ((bf16[64,4,128]{2,1,0:T(4,128)(2,1)}), bf16[64,4,128]{2,1,0:T(4,128)(2,1)S(1)}, u32[]{:S(2)}, u32[]{:S(2)}) async-start(bf16[64,4,128]{2,1,0:T(4,128)(2,1)} %get-tuple-element.38), calls=%async_computation.1 | async-start | bytes 131072 | tf_op jit(solution)/shard_map/all_to_all | solution.py:439
  55.4 5.8 %collective-permute-start.9 = (bf16[320,128]{1,0:T(8,128)(2,1)S(1)}, bf16[320,128]{1,0:T(8,128)(2,1)S(1)}, u32[]{:S(2)}, u32[]{:S(2)}) collective-permute-start(bf16[320,128]{1,0:T(8,128)(2,1)S(1)} %collective-permute-done.8.side), channel_id=1, source_target_pairs={{0,2},{1,3},{2,0},{3,1},{4,6},{5,7},{6,4},{7,5},{8,10},{9,11},{10,... | collective-permute-start | bytes 245768 | tf_op jit(solution)/shard_map/ppermute | solution.py:427

commit v7 on v6

--- a/solution.py
+++ b/solution.py
@@ -150,11 +150,8 @@
                 for t in range(tiles)
             ]
         copies[l].wait()
-        total = None
-        for k in range(kn):
-            part = jnp.concatenate(picked[k * tiles : (k + 1) * tiles], axis=1)
-            term = dot(part, weights[l, k], NT)
-            total = term if total is None else total + term
+        joined = jnp.concatenate([weights[l, k] for k in range(kn)], axis=1)
+        total = dot(jnp.concatenate(picked, axis=1), joined, NT)
         out[l * nrhs : (l + 1) * nrhs] = total
 
 
@@ -328,7 +325,7 @@
     proj_first = 0.5 * vv / square_first + ratio
     shift = proj_first - 0.5
     square_image = (uu - 2.0 * shift * vu + shift * shift * vv) / square_first
-    norm_image = jnp.sqrt(square_image + epsilon)
+    norm_image = jnp.sqrt(jnp.maximum(square_image, 0.0) + epsilon)
     scale = 1.0 / (norm_first * norm_image)
     on_z = scale * unit
     on_u = scale * (0.5 - shift)
@@ -348,7 +345,7 @@
         + 2.0 * on_v * (on_u * vu)
         + on_v * (on_v * vv)
     )
-    norm_last = jnp.sqrt(square_last + epsilon)
+    norm_last = jnp.sqrt(jnp.maximum(square_last, 0.0) + epsilon)
     for l in range(leaves):
         rows = pl.ds(l * nrhs, nrhs)
         v = vector[l]

time: 90.5 us -> 90.5 us (level)
  no operation moved by 1% of the time
where the time goes in v7:
time: 90.5 us; the launch traced here: 90 us
  starting transfers between devices  38.1 us (42%)
  blocking collectives  20.4 us (23%)
  Pallas kernels  17.4 us (19%)
  waiting for transfers between devices  13.4 us (15%)
    all_to_all x2, starting transfers between devices, exchange(): parents = lax.all_to_all(parent, ROWS, 0, 0, tiled=True)  26.1 us
    all_to_all x1, blocking collectives, shards(): sums = lax.all_to_all(sums, ROWS_GRP, 0, 0, tiled=True)  20.4 us
    pallas_call x10, Pallas kernels, call(): pl.pallas_call(kernel, in_specs=specs, out_specs=[VMEM] * len(outs), out_...  17.4 us
    ppermute x8, starting transfers between devices, swap(): lax.ppermute(array, ROWS_GRP, [(i, i ^ bits) for i in range(devices)])  10.7 us
    all_to_all x2, waiting for transfers between devices, exchange(): parents = lax.all_to_all(parent, ROWS, 0, 0, tiled=True)  8.61 us
    ppermute x8, waiting for transfers between devices, swap(): lax.ppermute(array, ROWS_GRP, [(i, i ^ bits) for i in range(devices)])  4.77 us
  transfers between devices with their start and end apart: 12, of which 5 were waited for; matrix products, arithmetic and copies ran while one was open for 0% of the time, Pallas kernels for 11%

profile of v7, /device:TPU:1, one launch (start us, length us, event | category | flops | bytes accessed | tf_op | source)
XLA Modules:
  0.0 90.0 jit_solution(12661099438227038202)
XLA Ops:
  0.6 1.5 %shard_map.148 = (bf16[240,128]{1,0:T(8,128)(2,1)S(1)}, bf16[48,128]{1,0:T(8,128)(2,1)S(1)}) custom-call(f32[4,16,384]{2,1,0:T(8,128)} %vector.3, bf16[4,32,384]{2,1,0:T(8,128)(2,1)} %col_basis.3, f32[4,32,32]{2,1,0:T(8,128)} %leaf_transfer.5, f32[1,32,32]{2,1,0:T(8,128)} %box_transfer.3), custom_call_target="tpu_custom_call" | custom-call | tf_op jit(solution)/shard_map/pallas_call | solution.py:407
  2.1 3.0 %collective-permute-start.1 = (bf16[240,128]{1,0:T(8,128)(2,1)S(1)}, bf16[240,128]{1,0:T(8,128)(2,1)S(1)}, u32[]{:S(2)}, u32[]{:S(2)}) collective-permute-start(bf16[240,128]{1,0:T(8,128)(2,1)S(1)} %get-tuple-element.25.own), channel_id=1, source_target_pairs={{0,3},{1,2},{2,1},{3,0},{4,7},{5,6},{6,5},{7,4},{8,11},{9,10},{10,... | collective-permute-start | bytes 184328 | tf_op jit(solution)/shard_map/ppermute | solution.py:424
  5.1 0.2 collective-permute-start
  5.3 1.4 %collective-permute-start.2 = (bf16[48,128]{1,0:T(8,128)(2,1)S(1)}, bf16[48,128]{1,0:T(8,128)(2,1)S(1)}, u32[]{:S(2)}, u32[]{:S(2)}) collective-permute-start(bf16[48,128]{1,0:T(8,128)(2,1)S(1)} %get-tuple-element.26), channel_id=1, source_target_pairs={{0,2},{1,3},{2,0},{3,1},{4,6},{5,7},{6,4},{7,5},{8,10},{9,11},{10,... | collective-permute-start | bytes 36872 | tf_op jit(solution)/shard_map/ppermute | solution.py:424
  6.7 1.9 %collective-permute-done.2.coef = bf16[48,128]{1,0:T(8,128)(2,1)S(1)} collective-permute-done((bf16[48,128]{1,0:T(8,128)(2,1)S(1)}, bf16[48,128]{1,0:T(8,128)(2,1)S(1)}, u32[]{:S(2)}, u32[]{:S(2)}) %collective-permute-start.2) | collective-permute-done | bytes 12320 | tf_op jit(solution)/shard_map/ppermute | solution.py:424
  8.6 0.0 collective-permute-done.1.cross
  8.6 0.0 collective-permute-done.chip
  8.6 0.7 shard_map.149
  9.2 0.7 collective-permute-start.3
  9.9 16.0 %all-to-all-start = ((bf16[64,4,128]{2,1,0:T(4,128)(2,1)}), bf16[64,4,128]{2,1,0:T(4,128)(2,1)S(1)}, u32[]{:S(2)}, u32[]{:S(2)}) async-start(bf16[64,4,128]{2,1,0:T(4,128)(2,1)} %get-tuple-element.27), calls=%async_computation | async-start | bytes 131072 | tf_op jit(solution)/shard_map/all_to_all | solution.py:436
  25.9 0.0 collective-permute-done.3.side
  25.9 1.5 %collective-permute-start.4 = (bf16[320,128]{1,0:T(8,128)(2,1)S(1)}, bf16[320,128]{1,0:T(8,128)(2,1)S(1)}, u32[]{:S(2)}, u32[]{:S(2)}) collective-permute-start(bf16[320,128]{1,0:T(8,128)(2,1)S(1)} %collective-permute-done.3.side), channel_id=1, source_target_pairs={{0,2},{1,3},{2,0},{3,1},{4,6},{5,7},{6,4},{7,5},{8,10},{9,11},{10,... | collective-permute-start | bytes 245768 | tf_op jit(solution)/shard_map/ppermute | solution.py:424
  27.5 3.6 %shard_map.150.near = f32[64,384]{1,0:T(8,128)S(1)} custom-call(s32[4,3]{1,0:T(4,128)} %near_cols.3, bf16[240,128]{1,0:T(8,128)(2,1)S(1)} %get-tuple-element.25.own, bf16[240,128]{1,0:T(8,128)(2,1)S(1)} %collective-permute-done.chip, bf16[240,128]{1,0:T(8,128)(2,1)S(1)} %collective-permute-done.1.cross, bf16[320,128]{1,0:T(8,128)(2,1)S(1)} %collective-permute-done.3.side, ...), custom_call_target="tpu_custom_call" | custom-call | tf_op jit(solution)/shard_map/pallas_call | solution.py:407
  31.1 0.4 collective-permute-done.4.other
  31.5 1.7 %shard_map.151 = (f32[64,128]{1,0:T(8,128)S(1)}, bf16[32,128]{1,0:T(8,128)(2,1)S(1)}, bf16[128,32]{1,0:T(8,128)(2,1)S(1)}, bf16[128,384]{1,0:T(8,128)(2,1)S(1)},...) custom-call(s32[4,8]{1,0:T(4,128)} %leaf_far.3, ...), custom_call_target="tpu_custom_call" | custom-call | tf_op jit(solution)/shard_map/pallas_call | solution.py:407
  33.2 4.2 %all-to-all-done.parents = bf16[64,4,128]{2,1,0:T(4,128)(2,1)S(1)} async-done(((bf16[64,4,128]{2,1,0:T(4,128)(2,1)}), bf16[64,4,128]{2,1,0:T(4,128)(2,1)S(1)}, u32[]{:S(2)}, u32[]{:S(2)}) %all-to-all-start) | async-done | bytes 65568 | tf_op jit(solution)/shard_map/all_to_all | solution.py:436
  37.4 1.8 %shard_map.152 = (f32[64,384]{1,0:T(8,128)S(1)}, bf16[240,128]{1,0:T(8,128)(2,1)S(1)}, bf16[48,128]{1,0:T(8,128)(2,1)S(1)}) custom-call(s32[1,4]{1,0:T(1,128)} %coarse_far.3, bf16[64,4,128]{2,1,0:T(4,128)(2,1)S(1)} %all-to-all-done.parents, f32[64,384]{1,0:T(8,128)S(1)} %shard_map.150.near, f32[64,128]{1,0:T(8,128)S(1)} %get-tuple-element.29.local_field, ...), custom_call_target="tpu_custom_call" | custom-call | tf_op jit(solution)/shard_map/pallas_call | solution.py:407
  39.2 2.3 %collective-permute-start.6 = (bf16[240,128]{1,0:T(8,128)(2,1)S(1)}, bf16[240,128]{1,0:T(8,128)(2,1)S(1)}, u32[]{:S(2)}, u32[]{:S(2)}) collective-permute-start(bf16[240,128]{1,0:T(8,128)(2,1)S(1)} %get-tuple-element.36.own), channel_id=1, source_target_pairs={{0,3},{1,2},{2,1},{3,0},{4,7},{5,6},{6,5},{7,4},{8,11},{9,10},{10,... | collective-permute-start | bytes 184328 | tf_op jit(solution)/shard_map/ppermute | solution.py:424
  41.5 0.0 collective-permute-start.5
  41.5 0.1 collective-permute-start.7
  41.6 2.4 %collective-permute-done.7.coef = bf16[48,128]{1,0:T(8,128)(2,1)S(1)} collective-permute-done((bf16[48,128]{1,0:T(8,128)(2,1)S(1)}, bf16[48,128]{1,0:T(8,128)(2,1)S(1)}, u32[]{:S(2)}, u32[]{:S(2)}) %collective-permute-start.7) | collective-permute-done | bytes 12320 | tf_op jit(solution)/shard_map/ppermute | solution.py:424
  44.0 0.0 collective-permute-done.6.cross
  44.0 0.0 collective-permute-done.5.chip
  44.0 0.7 shard_map.153
  44.7 0.7 collective-permute-start.8
  45.4 10.0 %all-to-all-start.1 = ((bf16[64,4,128]{2,1,0:T(4,128)(2,1)}), bf16[64,4,128]{2,1,0:T(4,128)(2,1)S(1)}, u32[]{:S(2)}, u32[]{:S(2)}) async-start(bf16[64,4,128]{2,1,0:T(4,128)(2,1)} %get-tuple-element.38), calls=%async_computation.1 | async-start | bytes 131072 | tf_op jit(solution)/shard_map/all_to_all | solution.py:436
  55.4 0.0 collective-permute-done.8.side
  55.4 2.2 %collective-permute-start.9 = (bf16[320,128]{1,0:T(8,128)(2,1)S(1)}, bf16[320,128]{1,0:T(8,128)(2,1)S(1)}, u32[]{:S(2)}, u32[]{:S(2)}) collective-permute-start(bf16[320,128]{1,0:T(8,128)(2,1)S(1)} %collective-permute-done.8.side), channel_id=1, source_target_pairs={{0,2},{1,3},{2,0},{3,1},{4,6},{5,7},{6,4},{7,5},{8,10},{9,11},{10,... | collective-permute-start | bytes 245768 | tf_op jit(solution)/shard_map/ppermute | solution.py:424
  57.6 3.6 %shard_map.154.near = f32[64,384]{1,0:T(8,128)S(1)} custom-call(s32[4,3]{1,0:T(4,128)} %near_cols.3, bf16[240,128]{1,0:T(8,128)(2,1)S(1)} %get-tuple-element.36.own, bf16[240,128]{1,0:T(8,128)(2,1)S(1)} %collective-permute-done.5.chip, bf16[240,128]{1,0:T(8,128)(2,1)S(1)} %collective-permute-done.6.cross, bf16[320,128]{1,0:T(8,128)(2,1)S(1)} %collective-permute-done.8.side, ...), custom_call_target="tpu_custom_call" | custom-call | tf_op jit(solution)/shard_map/pallas_call | solution.py:407
  61.2 0.0 collective-permute-done.9.other
  61.2 1.4 %shard_map.155.local_field = f32[64,128]{1,0:T(8,128)S(1)} custom-call(s32[4,8]{1,0:T(4,128)} %leaf_far.3, s32[1,4]{1,0:T(1,128)} %box_far.3, bf16[320,128]{1,0:T(8,128)(2,1)S(1)} %get-tuple-element.39.own, bf16[320,128]{1,0:T(8,128)(2,1)S(1)} %collective-permute-done.8.side, bf16[320,128]{1,0:T(8,128)(2,1)S(1)} %collective-permute-done.9.other, ...), custom_call_target="tpu_custom_call" | custom-call | tf_op jit(solution)/shard_map/pallas_call | solution.py:407
  62.6 4.4 %all-to-all-done.1.parents = bf16[64,4,128]{2,1,0:T(4,128)(2,1)S(1)} async-done(((bf16[64,4,128]{2,1,0:T(4,128)(2,1)}), bf16[64,4,128]{2,1,0:T(4,128)(2,1)S(1)}, u32[]{:S(2)}, u32[]{:S(2)}) %all-to-all-start.1) | async-done | bytes 65568 | tf_op jit(solution)/shard_map/all_to_all | solution.py:436
  67.0 1.5 %shard_map.156 = (f32[64,384]{1,0:T(8,128)S(1)}, f32[256,1,128]{2,1,0:T(1,128)S(1)}) custom-call(s32[1,4]{1,0:T(1,128)} %coarse_far.3, bf16[64,4,128]{2,1,0:T(4,128)(2,1)S(1)} %all-to-all-done.1.parents, f32[64,384]{1,0:T(8,128)S(1)} %shard_map.154.near, f32[64,128]{1,0:T(8,128)S(1)} %shard_map.155.local_field, ...), custom_call_target="tpu_custom_call" | custom-call | tf_op jit(solution)/shard_map/pallas_call | solution.py:407
  68.5 20.4 %all_to_all.15.sums = f32[256,1,128]{2,1,0:T(1,128)S(1)} all-to-all(f32[256,1,128]{2,1,0:T(1,128)S(1)} %get-tuple-element.42), channel_id=1, replica_groups=mesh['rows_0'=4,'rows_1'=4,'rows_2'=4,'grp_0'=2,'grp_1'=2] {'rows_0','ro..., dimensions={0} | all-to-all | bytes 262144 | tf_op jit(solution)/shard_map/all_to_all | solution.py:490
  89.0 1.1 %shard_map.157 = (f32[4,16,384]{2,1,0:T(8,128)}, f32[4,16,384]{2,1,0:T(8,128)}, f32[5,16]{1,0:T(8,128)}) custom-call(f32[256,1,128]{2,1,0:T(1,128)S(1)} %all_to_all.15.sums, f32[4,16,384]{2,1,0:T(8,128)S(1)} %get-tuple-element.40.vector, f32[64,384]{1,0:T(8,128)S(1)} %get-tuple-element.41.image, f32[64,384]{1,0:T(8,128)S(1)} %get-tuple-element.43.second), custom_call_target="tpu_custom_call" | custom-call | tf_op jit(solution)/shard_map/pallas_call | solution.py:407
Async XLA Ops:
  2.1 6.5 %collective-permute-start.1 = (bf16[240,128]{1,0:T(8,128)(2,1)S(1)}, bf16[240,128]{1,0:T(8,128)(2,1)S(1)}, u32[]{:S(2)}, u32[]{:S(2)}) collective-permute-start(bf16[240,128]{1,0:T(8,128)(2,1)S(1)} %get-tuple-element.25.own), channel_id=1, source_target_pairs={{0,3},{1,2},{2,1},{3,0},{4,7},{5,6},{6,5},{7,4},{8,11},{9,10},{10,... | collective-permute-start | bytes 184328 | tf_op jit(solution)/shard_map/ppermute | solution.py:424
  5.1 3.4 %collective-permute-start = (bf16[240,128]{1,0:T(8,128)(2,1)S(1)}, bf16[240,128]{1,0:T(8,128)(2,1)S(1)}, u32[]{:S(2)}, u32[]{:S(2)}) collective-permute-start(bf16[240,128]{1,0:T(8,128)(2,1)S(1)} %get-tuple-element.25.own), channel_id=1, source_target_pairs={{0,1},{1,0},{2,3},{3,2},{4,5},{5,4},{6,7},{7,6},{8,9},{9,8},{10,11... | collective-permute-start | bytes 184328 | tf_op jit(solution)/shard_map/ppermute | solution.py:424
  5.3 3.2 %collective-permute-start.2 = (bf16[48,128]{1,0:T(8,128)(2,1)S(1)}, bf16[48,128]{1,0:T(8,128)(2,1)S(1)}, u32[]{:S(2)}, u32[]{:S(2)}) collective-permute-start(bf16[48,128]{1,0:T(8,128)(2,1)S(1)} %get-tuple-element.26), channel_id=1, source_target_pairs={{0,2},{1,3},{2,0},{3,1},{4,6},{5,7},{6,4},{7,5},{8,10},{9,11},{10,... | collective-permute-start | bytes 36872 | tf_op jit(solution)/shard_map/ppermute | solution.py:424
  9.2 16.7 %collective-permute-start.3 = (bf16[320,128]{1,0:T(8,128)(2,1)S(1)}, bf16[320,128]{1,0:T(8,128)(2,1)S(1)}, u32[]{:S(2)}, u32[]{:S(2)}) collective-permute-start(bf16[320,128]{1,0:T(8,128)(2,1)S(1)} %get-tuple-element.28.own), channel_id=1, source_target_pairs={{3,4},{4,3},{2,5},{5,2},{7,8},{8,7},{6,9},{9,6},{11,12},{12,11},{1... | collective-permute-start | bytes 245768 | tf_op jit(solution)/shard_map/ppermute | solution.py:435
  9.9 27.5 %all-to-all-start = ((bf16[64,4,128]{2,1,0:T(4,128)(2,1)}), bf16[64,4,128]{2,1,0:T(4,128)(2,1)S(1)}, u32[]{:S(2)}, u32[]{:S(2)}) async-start(bf16[64,4,128]{2,1,0:T(4,128)(2,1)} %get-tuple-element.27), calls=%async_computation | async-start | bytes 131072 | tf_op jit(solution)/shard_map/all_to_all | solution.py:436
  25.9 5.6 %collective-permute-start.4 = (bf16[320,128]{1,0:T(8,128)(2,1)S(1)}, bf16[320,128]{1,0:T(8,128)(2,1)S(1)}, u32[]{:S(2)}, u32[]{:S(2)}) collective-permute-start(bf16[320,128]{1,0:T(8,128)(2,1)S(1)} %collective-permute-done.3.side), channel_id=1, source_target_pairs={{0,2},{1,3},{2,0},{3,1},{4,6},{5,7},{6,4},{7,5},{8,10},{9,11},{10,... | collective-permute-start | bytes 245768 | tf_op jit(solution)/shard_map/ppermute | solution.py:424
  39.2 4.9 %collective-permute-start.6 = (bf16[240,128]{1,0:T(8,128)(2,1)S(1)}, bf16[240,128]{1,0:T(8,128)(2,1)S(1)}, u32[]{:S(2)}, u32[]{:S(2)}) collective-permute-start(bf16[240,128]{1,0:T(8,128)(2,1)S(1)} %get-tuple-element.36.own), channel_id=1, source_target_pairs={{0,3},{1,2},{2,1},{3,0},{4,7},{5,6},{6,5},{7,4},{8,11},{9,10},{10,... | collective-permute-start | bytes 184328 | tf_op jit(solution)/shard_map/ppermute | solution.py:424
  41.5 2.6 %collective-permute-start.5 = (bf16[240,128]{1,0:T(8,128)(2,1)S(1)}, bf16[240,128]{1,0:T(8,128)(2,1)S(1)}, u32[]{:S(2)}, u32[]{:S(2)}) collective-permute-start(bf16[240,128]{1,0:T(8,128)(2,1)S(1)} %get-tuple-element.36.own), channel_id=1, source_target_pairs={{0,1},{1,0},{2,3},{3,2},{4,5},{5,4},{6,7},{7,6},{8,9},{9,8},{10,11... | collective-permute-start | bytes 184328 | tf_op jit(solution)/shard_map/ppermute | solution.py:424
  41.5 2.5 %collective-permute-start.7 = (bf16[48,128]{1,0:T(8,128)(2,1)S(1)}, bf16[48,128]{1,0:T(8,128)(2,1)S(1)}, u32[]{:S(2)}, u32[]{:S(2)}) collective-permute-start(bf16[48,128]{1,0:T(8,128)(2,1)S(1)} %get-tuple-element.37), channel_id=1, source_target_pairs={{0,2},{1,3},{2,0},{3,1},{4,6},{5,7},{6,4},{7,5},{8,10},{9,11},{10,... | collective-permute-start | bytes 36872 | tf_op jit(solution)/shard_map/ppermute | solution.py:424
  44.7 10.7 %collective-permute-start.8 = (bf16[320,128]{1,0:T(8,128)(2,1)S(1)}, bf16[320,128]{1,0:T(8,128)(2,1)S(1)}, u32[]{:S(2)}, u32[]{:S(2)}) collective-permute-start(bf16[320,128]{1,0:T(8,128)(2,1)S(1)} %get-tuple-element.39.own), channel_id=1, source_target_pairs={{3,4},{4,3},{2,5},{5,2},{7,8},{8,7},{6,9},{9,6},{11,12},{12,11},{1... | collective-permute-start | bytes 245768 | tf_op jit(solution)/shard_map/ppermute | solution.py:435
  45.4 21.7 %all-to-all-start.1 = ((bf16[64,4,128]{2,1,0:T(4,128)(2,1)}), bf16[64,4,128]{2,1,0:T(4,128)(2,1)S(1)}, u32[]{:S(2)}, u32[]{:S(2)}) async-start(bf16[64,4,128]{2,1,0:T(4,128)(2,1)} %get-tuple-element.38), calls=%async_computation.1 | async-start | bytes 131072 | tf_op jit(solution)/shard_map/all_to_all | solution.py:436
  55.4 5.8 %collective-permute-start.9 = (bf16[320,128]{1,0:T(8,128)(2,1)S(1)}, bf16[320,128]{1,0:T(8,128)(2,1)S(1)}, u32[]{:S(2)}, u32[]{:S(2)}) collective-permute-start(bf16[320,128]{1,0:T(8,128)(2,1)S(1)} %collective-permute-done.8.side), channel_id=1, source_target_pairs={{0,2},{1,3},{2,0},{3,1},{4,6},{5,7},{6,4},{7,5},{8,10},{9,11},{10,... | collective-permute-start | bytes 245768 | tf_op jit(solution)/shard_map/ppermute | solution.py:424
